TPU v7x, 16 devices: a whole 2x2x2 slice. The times are simulated.
16 devices in a mesh: dp: 4 (over z, y), x: 4 (over x, core).
Axes of the slice: x: 2, y: 2, z: 2, core: 2. Of those that a mesh axis runs over, the one named last changes fastest.
Arguments:
- start_pos: int32 [512], P('dp'), parts along dimension 0
- hidden_in: bfloat16 [4, 512, 4096], P(None, ('dp', 'x')), parts along dimension 1
- k_cache: bfloat16 [512, 256, 8, 128], P('dp', None, 'x'), parts along dimension 0
- v_cache: bfloat16 [512, 256, 8, 128], P('dp', None, 'x'), parts along dimension 0
- attn_norm: bfloat16 [4096], replicated
- w_q: bfloat16 [4096, 4096], replicated
- w_k: bfloat16 [4096, 1024], replicated
- w_v: bfloat16 [4096, 1024], replicated
- q_norm: bfloat16 [128], replicated
- k_norm: bfloat16 [128], replicated
- w_o: bfloat16 [4096, 4096], replicated
- mlp_norm: bfloat16 [4096], replicated
- w_gate: bfloat16 [4096, 12288], replicated
- w_up: bfloat16 [4096, 12288], replicated
- w_down: bfloat16 [12288, 4096], replicated
Outputs:
- output 1: bfloat16 [4, 512, 4096], P(None, ('dp', 'x')), parts along dimension 1
- output 2: bfloat16 [512, 256, 8, 128], P(('dp', 'x')), parts along dimension 0
- output 3: bfloat16 [512, 256, 8, 128], P(('dp', 'x')), parts along dimension 0
There are 4 independent parts. A program takes and returns all parts, laid end to end along the dimension named above; an argument that names none is the same for every part.
All inputs are finite; a program needn't handle non-finite values.
Results may differ from a plain program's by a relative error of at most 0.0104356.
Values are sent between devices in bfloat16 or wider.
A program may use at most 1.75 GiB of HBM per device.

v0:
```python
import jax
import jax.numpy as jnp
from jax import lax
from jax.sharding import PartitionSpec as P

EPS = 1e-6
THETA = 1000000.0


def rms_norm(values, gain_vec):
    values32 = values.astype(jnp.float32)
    inv_rms = lax.rsqrt(jnp.mean(values32 * values32, axis=-1, keepdims=True) + EPS)
    return values32 * inv_rms * gain_vec.astype(jnp.float32)


def rotary(values, positions):
    head_dim = values.shape[-1]
    half_dim = head_dim // 2
    inv_freq = jnp.power(THETA, -jnp.arange(half_dim, dtype=jnp.float32) * 2.0 / head_dim)
    angles = positions.astype(jnp.float32)[..., None, None] * inv_freq
    cos_part = jnp.cos(angles)
    sin_part = jnp.sin(angles)
    first_half = values[..., :half_dim]
    second_half = values[..., half_dim:]
    return jnp.concatenate([first_half * cos_part - second_half * sin_part, second_half * cos_part + first_half * sin_part], axis=-1)


def project(hidden, positions, attn_norm, w_q, w_k, w_v, q_norm, k_norm):
    n_steps, num_rows = hidden.shape[0], hidden.shape[1]
    head_dim = q_norm.shape[0]
    normed = rms_norm(hidden, attn_norm).astype(jnp.bfloat16)
    queries = jnp.einsum('sbd,de->sbe', normed, w_q, preferred_element_type=jnp.float32).reshape(n_steps, num_rows, -1, head_dim)
    keys_new = jnp.einsum('sbd,de->sbe', normed, w_k, preferred_element_type=jnp.float32).reshape(n_steps, num_rows, -1, head_dim)
    values_new = jnp.einsum('sbd,de->sbe', normed, w_v, preferred_element_type=jnp.float32).reshape(n_steps, num_rows, -1, head_dim)
    queries = rotary(rms_norm(queries, q_norm), positions).astype(jnp.bfloat16)
    keys_new = rotary(rms_norm(keys_new, k_norm), positions).astype(jnp.bfloat16)
    return queries, keys_new, values_new.astype(jnp.bfloat16)


def attend(queries, cache_k, cache_v, keys_new, values_new, start_pos):
    n_steps, num_rows, n_heads, head_dim = queries.shape
    num_slots, kv_local = cache_k.shape[1], cache_k.shape[2]
    grouped = queries.reshape(n_steps, num_rows, kv_local, n_heads // kv_local, head_dim)
    score_scale = head_dim ** -0.5
    old_scores = jnp.einsum('sbkgd,btkd->bkgst', grouped, cache_k, preferred_element_type=jnp.float32) * score_scale
    old_valid = (jnp.arange(num_slots)[None, :] < start_pos[:, None])[:, None, None, None, :]
    old_scores = jnp.where(old_valid, old_scores, -jnp.inf)
    new_scores = jnp.einsum('sbkgd,jbkd->bkgsj', grouped, keys_new, preferred_element_type=jnp.float32) * score_scale
    new_valid = jnp.arange(n_steps)[:, None] >= jnp.arange(n_steps)[None, :]
    new_scores = jnp.where(new_valid, new_scores, -jnp.inf)
    peak_score = jnp.maximum(jnp.max(old_scores, axis=-1, keepdims=True), jnp.max(new_scores, axis=-1, keepdims=True))
    old_weights = jnp.exp(old_scores - peak_score)
    new_weights = jnp.exp(new_scores - peak_score)
    weight_sum = jnp.sum(old_weights, axis=-1) + jnp.sum(new_weights, axis=-1)
    mixed_vals = jnp.einsum('bkgst,btkd->sbkgd', old_weights.astype(jnp.bfloat16), cache_v, preferred_element_type=jnp.float32)
    mixed_vals = mixed_vals + jnp.einsum('bkgsj,jbkd->sbkgd', new_weights.astype(jnp.bfloat16), values_new, preferred_element_type=jnp.float32)
    mixed_vals = mixed_vals / jnp.transpose(weight_sum, (3, 0, 1, 2))[..., None]
    return mixed_vals.astype(jnp.bfloat16).reshape(n_steps, num_rows, n_heads, head_dim)


def finish(hidden, attended, w_o, mlp_norm, w_gate, w_up, w_down):
    n_steps, num_rows = attended.shape[0], attended.shape[1]
    flat_attn = attended.reshape(n_steps, num_rows, -1)
    attn_out = jnp.einsum('sbe,ed->sbd', flat_attn, w_o, preferred_element_type=jnp.float32)
    residual = (hidden.astype(jnp.float32) + attn_out).astype(jnp.bfloat16)
    normed = rms_norm(residual, mlp_norm).astype(jnp.bfloat16)
    gate_val = jnp.einsum('sbd,df->sbf', normed, w_gate, preferred_element_type=jnp.float32)
    up_val = jnp.einsum('sbd,df->sbf', normed, w_up, preferred_element_type=jnp.float32)
    activated = (jax.nn.silu(gate_val) * up_val).astype(jnp.bfloat16)
    down_val = jnp.einsum('sbf,fd->sbd', activated, w_down, preferred_element_type=jnp.float32)
    return (residual.astype(jnp.float32) + down_val).astype(jnp.bfloat16)


def write_slots(cache_arr, fresh_rows, start_pos):
    slot_ids = jnp.arange(cache_arr.shape[1])[None, :, None, None]
    for step_idx in range(fresh_rows.shape[0]):
        slot_hit = slot_ids == (start_pos + step_idx)[:, None, None, None]
        cache_arr = jnp.where(slot_hit, fresh_rows[step_idx][:, None], cache_arr)
    return cache_arr


def solution(mesh):
    row_spec = P(None, ('dp', 'x'), None)
    cache_in = P('dp', None, 'x', None)
    cache_out = P(('dp', 'x'), None, None, None)

    def local_run(start_pos, hidden_in, k_heads, v_heads, attn_norm, w_q, w_k, w_v, q_norm, k_norm, w_o, mlp_norm, w_gate, w_up, w_down):
        num_rows = hidden_in.shape[1]
        my_pos = lax.dynamic_slice_in_dim(start_pos, lax.axis_index('x') * num_rows, num_rows)
        k_local = lax.all_to_all(k_heads, 'x', 0, 2, tiled=True)
        v_local = lax.all_to_all(v_heads, 'x', 0, 2, tiled=True)
        positions = my_pos[None, :] + jnp.arange(hidden_in.shape[0])[:, None]
        queries, keys_new, values_new = project(hidden_in, positions, attn_norm, w_q, w_k, w_v, q_norm, k_norm)
        attended = attend(queries, k_local, v_local, keys_new, values_new, my_pos)
        out_hidden = finish(hidden_in, attended, w_o, mlp_norm, w_gate, w_up, w_down)
        return out_hidden, write_slots(k_local, keys_new, my_pos), write_slots(v_local, values_new, my_pos)

    return jax.shard_map(local_run, mesh=mesh, in_specs=(P('dp'), row_spec, cache_in, cache_in) + (P(),) * 11, out_specs=(row_spec, cache_out, cache_out), check_vma=False)
```

profile of v0, /device:TPU:0, one launch (start us, length us, event | category | flops | bytes accessed | tf_op | source)
XLA Modules:
  0.0 613.7 jit_solution(5101473324233552022)
XLA Ops:
  0.6 194.7 %all_to_all.36 = bf16[128,256,2,128]{3,2,1,0:T(2,128)(2,1)} all-to-all(bf16[128,256,2,128]{3,2,1,0:T(2,128)(2,1)} %param.17), channel_id=1, replica_groups=mesh['dp'=4,'x'=4] {'x'}, dimensions={0} | all-to-all | bytes 33554432 | tf_op jit(solution)/shard_map/all_to_all | solution.py:90
  195.4 7.1 %all-to-all-start.1 = ((bf16[128,256,2,128]{3,2,1,0:T(2,128)(2,1)}), bf16[128,256,2,128]{3,2,1,0:T(2,128)(2,1)}, u32[]{:S(2)}, u32[]{:S(2)}) async-start(bf16[128,256,2,128]{3,2,1,0:T(2,128)(2,1)} %param.18), calls=%async_computation.1 | async-start | bytes 33554432 | tf_op jit(solution)/shard_map/all_to_all | solution.py:91
  204.3 4.8 fusion.59
  215.2 13.0 %fusion.8 = f32[4,32,4096]{2,1,0:T(8,128)S(1)} fusion(bf16[4096,4096]{1,0:T(8,128)(2,1)} %param.20, bf16[4,32,4096]{2,1,0:T(8,128)(2,1)S(1)} %copy-done.1, f32[4096]{0:T(1024)S(1)} %convert_element_type.62, f32[4,32]{1,0:T(4,128)S(1)} %add_rsqrt_fusion.3), kind=kOutput, calls=%fused_computation.8 | convolution fusion | flops 4297064448 | bytes 36717056 | tf_op jit(solution)/shard_map/sbd,de->sbe/dot_general | solution.py:32
  237.5 10.7 %fusion.72 = f32[32,8,4,4,4]{4,2,3,1,0:T(4,128)} fusion(bf16[4,32,8,64]{3,0,2,1:T(4,128)(2,1)S(1)} %get-tuple-element.28, bf16[4,32,8,64]{3,0,2,1:T(4,128)(2,1)S(1)} %get-tuple-element.27, bf16[4,32,8,4,64]{4,3,0,2,1:T(4,128)(2,1)S(1)} %copy.106, bf16[4,32,8,4,64]{4,3,0,2,1:T(4,128)(2,1)S(1)} %copy.105), kind=kOutput, calls=%fused_computation.67 | convolution fusion | flops 6815744 | bytes 1376256 | tf_op jit(solution)/shard_map/sbkgd,jbkd->bkgsj/dot_general | solution.py:48
  248.2 2.4 copy.111
  252.0 3.6 slice_maximum_fusion.3
  259.0 1.7 bitcast_bitcast_fusion
  260.6 15.2 %copy.107 = bf16[4,32,256,2,128]{4,2,3,0,1:T(8,128)(2,1)} copy(bf16[4,32,256,2,128]{4,3,2,1,0:T(2,128)(2,1)} %bitcast.161) | data formatting | bytes 33554432 | tf_op jit(solution)/shard_map/all_to_all | solution.py:90
  275.8 109.4 %all-to-all-done.1 = bf16[128,256,2,128]{3,2,1,0:T(2,128)(2,1)} async-done(((bf16[128,256,2,128]{3,2,1,0:T(2,128)(2,1)}), bf16[128,256,2,128]{3,2,1,0:T(2,128)(2,1)}, u32[]{:S(2)}, u32[]{:S(2)}) %all-to-all-start.1) | async-done | bytes 16777248 | tf_op jit(solution)/shard_map/all_to_all | solution.py:91
  385.2 15.4 %copy.113 = bf16[4,32,256,2,128]{4,2,3,0,1:T(8,128)(2,1)} copy(bf16[4,32,256,2,128]{4,3,2,1,0:T(2,128)(2,1)} %bitcast.13) | data formatting | bytes 33554432 | tf_op jit(solution)/shard_map/all_to_all | solution.py:91
  400.6 10.2 %bitcast_reduce_fusion = (f32[32,8,4,4]{2,3,1,0:T(4,128)S(1)}, f32[32,8,4,4,256]{4,3,2,1,0:T(4,128)}) fusion(pred[32,256]{1,0:T(8,128)(4,1)S(1)} %get-tuple-element.46, bf16[32,256,8,128,1]{3,1,4,2,0:T(8,128)(2,1)} %bitcast.157, bf16[4,32,8,4,64]{4,3,0,2,1:T(4,128)(2,1)S(1)} %copy.106, bf16[4,32,8,4,64]{4,3,0,2,1:T(4,128)(2,1)S(1)} %copy.105), kind=kOutput, calls=%fused_computation.29 | convolution fusion | flops 273674240 | bytes 22044672 | tf_op jit(solution)/shard_map/sbkgd,btkd->bkgst/dot_general | solution.py:45
  412.0 6.1 fusion.48
  418.9 2.1 copy.133
  421.0 2.1 add_bitcast_fusion
  423.2 3.4 copy.119
  426.6 2.7 copy.117
  429.4 8.2 %fusion.56 = f32[32,8,4,4,128]{4,3,2,1,0:T(4,128)S(1)} fusion(bf16[32,256,8,128,1]{3,1,4,2,0:T(8,128)(2,1)} %bitcast.159, bf16[32,8,4,4,256]{4,2,3,1,0:T(4,128)(2,1)S(1)} %get-tuple-element.24), kind=kOutput, calls=%fused_computation.46 | convolution fusion | flops 268435456 | bytes 20971520 | tf_op jit(solution)/shard_map/bkgst,btkd->sbkgd/dot_general | solution.py:55
  441.3 13.6 %multiply_reduce_fusion = (f32[4,32]{1,0:T(4,128)S(1)}, f32[4,32,4096]{2,1,0:T(8,128)S(1)}) fusion(bf16[4,32,4096]{2,1,0:T(8,128)(2,1)} %reshape_reshape.3, bf16[4096,4096]{1,0:T(8,128)(2,1)} %param.25, bf16[4,32,4096]{2,1,0:T(8,128)(2,1)S(1)} %copy-done.1), kind=kOutput, calls=%fused_computation.49 | convolution fusion | flops 4298113024 | bytes 37749248 | tf_op jit(solution)/shard_map/sbe,ed->sbd/dot_general | solution.py:64
  455.0 22.9 %select_select_fusion = (bf16[32,256,8,128]{3,1,2,0:T(8,128)(2,1)}, bf16[32,256,8,128]{3,1,2,0:T(8,128)(2,1)}) fusion(bf16[32,256,8,128]{3,1,2,0:T(8,128)(2,1)} %bitcast.160, pred[32,256]{1,0:T(8,128)(4,1)S(1)} %copy-done.21, pred[32,256]{1,0:T(8,128)(4,1)S(1)} %copy-done.22, pred[32,256]{1,0:T(8,128)(4,1)S(1)} %copy-done.23, ...), kind=kLoop, calls=%fused_computation.10 | loop fusion | flops 67108864 | bytes 67665920 | tf_op jit(solution)/shard_map/jit(_where)/select_n | solution.py:78
  478.0 20.0 %copy.122 = bf16[32,256,8,128]{3,2,1,0:T(8,128)(2,1)} copy(bf16[32,256,8,128]{3,1,2,0:T(8,128)(2,1)} %get-tuple-element.39) | data formatting | bytes 33554432
  498.0 12.1 %copy.121 = bf16[32,256,8,128]{3,2,1,0:T(8,128)(2,1)} copy(bf16[32,256,8,128]{3,1,2,0:T(8,128)(2,1)S(1)} %copy-done) | data formatting | bytes 33554432
  510.1 36.2 %fusion.4 = f32[4,32,12288]{2,1,0:T(8,128)} fusion(bf16[4096,12288]{1,0:T(8,128)(2,1)} %param.27, f32[4,32,4096]{2,1,0:T(8,128)S(1)} %get-tuple-element.50, f32[4096]{0:T(1024)S(1)} %convert_element_type.74, f32[4,32]{1,0:T(4,128)S(1)} %add_rsqrt_fusion.2), kind=kOutput, calls=%fused_computation.4 | convolution fusion | flops 12886474752 | bytes 109068800 | tf_op jit(solution)/shard_map/sbd,df->sbf/dot_general | solution.py:67
  546.3 66.9 %fusion.41 = bf16[4,32,4096]{2,1,0:T(8,128)(2,1)} fusion(f32[4,32,4096]{2,1,0:T(8,128)S(1)} %get-tuple-element.50, bf16[12288,4096]{1,0:T(8,128)(2,1)} %param.29, bf16[4096,12288]{1,0:T(8,128)(2,1)} %param.28, f32[4,32,12288]{2,1,0:T(8,128)} %fusion.4, f32[4096]{0:T(1024)S(1)} %convert_element_type.74, f32[4,32]{1,0:T(4,128)S(1)} %add_rsqrt_fusion.2), kind=kOutput, calls=%fused_computation.27 | convolution fusion | flops 25781862400 | bytes 210780672 | tf_op jit(solution)/shard_map/sbf,fd->sbd/dot_general | solution.py:70
  (117 shorter events, 27.3 us)
Async XLA Ops:
  195.3 7.2 %copy-start.25 = (bf16[4096]{0:T(1024)(128)(2,1)S(1)}, bf16[4096]{0:T(1024)(128)(2,1)}, u32[]{:S(2)}) copy-start(bf16[4096]{0:T(1024)(128)(2,1)} %param.26) | copy-start | bytes 24580
  195.3 7.3 %copy-start.28 = (s32[128]{0:T(128)S(1)}, s32[128]{0:T(128)}, u32[]{:S(2)}) copy-start(s32[128]{0:T(128)} %param.15) | copy-start | bytes 1540
  195.4 8.6 %copy-start.1 = (bf16[4,32,4096]{2,1,0:T(8,128)(2,1)S(1)}, bf16[4,32,4096]{2,1,0:T(8,128)(2,1)}, u32[]{:S(2)}) copy-start(bf16[4,32,4096]{2,1,0:T(8,128)(2,1)} %param.16) | copy-start | bytes 3145732
  195.4 189.9 %all-to-all-start.1 = ((bf16[128,256,2,128]{3,2,1,0:T(2,128)(2,1)}), bf16[128,256,2,128]{3,2,1,0:T(2,128)(2,1)}, u32[]{:S(2)}, u32[]{:S(2)}) async-start(bf16[128,256,2,128]{3,2,1,0:T(2,128)(2,1)} %param.18), calls=%async_computation.1 | async-start | bytes 33554432 | tf_op jit(solution)/shard_map/all_to_all | solution.py:91
  204.0 8.5 %slice-start = ((s8[8388608]{0:T(1024)(128)(4,1)}), s8[4194304]{0:T(1024)(128)(4,1)S(1)}, s32[]{:S(2)}) async-start(s8[8388608]{0:T(1024)(128)(4,1)} %bitcast.163), calls=%async_computation.2 | async-start | bytes 8388608
  204.3 8.2 %slice-start.1 = ((s8[8388608]{0:T(1024)(128)(4,1)}), s8[4194304]{0:T(1024)(128)(4,1)S(1)}, s32[]{:S(2)}) async-start(s8[8388608]{0:T(1024)(128)(4,1)} %bitcast.163), calls=%async_computation.3 | async-start | bytes 8388608
  250.6 25.2 %copy-start.26 = (pred[4,4]{1,0:T(4,128)(4,1)}, pred[4,4]{1,0:T(4,128)(4,1)S(1)}, u32[]{:S(2)}) copy-start(pred[4,4]{1,0:T(4,128)(4,1)S(1)} %iota_compare_fusion.5) | copy-start | bytes 52
  400.6 10.2 %copy-start.7 = (f32[32,8,4,4]{2,3,1,0:T(4,128)S(1)}, f32[32,8,4,4]{2,3,1,0:T(4,128)}, u32[]{:S(2)}) copy-start(f32[32,8,4,4]{2,3,1,0:T(4,128)} %copy.112) | copy-start | bytes 49156
  429.4 8.2 %copy-start.8 = (bf16[32,8,4,4,4]{4,3,2,1,0:T(4,128)(2,1)S(1)}, bf16[32,8,4,4,4]{4,3,2,1,0:T(4,128)(2,1)}, u32[]{:S(2)}) copy-start(bf16[32,8,4,4,4]{4,3,2,1,0:T(4,128)(2,1)} %copy.117) | copy-start | bytes 98308
  429.4 8.2 %copy-start.9 = (f32[4,32,8,4]{0,3,2,1:T(4,128)S(1)}, f32[4,32,8,4]{0,3,2,1:T(4,128)}, u32[]{:S(2)}) copy-start(f32[4,32,8,4]{0,3,2,1:T(4,128)} %copy.119) | copy-start | bytes 49156
  429.4 8.2 %copy-start.11 = (bf16[4,32,8,128,1]{3,2,1,0,4:T(8,128)(2,1)S(1)}, bf16[4,32,8,128,1]{3,2,1,0,4:T(8,128)(2,1)}, u32[]{:S(2)}) copy-start(bf16[4,32,8,128,1]{3,2,1,0,4:T(8,128)(2,1)} %bitcast_bitcast_fusion) | copy-start | bytes 786436
  441.2 13.7 %copy-start.12 = (bf16[4,8,8,128]{3,2,1,0:T(8,128)(2,1)S(1)}, bf16[4,8,8,128]{3,2,1,0:T(8,128)(2,1)}, u32[]{:S(2)}) copy-start(bf16[4,8,8,128]{3,2,1,0:T(8,128)(2,1)} %copy.138) | copy-start | bytes 196612
  441.2 13.7 %copy-start.13 = (bf16[4,8,8,128]{3,2,1,0:T(8,128)(2,1)S(1)}, bf16[4,8,8,128]{3,2,1,0:T(8,128)(2,1)}, u32[]{:S(2)}) copy-start(bf16[4,8,8,128]{3,2,1,0:T(8,128)(2,1)} %copy.141) | copy-start | bytes 196612
  441.2 13.7 %copy-start.14 = (bf16[4,8,8,128]{3,2,1,0:T(8,128)(2,1)S(1)}, bf16[4,8,8,128]{3,2,1,0:T(8,128)(2,1)}, u32[]{:S(2)}) copy-start(bf16[4,8,8,128]{3,2,1,0:T(8,128)(2,1)} %copy.140) | copy-start | bytes 196612
  441.2 13.7 %copy-start.15 = (bf16[4,8,8,128]{3,2,1,0:T(8,128)(2,1)S(1)}, bf16[4,8,8,128]{3,2,1,0:T(8,128)(2,1)}, u32[]{:S(2)}) copy-start(bf16[4,8,8,128]{3,2,1,0:T(8,128)(2,1)} %copy.139) | copy-start | bytes 196612
  441.2 13.7 %copy-start.16 = (bf16[32,8,128]{2,1,0:T(8,128)(2,1)S(1)}, bf16[32,8,128]{2,1,0:T(8,128)(2,1)}, u32[]{:S(2)}) copy-start(bf16[32,8,128]{2,1,0:T(8,128)(2,1)} %get-tuple-element.55) | copy-start | bytes 196612
  441.2 13.7 %copy-start.17 = (bf16[32,8,128]{2,1,0:T(8,128)(2,1)S(1)}, bf16[32,8,128]{2,1,0:T(8,128)(2,1)}, u32[]{:S(2)}) copy-start(bf16[32,8,128]{2,1,0:T(8,128)(2,1)} %get-tuple-element.56) | copy-start | bytes 196612
  441.2 13.7 %copy-start.18 = (bf16[32,8,128]{2,1,0:T(8,128)(2,1)S(1)}, bf16[32,8,128]{2,1,0:T(8,128)(2,1)}, u32[]{:S(2)}) copy-start(bf16[32,8,128]{2,1,0:T(8,128)(2,1)} %get-tuple-element.53) | copy-start | bytes 196612
  441.2 13.7 %copy-start.19 = (bf16[32,8,128]{2,1,0:T(8,128)(2,1)S(1)}, bf16[32,8,128]{2,1,0:T(8,128)(2,1)}, u32[]{:S(2)}) copy-start(bf16[32,8,128]{2,1,0:T(8,128)(2,1)} %get-tuple-element.54) | copy-start | bytes 196612
  441.2 13.7 %copy-start.20 = (pred[32,256]{1,0:T(8,128)(4,1)S(1)}, pred[32,256]{1,0:T(8,128)(4,1)}, u32[]{:S(2)}) copy-start(pred[32,256]{1,0:T(8,128)(4,1)} %iota_compare_fusion.3) | copy-start | bytes 24580
  441.2 13.7 %copy-start.21 = (pred[32,256]{1,0:T(8,128)(4,1)S(1)}, pred[32,256]{1,0:T(8,128)(4,1)}, u32[]{:S(2)}) copy-start(pred[32,256]{1,0:T(8,128)(4,1)} %get-tuple-element.45) | copy-start | bytes 24580
  441.3 13.7 %copy-start.22 = (pred[32,256]{1,0:T(8,128)(4,1)S(1)}, pred[32,256]{1,0:T(8,128)(4,1)}, u32[]{:S(2)}) copy-start(pred[32,256]{1,0:T(8,128)(4,1)} %get-tuple-element.51) | copy-start | bytes 24580
  441.3 13.7 %copy-start.23 = (pred[32,256]{1,0:T(8,128)(4,1)S(1)}, pred[32,256]{1,0:T(8,128)(4,1)}, u32[]{:S(2)}) copy-start(pred[32,256]{1,0:T(8,128)(4,1)} %get-tuple-element.52) | copy-start | bytes 24580
  477.9 20.0 %copy-start = (bf16[32,256,8,128]{3,1,2,0:T(8,128)(2,1)S(1)}, bf16[32,256,8,128]{3,1,2,0:T(8,128)(2,1)}, u32[]{:S(2)}) copy-start(bf16[32,256,8,128]{3,1,2,0:T(8,128)(2,1)} %get-tuple-element.40) | copy-start | bytes 50331652
  (10 other events, 40.0 us)
where the time goes:
time: 621 us; the launch traced here: 614 us
  blocking collectives  195 us (31%)
  matrix products  167 us (27%)
  waiting for transfers between devices  109 us (18%)
  local copies, waits for them, and re-layouts  89.6 us (14%)
  other arithmetic  44.5 us (7%)
  starting transfers between devices  7.14 us (1%)
    all_to_all x1, blocking collectives, local_run(): k_local = lax.all_to_all(k_heads, 'x', 0, 2, tiled=True)  195 us
    all_to_all x1, waiting for transfers between devices, local_run(): v_local = lax.all_to_all(v_heads, 'x', 0, 2, tiled=True)  109 us
    dot_general x1, matrix products, finish(): jnp.einsum('sbf,fd->sbd', activated, w_down, preferred_element_type=jnp.f...  66.9 us
    unnamed x79, local copies, waits for them, and re-layouts  41 us
    dot_general x1, matrix products, finish(): jnp.einsum('sbd,df->sbf', normed, w_gate, preferred_element_type=jnp.floa...  36.2 us
    select_n x1, other arithmetic, write_slots(): cache_arr = jnp.where(slot_hit, fresh_rows[step_idx][:, None], cache_arr)  22.9 us
    all_to_all x1, local copies, waits for them, and re-layouts, local_run(): v_local = lax.all_to_all(v_heads, 'x', 0, 2, tiled=True)  15.4 us
    all_to_all x1, local copies, waits for them, and re-layouts, local_run(): k_local = lax.all_to_all(k_heads, 'x', 0, 2, tiled=True)  15.2 us
  transfers between devices with their start and end apart: 1, of which 1 were waited for; matrix products, arithmetic and copies ran while one was open for 12% of the time, Pallas kernels for 0%

commit v1 on v0

v1 whole, which is shorter than its diff:
```python
import jax
import jax.numpy as jnp
from jax import lax
from jax.experimental import pallas as pl
from jax.experimental.pallas import tpu as pltpu
from jax.sharding import PartitionSpec as P


EPS = 1e-6
THETA = 1000000.0
GROUP = 4
STEPS = 4
ROWS = 48
BLK = 8
UNITS = ((0, 0, 8), (0, 8, 8), (0, 16, 8), (0, 24, 8), (1, 0, 8), (1, 8, 8), (1, 16, 8), (1, 24, 4), (1, 28, 4))


def rms_norm(values, gain_vec):
    values32 = values.astype(jnp.float32)
    inv_rms = lax.rsqrt(jnp.mean(values32 * values32, axis=-1, keepdims=True) + EPS)
    return values32 * inv_rms * gain_vec.astype(jnp.float32)


def rotary(values, positions):
    head_dim = values.shape[-1]
    half_dim = head_dim // 2
    inv_freq = jnp.power(THETA, -jnp.arange(half_dim, dtype=jnp.float32) * 2.0 / head_dim)
    angles = positions.astype(jnp.float32)[..., None, None] * inv_freq
    cos_part = jnp.cos(angles)
    sin_part = jnp.sin(angles)
    first_half = values[..., :half_dim]
    second_half = values[..., half_dim:]
    return jnp.concatenate([first_half * cos_part - second_half * sin_part, second_half * cos_part + first_half * sin_part], axis=-1)


def project(hidden, positions, attn_norm, w_q, w_k, w_v, q_norm, k_norm):
    n_steps, num_rows = hidden.shape[0], hidden.shape[1]
    head_dim = q_norm.shape[0]
    normed = rms_norm(hidden, attn_norm).astype(jnp.bfloat16)
    queries = jnp.einsum('sbd,de->sbe', normed, w_q, preferred_element_type=jnp.float32).reshape(n_steps, num_rows, -1, head_dim)
    keys_new = jnp.einsum('sbd,de->sbe', normed, w_k, preferred_element_type=jnp.float32).reshape(n_steps, num_rows, -1, head_dim)
    values_new = jnp.einsum('sbd,de->sbe', normed, w_v, preferred_element_type=jnp.float32).reshape(n_steps, num_rows, -1, head_dim)
    queries = rotary(rms_norm(queries, q_norm), positions).astype(jnp.bfloat16)
    keys_new = rotary(rms_norm(keys_new, k_norm), positions).astype(jnp.bfloat16)
    return queries, keys_new, values_new.astype(jnp.bfloat16)


def finish(hidden, flat_attn, w_o, mlp_norm, w_gate, w_up, w_down):
    attn_out = jnp.einsum('sbe,ed->sbd', flat_attn, w_o, preferred_element_type=jnp.float32)
    residual = (hidden.astype(jnp.float32) + attn_out).astype(jnp.bfloat16)
    normed = rms_norm(residual, mlp_norm).astype(jnp.bfloat16)
    gate_val = jnp.einsum('sbd,df->sbf', normed, w_gate, preferred_element_type=jnp.float32)
    up_val = jnp.einsum('sbd,df->sbf', normed, w_up, preferred_element_type=jnp.float32)
    activated = (jax.nn.silu(gate_val) * up_val).astype(jnp.bfloat16)
    down_val = jnp.einsum('sbf,fd->sbd', activated, w_down, preferred_element_type=jnp.float32)
    return (residual.astype(jnp.float32) + down_val).astype(jnp.bfloat16)


def one_sequence(packed, keys, values, pos):
    n_cols = keys.shape[0]
    head_dim = keys.shape[1]
    scale = head_dim ** -0.5
    q = packed[0:32]
    k_new = packed[32:40]
    v_new = packed[40:48]
    nt = (((1,), (1,)), ((), ()))
    old = lax.dot_general(q, keys, nt, preferred_element_type=jnp.float32) * scale
    new = lax.dot_general(q, k_new, nt, preferred_element_type=jnp.float32) * scale
    row = lax.broadcasted_iota(jnp.int32, (32, n_cols), 0)
    col = lax.broadcasted_iota(jnp.int32, (32, n_cols), 1)
    bound = 2 * pos
    ok = jnp.logical_and((col & 1) == (row >> 4), col < bound)
    old = jnp.where(ok, old, -jnp.inf)
    row2 = lax.broadcasted_iota(jnp.int32, (32, 8), 0)
    col2 = lax.broadcasted_iota(jnp.int32, (32, 8), 1)
    ok2 = jnp.logical_and((col2 & 1) == (row2 >> 4), (col2 >> 1) <= (row2 & 3))
    new = jnp.where(ok2, new, -jnp.inf)
    peak = jnp.maximum(jnp.max(old, axis=1, keepdims=True), jnp.max(new, axis=1, keepdims=True))
    w_old = jnp.exp(old - peak)
    w_new = jnp.exp(new - peak)
    total = jnp.sum(w_old, axis=1, keepdims=True) + jnp.sum(w_new, axis=1, keepdims=True)
    mixed = jnp.dot(w_old.astype(jnp.bfloat16), values, preferred_element_type=jnp.float32)
    mixed = mixed + jnp.dot(w_new.astype(jnp.bfloat16), v_new, preferred_element_type=jnp.float32)
    return (mixed / total).astype(jnp.bfloat16)


def attend_source(packed, k_rows, v_rows, start_pos, me):
    n = packed.shape[1]
    seqs = k_rows.shape[0] // GROUP
    per = seqs // BLK

    def body(me_ref, pos_ref, packed_ref, k_ref, v_ref, out_ref):
        base = (me_ref[0] ^ pl.program_id(0)) * seqs + pl.program_id(1) * BLK
        for b in range(BLK):
            out_ref[0, b] = one_sequence(packed_ref[0, b], k_ref[b], v_ref[b], pos_ref[base + b])

    cache_spec = pl.BlockSpec((BLK,) + k_rows.shape[1:], lambda o, i, me_ref, pos_ref: ((me_ref[0] ^ o) * per + i, 0, 0))
    return pl.pallas_call(
        body,
        grid_spec=pltpu.PrefetchScalarGridSpec(
            num_scalar_prefetch=2,
            grid=(GROUP, n // BLK),
            in_specs=[pl.BlockSpec((1, BLK, ROWS, 128), lambda o, i, *_: (o, i, 0, 0)), cache_spec, cache_spec],
            out_specs=pl.BlockSpec((1, BLK, 32, 128), lambda o, i, *_: (o, i, 0, 0)),
        ),
        out_shape=jax.ShapeDtypeStruct((GROUP, n, 32, 128), jnp.bfloat16),
        cost_estimate=pl.CostEstimate(flops=40_000_000_000, bytes_accessed=2 * k_rows.size * 2, transcendentals=0),
        name="attend_source",
    )(me, start_pos, packed, k_rows, v_rows)


def assemble(cache, recvs, fresh, pos, me, first, count, prev):
    seqs = cache.shape[0] // GROUP
    slots = cache.shape[1]
    half = count // 2 if count > 1 else count
    parts = [(p, half) for p in range(0, count, half)]

    def body(me_ref, pos_ref, cache_ref, r1, r2, r3, fresh_ref, *rest):
        out_ref, buf, in_sems, out_sems = rest[-4:]
        mine = me_ref[0]

        def load(p, size, k, off):
            if off == 0:
                src = cache_ref.at[pl.ds(mine * seqs + first + p, size)]
            else:
                src = (r1, r2, r3)[off - 1].at[pl.ds(p, size)]
            return pltpu.make_async_copy(src, buf.at[pl.ds(p, size), :, mine ^ off], in_sems.at[k, off])

        def store(p, size, k):
            return pltpu.make_async_copy(buf.at[pl.ds(p, size)], out_ref.at[pl.ds(first + p, size)], out_sems.at[k])

        for k, (p, size) in enumerate(parts):
            for off in range(GROUP):
                load(p, size, k, off).start()
        for k, (p, size) in enumerate(parts):
            for off in range(GROUP):
                load(p, size, k, off).wait()
            for b in range(size):
                where = pos_ref[first + p + b]
                for s in range(STEPS):
                    buf[p + b, where + s] = fresh_ref[first + p + b, s]
            store(p, size, k).start()
        for k, (p, size) in enumerate(parts):
            store(p, size, k).wait()

    any_spec = pl.BlockSpec(memory_space=pl.ANY)
    smem = pl.BlockSpec(memory_space=pltpu.SMEM)
    args = [me, pos, cache, *recvs, fresh]
    specs = [smem, smem, any_spec, any_spec, any_spec, any_spec, pl.BlockSpec(memory_space=pltpu.VMEM)]
    aliases = {}
    if prev is not None:
        aliases = {len(args): 0}
        args.append(prev)
        specs.append(any_spec)
    return pl.pallas_call(
        body,
        in_specs=specs,
        out_specs=any_spec,
        out_shape=jax.ShapeDtypeStruct((seqs, slots, GROUP, 2, 128), jnp.bfloat16),
        scratch_shapes=[
            pltpu.VMEM((count, slots, GROUP, 2, 128), jnp.bfloat16),
            pltpu.SemaphoreType.DMA((len(parts), GROUP)),
            pltpu.SemaphoreType.DMA((len(parts),)),
        ],
        input_output_aliases=aliases,
        cost_estimate=pl.CostEstimate(flops=count * 1_000_000_000, bytes_accessed=count * slots * 8 * 128 * 4, transcendentals=0),
        name="assemble",
    )(*args)


def solution(mesh):
    row_spec = P(None, ('dp', 'x'), None)
    cache_in = P('dp', None, 'x', None)
    cache_out = P(('dp', 'x'), None, None, None)

    def swap(arr, off):
        return lax.ppermute(arr, 'x', [(i, i ^ off) for i in range(GROUP)])

    def layer(start_pos, hidden_in, k_heads, v_heads, attn_norm, w_q, w_k, w_v, q_norm, k_norm, w_o, mlp_norm, w_gate, w_up, w_down):
        num_rows = hidden_in.shape[1]
        n_steps = hidden_in.shape[0]
        head_dim = q_norm.shape[0]
        slots = k_heads.shape[1]
        me = lax.axis_index('x')
        me_arr = me.reshape(1).astype(jnp.int32)
        my_pos = lax.dynamic_slice_in_dim(start_pos, me * num_rows, num_rows)
        k_rows = k_heads.reshape(k_heads.shape[0], slots * 2, head_dim)
        v_rows = v_heads.reshape(v_heads.shape[0], slots * 2, head_dim)

        def send_unit(u):
            which, first, count = UNITS[u]
            rows = (k_rows, v_rows)[which]
            out = {}
            for off in (2, 3, 1):
                block = lax.dynamic_slice_in_dim(rows, (me ^ off) * num_rows + first, count)
                out[off] = swap(block, off)
            return [out[off].reshape(count, slots, 2, head_dim) for off in (1, 2, 3)]

        recvs = [send_unit(u) for u in range(len(UNITS))]

        positions = my_pos[None, :] + jnp.arange(n_steps)[:, None]
        queries, keys_new, values_new = project(hidden_in, positions, attn_norm, w_q, w_k, w_v, q_norm, k_norm)
        q_pack = queries.reshape(n_steps, num_rows, GROUP, 2, 4, head_dim).transpose(2, 1, 3, 4, 0, 5).reshape(GROUP, num_rows, 32, head_dim)
        kv_shape = (n_steps, num_rows, GROUP, 2, head_dim)
        k_pack = keys_new.reshape(kv_shape).transpose(2, 1, 0, 3, 4).reshape(GROUP, num_rows, 8, head_dim)
        v_pack = values_new.reshape(kv_shape).transpose(2, 1, 0, 3, 4).reshape(GROUP, num_rows, 8, head_dim)
        packed = jnp.concatenate([q_pack, k_pack, v_pack], axis=2)

        def owner_part(arr, off):
            return lax.dynamic_index_in_dim(arr, me ^ off, 0, keepdims=False)

        by_off = [owner_part(packed, 0)] + [swap(owner_part(packed, off), off) for off in (1, 2, 3)]
        mixed = attend_source(jnp.stack(by_off), k_rows, v_rows, start_pos, me_arr)
        back = jnp.stack([mixed[0]] + [swap(mixed[off], off) for off in (1, 2, 3)])
        owners = jnp.stack([owner_part(back, j) for j in range(GROUP)])
        attended = owners.reshape(GROUP, num_rows, 2, 4, n_steps, head_dim).transpose(4, 1, 0, 2, 3, 5).reshape(n_steps, num_rows, -1)
        out_hidden = finish(hidden_in, attended, w_o, mlp_norm, w_gate, w_up, w_down)

        k_fresh = keys_new.reshape(kv_shape).transpose(1, 0, 2, 3, 4)
        v_fresh = values_new.reshape(kv_shape).transpose(1, 0, 2, 3, 4)
        outs = [None, None]
        for u, (which, first, count) in enumerate(UNITS):
            outs[which] = assemble((k_heads, v_heads)[which], recvs[u], (k_fresh, v_fresh)[which], my_pos, me_arr, first, count, outs[which])
        k_out, v_out = outs
        full = (num_rows, slots, 2 * GROUP, head_dim)
        return out_hidden, k_out.reshape(full), v_out.reshape(full)

    return jax.shard_map(layer, mesh=mesh, in_specs=(P('dp'), row_spec, cache_in, cache_in) + (P(),) * 11, out_specs=(row_spec, cache_out, cache_out), check_vma=False)
```

time: 621 us -> 514 us (0.83); the launches traced: 614 us -> 514 us
  blocking collectives: 195 us -> 0 us
  waiting for transfers between devices: 109 us -> 230 us
  Pallas kernels: 0 us -> 78.8 us
  local copies, waits for them, and re-layouts: 89.6 us -> 30.7 us
  other arithmetic: 44.5 us -> 10.3 us
  matrix products: 167 us -> 139 us
  starting transfers between devices: 7.14 us -> 24 us
    ppermute x0 -> x33, waiting for transfers between devices: none -> 230 us  [swap(): return lax.ppermute(arr, 'x', [(i, i ^ off) for i in range(GROUP)])]
    all_to_all x1 -> x0, blocking collectives: 195 us -> none  [local_run(): k_local = lax.all_to_all(k_heads, 'x', 0, 2, tiled=True)]
    all_to_all x1 -> x0, waiting for transfers between devices: 109 us -> none  [local_run(): v_local = lax.all_to_all(v_heads, 'x', 0, 2, tiled=True)]
    pallas_call x0 -> x10, Pallas kernels: none -> 78.8 us  [the longest x9 39.4 us: assemble(): pl.pallas_call(body, in_specs=specs, out_specs=any_spec, out_shape=jax.Sh...]
    unnamed x79 -> x40, local copies, waits for them, and re-layouts: 41 us -> 0.56 us
    dot_general x4 -> x0, matrix products: 30.7 us -> none  [the longest x1 10.7 us: attend(): jnp.einsum('sbkgd,jbkd->bkgsj', grouped, keys_new, preferred_element_type...]
    all_to_all x2 -> x0, local copies, waits for them, and re-layouts: 30.6 us -> none  [the longest x1 15.4 us: local_run(): v_local = lax.all_to_all(v_heads, 'x', 0, 2, tiled=True)]
    ppermute x0 -> x33, starting transfers between devices: none -> 24 us  [swap(): return lax.ppermute(arr, 'x', [(i, i ^ off) for i in range(GROUP)])]
  transfers between devices with their start and end apart: 1 -> 33, of which waited for: 1 -> 15; matrix products, arithmetic and copies ran while one was open for 12% -> 33% of each run, Pallas kernels for 0% -> 14%
where the time goes in v1:
time: 514 us
  waiting for transfers between devices  230 us (45%)
  matrix products  139 us (27%)
  Pallas kernels  78.8 us (15%)
  local copies, waits for them, and re-layouts  30.7 us (6%)
  starting transfers between devices  24 us (5%)
  other arithmetic  10.3 us (2%)
    ppermute x33, waiting for transfers between devices, swap(): return lax.ppermute(arr, 'x', [(i, i ^ off) for i in range(GROUP)])  230 us
    dot_general x1, matrix products, finish(): jnp.einsum('sbf,fd->sbd', activated, w_down, preferred_element_type=jnp.f...  66.7 us
    pallas_call x9, Pallas kernels, assemble(): pl.pallas_call(body, in_specs=specs, out_specs=any_spec, out_shape=jax.Sh...  39.4 us
    pallas_call x1, Pallas kernels, attend_source(): pl.pallas_call(body, grid_spec=pltpu.PrefetchScalarGridSpec(num_scalar_pr...  39.4 us
    dot_general x1, matrix products, finish(): jnp.einsum('sbd,df->sbf', normed, w_gate, preferred_element_type=jnp.floa...  36.2 us
    ppermute x33, starting transfers between devices, swap(): return lax.ppermute(arr, 'x', [(i, i ^ off) for i in range(GROUP)])  24 us
    dynamic_slice x3, local copies, waits for them, and re-layouts, send_unit(): block = lax.dynamic_slice_in_dim(rows, (me ^ off) * num_rows + first, count)  20.3 us
    dot_general x1, matrix products, finish(): jnp.einsum('sbe,ed->sbd', flat_attn, w_o, preferred_element_type=jnp.floa...  13.3 us
  transfers between devices with their start and end apart: 33, of which 15 were waited for; matrix products, arithmetic and copies ran while one was open for 33% of the time, Pallas kernels for 14%

profile of v1, /device:TPU:0, one launch (start us, length us, event | category | flops | bytes accessed | tf_op | source)
XLA Modules:
  0.0 513.9 jit_solution(3060756204840370114)
XLA Ops:
  0.7 7.5 %constant_dynamic-slice_fusion = (bf16[8,512,128]{2,1,0:T(8,128)(2,1)}, bf16[8,512,128]{2,1,0:T(8,128)(2,1)}, bf16[8,512,128]{2,1,0:T(8,128)(2,1)}, bf16[8,512,1...) fusion(bf16[128,512,128]{2,1,0:T(8,128)(2,1)} %bitcast.147, ...), kind=kLoop, calls=%fused_computation.68 | loop fusion | bytes 18874404 | tf_op jit(solution)/shard_map/dynamic_slice | solution.py:195
  11.8 4.7 fusion.52
  17.4 4.7 fusion.20
  25.1 12.9 %fusion.8 = f32[4,32,4096]{2,1,0:T(8,128)S(1)} fusion(bf16[4096,4096]{1,0:T(8,128)(2,1)} %param.20, bf16[4,32,4096]{2,1,0:T(8,128)(2,1)S(1)} %copy-done, f32[4096]{0:T(1024)S(1)} %convert_element_type.55, f32[4,32]{1,0:T(4,128)S(1)} %copy-done.12), kind=kOutput, calls=%fused_computation.8 | convolution fusion | flops 4297064448 | bytes 36717056 | tf_op jit(solution)/shard_map/sbd,de->sbe/dot_general | solution.py:40
  50.1 9.4 %constant_dynamic-slice_fusion.15 = (bf16[8,512,128]{2,1,0:T(8,128)(2,1)}, bf16[8,512,128]{2,1,0:T(8,128)(2,1)}, bf16[8,512,128]{2,1,0:T(8,128)(2,1)}, bf16[8,51...) fusion(bf16[128,512,128]{2,1,0:T(8,128)(2,1)} %bitcast.151, ...), kind=kLoop, calls=%fused_computation.83 | loop fusion | bytes 25165872 | tf_op jit(solution)/shard_map/dynamic_slice | solution.py:195
  59.7 7.1 %collective-permute-done.2 = bf16[32,48,128]{2,1,0:T(8,128)(2,1)S(1)} collective-permute-done((bf16[32,48,128]{2,1,0:T(8,128)(2,1)S(1)}, bf16[32,48,128]{2,1,0:T(8,128)(2,1)S(1)}, u32[]{:S(2)}, u32[]{:S(2)}) %collective-permute-start.2) | collective-permute-done | bytes 393248 | tf_op jit(solution)/shard_map/ppermute | solution.py:177
  68.2 39.4 %attend_source.1 = bf16[4,32,32,128]{3,2,1,0:T(8,128)(2,1)} custom-call(s32[1]{0:T(128)} %bitcast.me_ref, s32[128]{0:T(128)} %pos_ref.1, bf16[4,32,48,128]{3,2,1,0:T(8,128)(2,1)} %pad_maximum_fusion.1.packed_ref, bf16[128,512,128]{2,1,0:T(8,128)(2,1)} %bitcast.152, bf16[128,512,128]{2,1,0:T(8,128)(2,1)} %bitcast.148), custom_call_target="tpu_custom_call" | custom-call | flops 40000000000 | bytes 33554432 | tf_op jit(solution)/shard_map/attend_source/pallas_call | solution.py:98
  126.1 13.3 %multiply_reduce_fusion = (f32[4,32]{1,0:T(4,128)S(1)}, f32[4,32,4096]{2,1,0:T(8,128)S(1)}) fusion(bf16[4,32,4096]{2,1,0:T(8,128)(2,1)} %reshape.219, bf16[4096,4096]{1,0:T(8,128)(2,1)} %param.25, bf16[4,32,4096]{2,1,0:T(8,128)(2,1)S(1)} %copy-done), kind=kOutput, calls=%fused_computation.37 | convolution fusion | flops 4298113024 | bytes 37749248 | tf_op jit(solution)/shard_map/sbe,ed->sbd/dot_general | solution.py:49
  139.5 36.2 %fusion.4 = f32[4,32,12288]{2,1,0:T(8,128)} fusion(bf16[4096,12288]{1,0:T(8,128)(2,1)} %param.27, f32[4,32,4096]{2,1,0:T(8,128)S(1)} %get-tuple-element.49, f32[4096]{0:T(1024)S(1)} %convert_element_type.64, f32[4,32]{1,0:T(4,128)S(1)} %add_rsqrt_fusion.2), kind=kOutput, calls=%fused_computation.4 | convolution fusion | flops 12886474752 | bytes 109068800 | tf_op jit(solution)/shard_map/sbd,df->sbf/dot_general | solution.py:52
  178.5 66.7 %fusion.41 = bf16[4,32,4096]{2,1,0:T(8,128)(2,1)} fusion(f32[4,32,4096]{2,1,0:T(8,128)S(1)} %get-tuple-element.49, bf16[12288,4096]{1,0:T(8,128)(2,1)} %param.29, bf16[4096,12288]{1,0:T(8,128)(2,1)} %param.28, f32[4,32,12288]{2,1,0:T(8,128)} %fusion.4, f32[4096]{0:T(1024)S(1)} %convert_element_type.64, f32[4,32]{1,0:T(4,128)S(1)} %add_rsqrt_fusion.2), kind=kOutput, calls=%fused_computation.25 | convolution fusion | flops 25781862400 | bytes 210780672 | tf_op jit(solution)/shard_map/sbf,fd->sbd/dot_general | solution.py:55
  253.8 4.7 assemble.14.rest_0_
  258.5 13.1 %collective-permute-done.25 = bf16[8,512,128]{2,1,0:T(8,128)(2,1)} collective-permute-done((bf16[8,512,128]{2,1,0:T(8,128)(2,1)}, bf16[8,512,128]{2,1,0:T(8,128)(2,1)}, u32[]{:S(2)}, u32[]{:S(2)}) %collective-permute-start.25) | collective-permute-done | bytes 1048608 | tf_op jit(solution)/shard_map/ppermute | solution.py:177
  271.6 21.7 %collective-permute-done.26 = bf16[8,512,128]{2,1,0:T(8,128)(2,1)} collective-permute-done((bf16[8,512,128]{2,1,0:T(8,128)(2,1)}, bf16[8,512,128]{2,1,0:T(8,128)(2,1)}, u32[]{:S(2)}, u32[]{:S(2)}) %collective-permute-start.26) | collective-permute-done | bytes 1048608 | tf_op jit(solution)/shard_map/ppermute | solution.py:177
  295.3 4.6 assemble.15.rest_0_
  299.9 16.7 %collective-permute-done.16 = bf16[8,512,128]{2,1,0:T(8,128)(2,1)} collective-permute-done((bf16[8,512,128]{2,1,0:T(8,128)(2,1)}, bf16[8,512,128]{2,1,0:T(8,128)(2,1)}, u32[]{:S(2)}, u32[]{:S(2)}) %collective-permute-start.16) | collective-permute-done | bytes 1048608 | tf_op jit(solution)/shard_map/ppermute | solution.py:177
  316.5 21.7 %collective-permute-done.17 = bf16[8,512,128]{2,1,0:T(8,128)(2,1)} collective-permute-done((bf16[8,512,128]{2,1,0:T(8,128)(2,1)}, bf16[8,512,128]{2,1,0:T(8,128)(2,1)}, u32[]{:S(2)}, u32[]{:S(2)}) %collective-permute-start.17) | collective-permute-done | bytes 1048608 | tf_op jit(solution)/shard_map/ppermute | solution.py:177
  343.4 50.1 %collective-permute-done.23 = bf16[4,512,128]{2,1,0:T(8,128)(2,1)} collective-permute-done((bf16[4,512,128]{2,1,0:T(8,128)(2,1)}, bf16[4,512,128]{2,1,0:T(8,128)(2,1)}, u32[]{:S(2)}, u32[]{:S(2)}) %collective-permute-start.23) | collective-permute-done | bytes 524320 | tf_op jit(solution)/shard_map/ppermute | solution.py:177
  408.7 10.6 %collective-permute-done.20 = bf16[4,512,128]{2,1,0:T(8,128)(2,1)} collective-permute-done((bf16[4,512,128]{2,1,0:T(8,128)(2,1)}, bf16[4,512,128]{2,1,0:T(8,128)(2,1)}, u32[]{:S(2)}, u32[]{:S(2)}) %collective-permute-start.20) | collective-permute-done | bytes 524320 | tf_op jit(solution)/shard_map/ppermute | solution.py:177
  424.6 17.7 %collective-permute-done.10 = bf16[8,512,128]{2,1,0:T(8,128)(2,1)} collective-permute-done((bf16[8,512,128]{2,1,0:T(8,128)(2,1)}, bf16[8,512,128]{2,1,0:T(8,128)(2,1)}, u32[]{:S(2)}, u32[]{:S(2)}) %collective-permute-start.10) | collective-permute-done | bytes 1048608 | tf_op jit(solution)/shard_map/ppermute | solution.py:177
  442.4 21.8 %collective-permute-done.11 = bf16[8,512,128]{2,1,0:T(8,128)(2,1)} collective-permute-done((bf16[8,512,128]{2,1,0:T(8,128)(2,1)}, bf16[8,512,128]{2,1,0:T(8,128)(2,1)}, u32[]{:S(2)}, u32[]{:S(2)}) %collective-permute-start.11) | collective-permute-done | bytes 1048608 | tf_op jit(solution)/shard_map/ppermute | solution.py:177
  464.2 4.6 assemble.11.rest_0_
  468.8 18.5 %collective-permute-done.7 = bf16[8,512,128]{2,1,0:T(8,128)(2,1)} collective-permute-done((bf16[8,512,128]{2,1,0:T(8,128)(2,1)S(1)}, bf16[8,512,128]{2,1,0:T(8,128)(2,1)}, u32[]{:S(2)}, u32[]{:S(2)}) %collective-permute-start.7) | collective-permute-done | bytes 1048608 | tf_op jit(solution)/shard_map/ppermute | solution.py:177
  487.3 21.8 %collective-permute-done.8 = bf16[8,512,128]{2,1,0:T(8,128)(2,1)} collective-permute-done((bf16[8,512,128]{2,1,0:T(8,128)(2,1)S(1)}, bf16[8,512,128]{2,1,0:T(8,128)(2,1)}, u32[]{:S(2)}, u32[]{:S(2)}) %collective-permute-start.8) | collective-permute-done | bytes 1048608 | tf_op jit(solution)/shard_map/ppermute | solution.py:177
  509.1 4.6 assemble.12
  (142 shorter events, 78.3 us)
Async XLA Ops:
  8.2 169.9 %collective-permute-start.30 = (bf16[8,512,128]{2,1,0:T(8,128)(2,1)}, bf16[8,512,128]{2,1,0:T(8,128)(2,1)}, u32[]{:S(2)}, u32[]{:S(2)}) collective-permute-start(bf16[8,512,128]{2,1,0:T(8,128)(2,1)} %get-tuple-element.5), channel_id=1, source_target_pairs={{0,1},{1,0},{2,3},{3,2},{4,5},{5,4},{6,7},{7,6},{8,9},{9,8},{10,11... | collective-permute-start | bytes 3145736 | tf_op jit(solution)/shard_map/ppermute | solution.py:177
  8.9 169.2 %collective-permute-start.31 = (bf16[8,512,128]{2,1,0:T(8,128)(2,1)}, bf16[8,512,128]{2,1,0:T(8,128)(2,1)}, u32[]{:S(2)}, u32[]{:S(2)}) collective-permute-start(bf16[8,512,128]{2,1,0:T(8,128)(2,1)} %get-tuple-element.4), channel_id=1, source_target_pairs={{0,2},{1,3},{2,0},{3,1},{4,6},{5,7},{6,4},{7,5},{8,10},{9,11},{10,... | collective-permute-start | bytes 3145736 | tf_op jit(solution)/shard_map/ppermute | solution.py:177
  115.7 129.5 %collective-permute-start.32 = (bf16[8,512,128]{2,1,0:T(8,128)(2,1)}, bf16[8,512,128]{2,1,0:T(8,128)(2,1)}, u32[]{:S(2)}, u32[]{:S(2)}) collective-permute-start(bf16[8,512,128]{2,1,0:T(8,128)(2,1)} %get-tuple-element.3), channel_id=1, source_target_pairs={{0,3},{1,2},{2,1},{3,0},{4,7},{5,6},{6,5},{7,4},{8,11},{9,10},{10,... | collective-permute-start | bytes 3145736 | tf_op jit(solution)/shard_map/ppermute | solution.py:177
  118.5 57.1 %collective-permute-start.21 = (bf16[4,512,128]{2,1,0:T(8,128)(2,1)}, bf16[4,512,128]{2,1,0:T(8,128)(2,1)}, u32[]{:S(2)}, u32[]{:S(2)}) collective-permute-start(bf16[4,512,128]{2,1,0:T(8,128)(2,1)} %get-tuple-element.14), channel_id=1, source_target_pairs={{0,1},{1,0},{2,3},{3,2},{4,5},{5,4},{6,7},{7,6},{8,9},{9,8},{10,11... | collective-permute-start | bytes 1572872 | tf_op jit(solution)/shard_map/ppermute | solution.py:177
  122.3 54.0 %collective-permute-start.22 = (bf16[4,512,128]{2,1,0:T(8,128)(2,1)}, bf16[4,512,128]{2,1,0:T(8,128)(2,1)}, u32[]{:S(2)}, u32[]{:S(2)}) collective-permute-start(bf16[4,512,128]{2,1,0:T(8,128)(2,1)} %get-tuple-element.13), channel_id=1, source_target_pairs={{0,2},{1,3},{2,0},{3,1},{4,6},{5,7},{6,4},{7,5},{8,10},{9,11},{10,... | collective-permute-start | bytes 1572872 | tf_op jit(solution)/shard_map/ppermute | solution.py:177
  175.7 71.3 %collective-permute-start.27 = (bf16[8,512,128]{2,1,0:T(8,128)(2,1)}, bf16[8,512,128]{2,1,0:T(8,128)(2,1)}, u32[]{:S(2)}, u32[]{:S(2)}) collective-permute-start(bf16[8,512,128]{2,1,0:T(8,128)(2,1)} %get-tuple-element.8), channel_id=1, source_target_pairs={{0,1},{1,0},{2,3},{3,2},{4,5},{5,4},{6,7},{7,6},{8,9},{9,8},{10,11... | collective-permute-start | bytes 3145736 | tf_op jit(solution)/shard_map/ppermute | solution.py:177
  176.4 70.6 %collective-permute-start.28 = (bf16[8,512,128]{2,1,0:T(8,128)(2,1)}, bf16[8,512,128]{2,1,0:T(8,128)(2,1)}, u32[]{:S(2)}, u32[]{:S(2)}) collective-permute-start(bf16[8,512,128]{2,1,0:T(8,128)(2,1)} %get-tuple-element.7), channel_id=1, source_target_pairs={{0,2},{1,3},{2,0},{3,1},{4,6},{5,7},{6,4},{7,5},{8,10},{9,11},{10,... | collective-permute-start | bytes 3145736 | tf_op jit(solution)/shard_map/ppermute | solution.py:177
  178.1 73.9 %collective-permute-start.29 = (bf16[8,512,128]{2,1,0:T(8,128)(2,1)}, bf16[8,512,128]{2,1,0:T(8,128)(2,1)}, u32[]{:S(2)}, u32[]{:S(2)}) collective-permute-start(bf16[8,512,128]{2,1,0:T(8,128)(2,1)} %get-tuple-element.6), channel_id=1, source_target_pairs={{0,3},{1,2},{2,1},{3,0},{4,7},{5,6},{6,5},{7,4},{8,11},{9,10},{10,... | collective-permute-start | bytes 3145736 | tf_op jit(solution)/shard_map/ppermute | solution.py:177
  178.1 75.6 %collective-permute-start.24 = (bf16[8,512,128]{2,1,0:T(8,128)(2,1)}, bf16[8,512,128]{2,1,0:T(8,128)(2,1)}, u32[]{:S(2)}, u32[]{:S(2)}) collective-permute-start(bf16[8,512,128]{2,1,0:T(8,128)(2,1)} %get-tuple-element.11), channel_id=1, source_target_pairs={{0,1},{1,0},{2,3},{3,2},{4,5},{5,4},{6,7},{7,6},{8,9},{9,8},{10,11... | collective-permute-start | bytes 3145736 | tf_op jit(solution)/shard_map/ppermute | solution.py:177
  245.2 26.3 %collective-permute-start.25 = (bf16[8,512,128]{2,1,0:T(8,128)(2,1)}, bf16[8,512,128]{2,1,0:T(8,128)(2,1)}, u32[]{:S(2)}, u32[]{:S(2)}) collective-permute-start(bf16[8,512,128]{2,1,0:T(8,128)(2,1)} %get-tuple-element.10), channel_id=1, source_target_pairs={{0,2},{1,3},{2,0},{3,1},{4,6},{5,7},{6,4},{7,5},{8,10},{9,11},{10,... | collective-permute-start | bytes 3145736 | tf_op jit(solution)/shard_map/ppermute | solution.py:177
  247.0 46.3 %collective-permute-start.26 = (bf16[8,512,128]{2,1,0:T(8,128)(2,1)}, bf16[8,512,128]{2,1,0:T(8,128)(2,1)}, u32[]{:S(2)}, u32[]{:S(2)}) collective-permute-start(bf16[8,512,128]{2,1,0:T(8,128)(2,1)} %get-tuple-element.9), channel_id=1, source_target_pairs={{0,3},{1,2},{2,1},{3,0},{4,7},{5,6},{6,5},{7,4},{8,11},{9,10},{10,... | collective-permute-start | bytes 3145736 | tf_op jit(solution)/shard_map/ppermute | solution.py:177
  247.0 46.9 %collective-permute-start.15 = (bf16[8,512,128]{2,1,0:T(8,128)(2,1)}, bf16[8,512,128]{2,1,0:T(8,128)(2,1)}, u32[]{:S(2)}, u32[]{:S(2)}) collective-permute-start(bf16[8,512,128]{2,1,0:T(8,128)(2,1)} %get-tuple-element.20), channel_id=1, source_target_pairs={{0,1},{1,0},{2,3},{3,2},{4,5},{5,4},{6,7},{7,6},{8,9},{9,8},{10,11... | collective-permute-start | bytes 3145736 | tf_op jit(solution)/shard_map/ppermute | solution.py:177
  252.0 64.5 %collective-permute-start.16 = (bf16[8,512,128]{2,1,0:T(8,128)(2,1)}, bf16[8,512,128]{2,1,0:T(8,128)(2,1)}, u32[]{:S(2)}, u32[]{:S(2)}) collective-permute-start(bf16[8,512,128]{2,1,0:T(8,128)(2,1)} %get-tuple-element.19), channel_id=1, source_target_pairs={{0,2},{1,3},{2,0},{3,1},{4,6},{5,7},{6,4},{7,5},{8,10},{9,11},{10,... | collective-permute-start | bytes 3145736 | tf_op jit(solution)/shard_map/ppermute | solution.py:177
  253.8 84.5 %collective-permute-start.17 = (bf16[8,512,128]{2,1,0:T(8,128)(2,1)}, bf16[8,512,128]{2,1,0:T(8,128)(2,1)}, u32[]{:S(2)}, u32[]{:S(2)}) collective-permute-start(bf16[8,512,128]{2,1,0:T(8,128)(2,1)} %get-tuple-element.18), channel_id=1, source_target_pairs={{0,3},{1,2},{2,1},{3,0},{4,7},{5,6},{6,5},{7,4},{8,11},{9,10},{10,... | collective-permute-start | bytes 3145736 | tf_op jit(solution)/shard_map/ppermute | solution.py:177
  271.6 123.9 %collective-permute-start.12 = (bf16[8,512,128]{2,1,0:T(8,128)(2,1)S(1)}, bf16[8,512,128]{2,1,0:T(8,128)(2,1)}, u32[]{:S(2)}, u32[]{:S(2)}) collective-permute-start(bf16[8,512,128]{2,1,0:T(8,128)(2,1)S(1)} %copy-done.10), channel_id=1, source_target_pairs={{0,1},{1,0},{2,3},{3,2},{4,5},{5,4},{6,7},{7,6},{8,9},{9,8},{10,11... | collective-permute-start | bytes 3145736 | tf_op jit(solution)/shard_map/ppermute | solution.py:177
  293.3 102.4 %collective-permute-start.13 = (bf16[8,512,128]{2,1,0:T(8,128)(2,1)S(1)}, bf16[8,512,128]{2,1,0:T(8,128)(2,1)}, u32[]{:S(2)}, u32[]{:S(2)}) collective-permute-start(bf16[8,512,128]{2,1,0:T(8,128)(2,1)S(1)} %copy-done.9), channel_id=1, source_target_pairs={{0,2},{1,3},{2,0},{3,1},{4,6},{5,7},{6,4},{7,5},{8,10},{9,11},{10,... | collective-permute-start | bytes 3145736 | tf_op jit(solution)/shard_map/ppermute | solution.py:177
  293.9 103.3 %collective-permute-start.14 = (bf16[8,512,128]{2,1,0:T(8,128)(2,1)S(1)}, bf16[8,512,128]{2,1,0:T(8,128)(2,1)}, u32[]{:S(2)}, u32[]{:S(2)}) collective-permute-start(bf16[8,512,128]{2,1,0:T(8,128)(2,1)S(1)} %copy-done.8), channel_id=1, source_target_pairs={{0,3},{1,2},{2,1},{3,0},{4,7},{5,6},{6,5},{7,4},{8,11},{9,10},{10,... | collective-permute-start | bytes 3145736 | tf_op jit(solution)/shard_map/ppermute | solution.py:177
  316.5 77.0 %collective-permute-start.23 = (bf16[4,512,128]{2,1,0:T(8,128)(2,1)}, bf16[4,512,128]{2,1,0:T(8,128)(2,1)}, u32[]{:S(2)}, u32[]{:S(2)}) collective-permute-start(bf16[4,512,128]{2,1,0:T(8,128)(2,1)} %get-tuple-element.12), channel_id=1, source_target_pairs={{0,3},{1,2},{2,1},{3,0},{4,7},{5,6},{6,5},{7,4},{8,11},{9,10},{10,... | collective-permute-start | bytes 1572872 | tf_op jit(solution)/shard_map/ppermute | solution.py:177
  338.3 56.7 %collective-permute-start.18 = (bf16[4,512,128]{2,1,0:T(8,128)(2,1)}, bf16[4,512,128]{2,1,0:T(8,128)(2,1)}, u32[]{:S(2)}, u32[]{:S(2)}) collective-permute-start(bf16[4,512,128]{2,1,0:T(8,128)(2,1)} %get-tuple-element.17), channel_id=1, source_target_pairs={{0,1},{1,0},{2,3},{3,2},{4,5},{5,4},{6,7},{7,6},{8,9},{9,8},{10,11... | collective-permute-start | bytes 1572872 | tf_op jit(solution)/shard_map/ppermute | solution.py:177
  395.7 46.7 %collective-permute-start.10 = (bf16[8,512,128]{2,1,0:T(8,128)(2,1)}, bf16[8,512,128]{2,1,0:T(8,128)(2,1)}, u32[]{:S(2)}, u32[]{:S(2)}) collective-permute-start(bf16[8,512,128]{2,1,0:T(8,128)(2,1)} %get-tuple-element.25), channel_id=1, source_target_pairs={{0,2},{1,3},{2,0},{3,1},{4,6},{5,7},{6,4},{7,5},{8,10},{9,11},{10,... | collective-permute-start | bytes 3145736 | tf_op jit(solution)/shard_map/ppermute | solution.py:177
  397.2 67.0 %collective-permute-start.11 = (bf16[8,512,128]{2,1,0:T(8,128)(2,1)}, bf16[8,512,128]{2,1,0:T(8,128)(2,1)}, u32[]{:S(2)}, u32[]{:S(2)}) collective-permute-start(bf16[8,512,128]{2,1,0:T(8,128)(2,1)} %get-tuple-element.24), channel_id=1, source_target_pairs={{0,3},{1,2},{2,1},{3,0},{4,7},{5,6},{6,5},{7,4},{8,11},{9,10},{10,... | collective-permute-start | bytes 3145736 | tf_op jit(solution)/shard_map/ppermute | solution.py:177
  408.7 60.1 %collective-permute-start.6 = (bf16[8,512,128]{2,1,0:T(8,128)(2,1)S(1)}, bf16[8,512,128]{2,1,0:T(8,128)(2,1)}, u32[]{:S(2)}, u32[]{:S(2)}) collective-permute-start(bf16[8,512,128]{2,1,0:T(8,128)(2,1)S(1)} %copy-done.7), channel_id=1, source_target_pairs={{0,1},{1,0},{2,3},{3,2},{4,5},{5,4},{6,7},{7,6},{8,9},{9,8},{10,11... | collective-permute-start | bytes 3145736 | tf_op jit(solution)/shard_map/ppermute | solution.py:177
  419.2 68.1 %collective-permute-start.7 = (bf16[8,512,128]{2,1,0:T(8,128)(2,1)S(1)}, bf16[8,512,128]{2,1,0:T(8,128)(2,1)}, u32[]{:S(2)}, u32[]{:S(2)}) collective-permute-start(bf16[8,512,128]{2,1,0:T(8,128)(2,1)S(1)} %copy-done.6), channel_id=1, source_target_pairs={{0,2},{1,3},{2,0},{3,1},{4,6},{5,7},{6,4},{7,5},{8,10},{9,11},{10,... | collective-permute-start | bytes 3145736 | tf_op jit(solution)/shard_map/ppermute | solution.py:177
  421.0 88.1 %collective-permute-start.8 = (bf16[8,512,128]{2,1,0:T(8,128)(2,1)S(1)}, bf16[8,512,128]{2,1,0:T(8,128)(2,1)}, u32[]{:S(2)}, u32[]{:S(2)}) collective-permute-start(bf16[8,512,128]{2,1,0:T(8,128)(2,1)S(1)} %copy-done.5), channel_id=1, source_target_pairs={{0,3},{1,2},{2,1},{3,0},{4,7},{5,6},{6,5},{7,4},{8,11},{9,10},{10,... | collective-permute-start | bytes 3145736 | tf_op jit(solution)/shard_map/ppermute | solution.py:177
  (28 other events, 336.7 us)

commit v2 on v0

v2 whole, which is shorter than its diff:
```python
import jax
import jax.numpy as jnp
from jax import lax
from jax.experimental import pallas as pl
from jax.experimental.pallas import tpu as pltpu
from jax.sharding import PartitionSpec as P


EPS = 1e-6
THETA = 1000000.0
GROUP = 4
STEPS = 4
GROUPS = ((0, 2), (2, 8), (10, 6), (16, 2))
EARLY = 18
LATE = ((18, 8), (26, 5), (31, 1))
UNITS = GROUPS + LATE


def rms_norm(values, gain_vec):
    values32 = values.astype(jnp.float32)
    inv_rms = lax.rsqrt(jnp.mean(values32 * values32, axis=-1, keepdims=True) + EPS)
    return values32 * inv_rms * gain_vec.astype(jnp.float32)


def rotary(values, positions):
    head_dim = values.shape[-1]
    half_dim = head_dim // 2
    inv_freq = jnp.power(THETA, -jnp.arange(half_dim, dtype=jnp.float32) * 2.0 / head_dim)
    angles = positions.astype(jnp.float32)[..., None, None] * inv_freq
    cos_part = jnp.cos(angles)
    sin_part = jnp.sin(angles)
    first_half = values[..., :half_dim]
    second_half = values[..., half_dim:]
    return jnp.concatenate([first_half * cos_part - second_half * sin_part, second_half * cos_part + first_half * sin_part], axis=-1)


def project(hidden, positions, attn_norm, w_q, w_k, w_v, q_norm, k_norm):
    n_steps, num_rows = hidden.shape[0], hidden.shape[1]
    head_dim = q_norm.shape[0]
    normed = rms_norm(hidden, attn_norm).astype(jnp.bfloat16)
    queries = jnp.einsum('sbd,de->sbe', normed, w_q, preferred_element_type=jnp.float32).reshape(n_steps, num_rows, -1, head_dim)
    keys_new = jnp.einsum('sbd,de->sbe', normed, w_k, preferred_element_type=jnp.float32).reshape(n_steps, num_rows, -1, head_dim)
    values_new = jnp.einsum('sbd,de->sbe', normed, w_v, preferred_element_type=jnp.float32).reshape(n_steps, num_rows, -1, head_dim)
    queries = rotary(rms_norm(queries, q_norm), positions).astype(jnp.bfloat16)
    keys_new = rotary(rms_norm(keys_new, k_norm), positions).astype(jnp.bfloat16)
    return queries, keys_new, values_new.astype(jnp.bfloat16)


def finish(hidden, flat_attn, w_o, mlp_norm, w_gate, w_up, w_down):
    attn_out = jnp.einsum('sbe,ed->sbd', flat_attn, w_o, preferred_element_type=jnp.float32)
    residual = (hidden.astype(jnp.float32) + attn_out).astype(jnp.bfloat16)
    normed = rms_norm(residual, mlp_norm).astype(jnp.bfloat16)
    gate_val = jnp.einsum('sbd,df->sbf', normed, w_gate, preferred_element_type=jnp.float32)
    up_val = jnp.einsum('sbd,df->sbf', normed, w_up, preferred_element_type=jnp.float32)
    activated = (jax.nn.silu(gate_val) * up_val).astype(jnp.bfloat16)
    down_val = jnp.einsum('sbf,fd->sbd', activated, w_down, preferred_element_type=jnp.float32)
    return (residual.astype(jnp.float32) + down_val).astype(jnp.bfloat16)


def attend_four(packed, keys, values, bounds, own_cols, new_ok):
    scale = keys[0].shape[1] ** -0.5
    nt = (((1,), (1,)), ((), ()))
    items = range(len(keys))
    old = [lax.dot_general(packed[i][0:32], keys[i], nt, preferred_element_type=jnp.float32) for i in items]
    new = [lax.dot_general(packed[i][0:32], packed[i][32:40], nt, preferred_element_type=jnp.float32) for i in items]
    old = [jnp.where(own_cols < bounds[i], old[i] * scale, -jnp.inf) for i in items]
    new = [jnp.where(new_ok, new[i] * scale, -jnp.inf) for i in items]
    peak = [jnp.maximum(jnp.max(old[i], axis=1, keepdims=True), jnp.max(new[i], axis=1, keepdims=True)) for i in items]
    w_old = [jnp.exp(old[i] - peak[i]) for i in items]
    w_new = [jnp.exp(new[i] - peak[i]) for i in items]
    mixed = [jnp.dot(w_old[i].astype(jnp.bfloat16), values[i], preferred_element_type=jnp.float32) for i in items]
    fresh = [jnp.dot(w_new[i].astype(jnp.bfloat16), packed[i][40:48], preferred_element_type=jnp.float32) for i in items]
    total = [jnp.sum(w_old[i], axis=1, keepdims=True) + jnp.sum(w_new[i], axis=1, keepdims=True) for i in items]
    return [((mixed[i] + fresh[i]) / total[i]).astype(jnp.bfloat16) for i in items]


def attend(packed, k_rows, v_rows, recvs, pos, me, first, count):
    seqs = k_rows.shape[0] // GROUP
    rows = k_rows.shape[1]
    here = recvs is not None
    live = rows - 2 * STEPS
    n_in = 5 if here else 2

    def body(me_ref, pos_ref, packed_ref, *rest):
        k_own, v_own = rest[0:2]
        out_ref, k_buf, v_buf, cols, sems = rest[n_in:]
        mine = me_ref[0]

        def load(which, off, b):
            if here and off > 0:
                src = rest[1 + off].at[which, b]
            else:
                src = (k_own, v_own)[which].at[(mine ^ off) * seqs + first + b, pl.ds(0, live)]
            return pltpu.make_async_copy(src, (k_buf, v_buf)[which].at[off, b, pl.ds(0, live)], sems.at[which, off, b])

        @pl.loop(0, count)
        def _(b):
            for off in range(GROUP):
                v_buf[off, b, live:rows] = jnp.zeros((rows - live, 128), jnp.bfloat16)
                load(0, off, b).start()
                load(1, off, b).start()

        row = lax.broadcasted_iota(jnp.int32, (32, rows), 0)
        col = lax.broadcasted_iota(jnp.int32, (32, rows), 1)
        cols[...] = jnp.where((col & 1) == (row >> 4), col, 2 * rows)
        row2 = lax.broadcasted_iota(jnp.int32, (32, 2 * STEPS), 0)
        col2 = lax.broadcasted_iota(jnp.int32, (32, 2 * STEPS), 1)
        new_ok = jnp.logical_and((col2 & 1) == (row2 >> 4), (col2 >> 1) <= (row2 & 3))

        @pl.loop(0, count)
        def _(b):
            for off in range(GROUP):
                load(0, off, b).wait()
                load(1, off, b).wait()
            if here:
                slot = [mine ^ off for off in range(GROUP)]
                items = [packed_ref[slot[off], first + b] for off in range(GROUP)]
                bounds = [2 * pos_ref[first + b]] * GROUP
            else:
                slot = list(range(GROUP))
                items = [packed_ref[off, b] for off in range(GROUP)]
                bounds = [2 * pos_ref[(mine ^ off) * seqs + first + b] for off in range(GROUP)]
            done = attend_four(items, [k_buf[off, b] for off in range(GROUP)], [v_buf[off, b] for off in range(GROUP)], bounds, cols[...], new_ok)
            for off in range(GROUP):
                out_ref[slot[off], b] = done[off]

    any_spec = pl.BlockSpec(memory_space=pl.ANY)
    smem = pl.BlockSpec(memory_space=pltpu.SMEM)
    vmem = pl.BlockSpec(memory_space=pltpu.VMEM)
    return pl.pallas_call(
        body,
        in_specs=[smem, smem, vmem] + [any_spec] * n_in,
        out_specs=vmem,
        out_shape=jax.ShapeDtypeStruct((GROUP, count, 32, 128), jnp.bfloat16),
        scratch_shapes=[
            pltpu.VMEM((GROUP, count, rows, 128), jnp.bfloat16),
            pltpu.VMEM((GROUP, count, rows, 128), jnp.bfloat16),
            pltpu.VMEM((32, rows), jnp.int32),
            pltpu.SemaphoreType.DMA((2, GROUP, count)),
        ],
        cost_estimate=pl.CostEstimate(flops=count * 1_000_000_000, bytes_accessed=4 * count * 512 * 128 * 4, transcendentals=0),
        name="attend_here" if here else "attend_source",
    )(me, pos, packed, k_rows, v_rows, *(recvs or ()))


def spare_slot(where, i, live):
    return jnp.where(where <= live - STEPS, live + i, jnp.minimum(where + STEPS + i, live + STEPS - 1))


def cut(k_heads, v_heads, start_pos, me, first, count):
    seqs = k_heads.shape[0] // GROUP
    slots = k_heads.shape[1]
    live = slots - STEPS
    offs = (2, 3, 1)

    def body(me_ref, pos_ref, k_ref, v_ref, out2, out3, out1, buf, in_sems, out_sems):
        mine = me_ref[0]
        outs = (out2, out3, out1)

        def load(k, c, b):
            return pltpu.make_async_copy((k_ref, v_ref)[c].at[(mine ^ offs[k]) * seqs + first + b], buf.at[k, c, b], in_sems.at[k, c, b])

        def store(k, c, b):
            return pltpu.make_async_copy(buf.at[k, c, b, pl.ds(0, live)], outs[k].at[c, b], out_sems.at[k, c, b])

        for k in range(3):

            @pl.loop(0, count)
            def _(b):
                for c in range(2):
                    load(k, c, b).start()

        for k in range(3):

            @pl.loop(0, count)
            def _(b):
                where = pos_ref[(mine ^ offs[k]) * seqs + first + b]
                for c in range(2):
                    load(k, c, b).wait()
                    for i in range(STEPS):
                        buf[k, c, b, where + i] = buf[k, c, b, spare_slot(where, i, live)]
                    store(k, c, b).start()

        for k in range(3):

            @pl.loop(0, count)
            def _(b):
                for c in range(2):
                    store(k, c, b).wait()

    any_spec = pl.BlockSpec(memory_space=pl.ANY)
    smem = pl.BlockSpec(memory_space=pltpu.SMEM)
    out = pl.pallas_call(
        body,
        in_specs=[smem, smem, any_spec, any_spec],
        out_specs=[any_spec] * 3,
        out_shape=[jax.ShapeDtypeStruct((2, count, live, 2, 128), jnp.bfloat16)] * 3,
        scratch_shapes=[
            pltpu.VMEM((3, 2, count, slots, 2, 128), jnp.bfloat16),
            pltpu.SemaphoreType.DMA((3, 2, count)),
            pltpu.SemaphoreType.DMA((3, 2, count)),
        ],
        cost_estimate=pl.CostEstimate(flops=count * 600_000_000, bytes_accessed=6 * count * slots * 2 * 128 * 4, transcendentals=0),
        name="cut",
    )(me, start_pos, k_heads, v_heads)
    return dict(zip(offs, out))


def assemble(k_heads, v_heads, recvs, fresh, pos, me, first, count, prev):
    seqs = k_heads.shape[0] // GROUP
    slots = k_heads.shape[1]
    live = slots - STEPS

    def body(me_ref, pos_ref, k_ref, v_ref, r1, r2, r3, k_fresh, v_fresh, *rest):
        k_out, v_out, buf, fresh_buf, in_sems, fresh_sems, out_sems = rest[-7:]
        mine = me_ref[0]

        def load(c, b, off):
            if off == 0:
                return pltpu.make_async_copy((k_ref, v_ref)[c].at[mine * seqs + first + b], buf.at[c, b, :, mine], in_sems.at[c, b, 0])
            return pltpu.make_async_copy((r1, r2, r3)[off - 1].at[c, b], buf.at[c, b, pl.ds(0, live), mine ^ off], in_sems.at[c, b, off])

        def load_fresh(c):
            return pltpu.make_async_copy((k_fresh, v_fresh)[c].at[pl.ds(first, count)], fresh_buf.at[c], fresh_sems.at[c])

        def store(c, b):
            return pltpu.make_async_copy(buf.at[c, b], (k_out, v_out)[c].at[first + b], out_sems.at[c, b])

        own = lax.broadcasted_iota(jnp.int32, (GROUP, 2, 128), 0) == mine
        for c in range(2):
            load_fresh(c).start()

        @pl.loop(0, count)
        def _(b):
            for c in range(2):
                for off in range(GROUP):
                    load(c, b, off).start()

        for c in range(2):
            load_fresh(c).wait()

        @pl.loop(0, count)
        def _(b):
            where = pos_ref[first + b]
            for c in range(2):
                for off in range(GROUP):
                    load(c, b, off).wait()
                for i in range(STEPS):
                    spare = spare_slot(where, i, live)
                    moved = jnp.where(own, buf[c, b, spare], buf[c, b, where + i])

                    @pl.when(where + i < live)
                    def _():
                        buf[c, b, spare] = moved

                for s in range(STEPS):
                    buf[c, b, where + s] = fresh_buf[c, b, s]
                store(c, b).start()

        @pl.loop(0, count)
        def _(b):
            for c in range(2):
                store(c, b).wait()

    any_spec = pl.BlockSpec(memory_space=pl.ANY)
    smem = pl.BlockSpec(memory_space=pltpu.SMEM)
    args = [me, pos, k_heads, v_heads, *recvs, *fresh]
    aliases = {}
    if prev is not None:
        aliases = {len(args): 0, len(args) + 1: 1}
        args += prev
    return pl.pallas_call(
        body,
        in_specs=[smem, smem] + [any_spec] * (len(args) - 2),
        out_specs=[any_spec] * 2,
        out_shape=[jax.ShapeDtypeStruct((seqs, slots, GROUP, 2, 128), jnp.bfloat16)] * 2,
        scratch_shapes=[
            pltpu.VMEM((2, count, slots, GROUP, 2, 128), jnp.bfloat16),
            pltpu.VMEM((2, count, STEPS, GROUP, 2, 128), jnp.bfloat16),
            pltpu.SemaphoreType.DMA((2, count, GROUP)),
            pltpu.SemaphoreType.DMA((2,)),
            pltpu.SemaphoreType.DMA((2, count)),
        ],
        input_output_aliases=aliases,
        cost_estimate=pl.CostEstimate(flops=count * 600_000_000, bytes_accessed=2 * count * slots * 8 * 128 * 4, transcendentals=0),
        name="assemble",
    )(*args)


def solution(mesh):
    row_spec = P(None, ('dp', 'x'), None)
    cache_in = P('dp', None, 'x', None)
    cache_out = P(('dp', 'x'), None, None, None)

    def swap(arr, off):
        return lax.ppermute(arr, 'x', [(i, i ^ off) for i in range(GROUP)])

    def layer(start_pos, hidden_in, k_heads, v_heads, attn_norm, w_q, w_k, w_v, q_norm, k_norm, w_o, mlp_norm, w_gate, w_up, w_down):
        num_rows = hidden_in.shape[1]
        n_steps = hidden_in.shape[0]
        head_dim = q_norm.shape[0]
        slots = k_heads.shape[1]
        me = lax.axis_index('x')
        me_arr = me.reshape(1).astype(jnp.int32)
        my_pos = lax.dynamic_slice_in_dim(start_pos, me * num_rows, num_rows)
        k_rows = k_heads.reshape(k_heads.shape[0], slots * 2, head_dim)
        v_rows = v_heads.reshape(v_heads.shape[0], slots * 2, head_dim)

        def send_unit(u):
            first, count = UNITS[u]
            parts = cut(k_heads, v_heads, start_pos, me_arr, first, count)
            out = {off: swap(parts[off], off) for off in (2, 3, 1)}
            return [out[off] for off in (1, 2, 3)]

        recvs = [send_unit(u) for u in range(len(UNITS))]

        positions = my_pos[None, :] + jnp.arange(n_steps)[:, None]
        queries, keys_new, values_new = project(hidden_in, positions, attn_norm, w_q, w_k, w_v, q_norm, k_norm)
        q_pack = queries.reshape(n_steps, num_rows, GROUP, 2, 4, head_dim).transpose(2, 1, 3, 4, 0, 5).reshape(GROUP, num_rows, 32, head_dim)
        kv_shape = (n_steps, num_rows, GROUP, 2, head_dim)
        k_pack = keys_new.reshape(kv_shape).transpose(2, 1, 0, 3, 4).reshape(GROUP, num_rows, 8, head_dim)
        v_pack = values_new.reshape(kv_shape).transpose(2, 1, 0, 3, 4).reshape(GROUP, num_rows, 8, head_dim)
        packed = jnp.concatenate([q_pack, k_pack, v_pack], axis=2)

        def owner_part(arr, off):
            return lax.dynamic_index_in_dim(arr, me ^ off, 0, keepdims=False)

        late = packed[:, EARLY:]
        by_off = [owner_part(late, 0)] + [swap(owner_part(late, off), off) for off in (1, 2, 3)]
        mixed = attend(jnp.stack(by_off), k_rows, v_rows, None, start_pos, me_arr, EARLY, num_rows - EARLY)
        back = jnp.stack([mixed[0]] + [swap(mixed[off], off) for off in (1, 2, 3)])
        here = []
        for g, (first, count) in enumerate(GROUPS):
            arrived = [r.reshape(2, count, -1, head_dim) for r in recvs[g]]
            here.append(attend(packed, k_rows, v_rows, arrived, my_pos, me_arr, first, count))
        there = jnp.stack([owner_part(back, j) for j in range(GROUP)])
        owners = jnp.concatenate(here + [there], axis=1)
        attended = owners.reshape(GROUP, num_rows, 2, 4, n_steps, head_dim).transpose(4, 1, 0, 2, 3, 5).reshape(n_steps, num_rows, -1)
        out_hidden = finish(hidden_in, attended, w_o, mlp_norm, w_gate, w_up, w_down)

        k_fresh = keys_new.reshape(kv_shape).transpose(1, 0, 2, 3, 4)
        v_fresh = values_new.reshape(kv_shape).transpose(1, 0, 2, 3, 4)
        outs = None
        for u, (first, count) in enumerate(UNITS):
            outs = assemble(k_heads, v_heads, recvs[u], (k_fresh, v_fresh), my_pos, me_arr, first, count, outs)
        k_out, v_out = outs
        full = (num_rows, slots, 2 * GROUP, head_dim)
        return out_hidden, k_out.reshape(full), v_out.reshape(full)


    return jax.shard_map(layer, mesh=mesh, in_specs=(P('dp'), row_spec, cache_in, cache_in) + (P(),) * 11, out_specs=(row_spec, cache_out, cache_out), check_vma=False)
```

time: 621 us -> 451 us (0.73); the launches traced: 614 us -> 450 us
  blocking collectives: 195 us -> 0 us
  Pallas kernels: 0 us -> 109 us
  local copies, waits for them, and re-layouts: 89.6 us -> 18.9 us
  waiting for transfers between devices: 109 us -> 153 us
  other arithmetic: 44.5 us -> 11.5 us
  matrix products: 167 us -> 136 us
  starting transfers between devices: 7.14 us -> 19.6 us
    all_to_all x1 -> x0, blocking collectives: 195 us -> none  [local_run(): k_local = lax.all_to_all(k_heads, 'x', 0, 2, tiled=True)]
    ppermute x0 -> x27, waiting for transfers between devices: none -> 153 us  [swap(): return lax.ppermute(arr, 'x', [(i, i ^ off) for i in range(GROUP)])]
    pallas_call x0 -> x19, Pallas kernels: none -> 109 us  [the longest x5 39.4 us: attend(): pl.pallas_call(body, in_specs=[smem, smem, vmem] + [any_spec] * n_in, out...]
    all_to_all x1 -> x0, waiting for transfers between devices: 109 us -> none  [local_run(): v_local = lax.all_to_all(v_heads, 'x', 0, 2, tiled=True)]
    unnamed x79 -> x68, local copies, waits for them, and re-layouts: 41 us -> 8.25 us
    dot_general x4 -> x0, matrix products: 30.7 us -> none  [the longest x1 10.7 us: attend(): jnp.einsum('sbkgd,jbkd->bkgsj', grouped, keys_new, preferred_element_type...]
    all_to_all x2 -> x0, local copies, waits for them, and re-layouts: 30.6 us -> none  [the longest x1 15.4 us: local_run(): v_local = lax.all_to_all(v_heads, 'x', 0, 2, tiled=True)]
    select_n x1 -> x0, other arithmetic: 22.9 us -> none  [write_slots(): cache_arr = jnp.where(slot_hit, fresh_rows[step_idx][:, None], cache_arr)]
  transfers between devices with their start and end apart: 1 -> 27, of which waited for: 1 -> 10; matrix products, arithmetic and copies ran while one was open for 12% -> 36% of each run, Pallas kernels for 0% -> 23%
where the time goes in v2:
time: 451 us; the launch traced here: 450 us
  waiting for transfers between devices  153 us (34%)
  matrix products  136 us (30%)
  Pallas kernels  109 us (24%)
  starting transfers between devices  19.6 us (4%)
  local copies, waits for them, and re-layouts  18.9 us (4%)
  other arithmetic  11.5 us (3%)
    ppermute x27, waiting for transfers between devices, swap(): return lax.ppermute(arr, 'x', [(i, i ^ off) for i in range(GROUP)])  153 us
    dot_general x1, matrix products, finish(): jnp.einsum('sbf,fd->sbd', activated, w_down, preferred_element_type=jnp.f...  66.6 us
    pallas_call x5, Pallas kernels, attend(): pl.pallas_call(body, in_specs=[smem, smem, vmem] + [any_spec] * n_in, out...  39.4 us
    pallas_call x7, Pallas kernels, assemble(): pl.pallas_call(body, in_specs=[smem, smem] + [any_spec] * (len(args) - 2)...  37.6 us
    dot_general x1, matrix products, finish(): jnp.einsum('sbd,df->sbf', normed, w_gate, preferred_element_type=jnp.floa...  36.5 us
    pallas_call x7, Pallas kernels, cut(): pl.pallas_call(body, in_specs=[smem, smem, any_spec, any_spec], out_specs...  32.5 us
    ppermute x27, starting transfers between devices, swap(): return lax.ppermute(arr, 'x', [(i, i ^ off) for i in range(GROUP)])  19.6 us
    dot_general x1, matrix products, finish(): jnp.einsum('sbe,ed->sbd', flat_attn, w_o, preferred_element_type=jnp.floa...  13.3 us
  transfers between devices with their start and end apart: 27, of which 10 were waited for; matrix products, arithmetic and copies ran while one was open for 36% of the time, Pallas kernels for 23%

profile of v2, /device:TPU:0, one launch (start us, length us, event | category | flops | bytes accessed | tf_op | source)
XLA Modules:
  0.0 450.1 jit_solution(7178653965924848904)
XLA Ops:
  8.1 4.8 %fusion.20 = f32[4,32,1024]{2,1,0:T(8,128)S(1)} fusion(bf16[4096,1024]{1,0:T(8,128)(2,1)} %param.21, bf16[4,32,4096]{2,1,0:T(8,128)(2,1)S(1)} %copy-done.1, f32[4096]{0:T(1024)S(1)} %convert_element_type.55, f32[4,32]{1,0:T(4,128)S(1)} %add_rsqrt_fusion.3), kind=kOutput, calls=%fused_computation.14 | convolution fusion | flops 1075838976 | bytes 9978368 | tf_op jit(solution)/shard_map/sbd,de->sbe/dot_general | solution.py:42
  17.5 13.0 %fusion.8 = f32[4,32,4096]{2,1,0:T(8,128)S(1)} fusion(bf16[4096,4096]{1,0:T(8,128)(2,1)} %param.20, bf16[4,32,4096]{2,1,0:T(8,128)(2,1)S(1)} %copy-done.1, f32[4096]{0:T(1024)S(1)} %convert_element_type.55, f32[4,32]{1,0:T(4,128)} %copy-done.17), kind=kOutput, calls=%fused_computation.8 | convolution fusion | flops 4297064448 | bytes 36717056 | tf_op jit(solution)/shard_map/sbd,de->sbe/dot_general | solution.py:41
  40.7 5.6 %cut.9 = (bf16[2,6,252,2,128]{4,3,2,1,0:T(2,128)(2,1)}, bf16[2,6,252,2,128]{4,3,2,1,0:T(2,128)(2,1)}, bf16[2,6,252,2,128]{4,3,2,1,0:T(2,128)(2,1)}) custom-call(s32[1]{0:T(128)} %bitcast.me_ref, s32[128]{0:T(128)} %pos_ref.15, bf16[128,256,2,128]{3,2,1,0:T(2,128)(2,1)} %k_ref.27, bf16[128,256,2,128]{3,2,1,0:T(2,128)(2,1)} %v_ref.27), custom_call_target="tpu_custom_call" | custom-call | flops 3600000000 | bytes 9437184 | tf_op jit(solution)/shard_map/cut/pallas_call | solution.py:193
  49.8 13.1 %attend_source.1 = bf16[4,14,32,128]{3,2,1,0:T(8,128)(2,1)} custom-call(s32[1]{0:T(128)} %bitcast.me_ref, s32[128]{0:T(128)} %pos_ref.15, bf16[4,14,48,128]{3,2,1,0:T(8,128)(2,1)} %pad_maximum_fusion.1.packed_ref, bf16[128,512,128]{2,1,0:T(8,128)(2,1)} %bitcast.132, bf16[128,512,128]{2,1,0:T(8,128)(2,1)} %bitcast.137), custom_call_target="tpu_custom_call" | custom-call | flops 14000000000 | bytes 14680064 | tf_op jit(solution)/shard_map/attend_source/pallas_call | solution.py:130
  78.3 6.6 %cut.8 = (bf16[2,8,252,2,128]{4,3,2,1,0:T(2,128)(2,1)}, bf16[2,8,252,2,128]{4,3,2,1,0:T(2,128)(2,1)}, bf16[2,8,252,2,128]{4,3,2,1,0:T(2,128)(2,1)}) custom-call(s32[1]{0:T(128)} %bitcast.me_ref, s32[128]{0:T(128)} %pos_ref.15, bf16[128,256,2,128]{3,2,1,0:T(2,128)(2,1)} %k_ref.27, bf16[128,256,2,128]{3,2,1,0:T(2,128)(2,1)} %v_ref.27), custom_call_target="tpu_custom_call" | custom-call | flops 4800000000 | bytes 12582912 | tf_op jit(solution)/shard_map/cut/pallas_call | solution.py:193
  86.1 8.6 %collective-permute-done.10.r2 = bf16[2,2,252,2,128]{4,3,2,1,0:T(2,128)(2,1)} collective-permute-done((bf16[2,2,252,2,128]{4,3,2,1,0:T(2,128)(2,1)}, bf16[2,2,252,2,128]{4,3,2,1,0:T(2,128)(2,1)}, u32[]{:S(2)}, u32[]{:S(2)}) %collective-permute-start.10) | collective-permute-done | bytes 516128 | tf_op jit(solution)/shard_map/ppermute | solution.py:296
  96.3 10.5 %collective-permute-done.11.r3 = bf16[2,2,252,2,128]{4,3,2,1,0:T(2,128)(2,1)} collective-permute-done((bf16[2,2,252,2,128]{4,3,2,1,0:T(2,128)(2,1)}, bf16[2,2,252,2,128]{4,3,2,1,0:T(2,128)(2,1)}, u32[]{:S(2)}, u32[]{:S(2)}) %collective-permute-start.11) | collective-permute-done | bytes 516128 | tf_op jit(solution)/shard_map/ppermute | solution.py:296
  108.6 4.9 %cut.12 = (bf16[2,5,252,2,128]{4,3,2,1,0:T(2,128)(2,1)}, bf16[2,5,252,2,128]{4,3,2,1,0:T(2,128)(2,1)}, bf16[2,5,252,2,128]{4,3,2,1,0:T(2,128)(2,1)}) custom-call(s32[1]{0:T(128)} %bitcast.me_ref, s32[128]{0:T(128)} %pos_ref.15, bf16[128,256,2,128]{3,2,1,0:T(2,128)(2,1)} %k_ref.27, bf16[128,256,2,128]{3,2,1,0:T(2,128)(2,1)} %v_ref.27), custom_call_target="tpu_custom_call" | custom-call | flops 3000000000 | bytes 7864320 | tf_op jit(solution)/shard_map/cut/pallas_call | solution.py:193
  113.5 6.6 %cut.13 = (bf16[2,8,252,2,128]{4,3,2,1,0:T(2,128)(2,1)}, bf16[2,8,252,2,128]{4,3,2,1,0:T(2,128)(2,1)}, bf16[2,8,252,2,128]{4,3,2,1,0:T(2,128)(2,1)}) custom-call(s32[1]{0:T(128)} %bitcast.me_ref, s32[128]{0:T(128)} %pos_ref.15, bf16[128,256,2,128]{3,2,1,0:T(2,128)(2,1)} %k_ref.27, bf16[128,256,2,128]{3,2,1,0:T(2,128)(2,1)} %v_ref.27), custom_call_target="tpu_custom_call" | custom-call | flops 4800000000 | bytes 12582912 | tf_op jit(solution)/shard_map/cut/pallas_call | solution.py:193
  125.1 4.7 %attend_here.4 = bf16[4,2,32,128]{3,2,1,0:T(8,128)(2,1)} custom-call(s32[1]{0:T(128)} %bitcast.me_ref, s32[32]{0:T(128)} %copy-done.19, bf16[4,32,48,128]{3,2,1,0:T(8,128)(2,1)} %copy-done, bf16[128,512,128]{2,1,0:T(8,128)(2,1)} %bitcast.133, bf16[128,512,128]{2,1,0:T(8,128)(2,1)} %bitcast.138, bf16[2,2,504,128]{3,2,1,0:T(8,128)(2,1)} %bitcast.17.rest_2_, ...), custom_call_target="tpu_custom_call" | custom-call | flops 2000000000 | bytes 2097152 | tf_op jit(solution)/shard_map/attend_here/pallas_call | solution.py:130
  131.4 4.7 %attend_here.7 = bf16[4,2,32,128]{3,2,1,0:T(8,128)(2,1)} custom-call(s32[1]{0:T(128)} %bitcast.me_ref, s32[32]{0:T(128)} %copy-done.19, bf16[4,32,48,128]{3,2,1,0:T(8,128)(2,1)} %copy-done, bf16[128,512,128]{2,1,0:T(8,128)(2,1)} %bitcast.134, bf16[128,512,128]{2,1,0:T(8,128)(2,1)} %bitcast.139, bf16[2,2,504,128]{3,2,1,0:T(8,128)(2,1)} %bitcast.26.rest_2_, ...), custom_call_target="tpu_custom_call" | custom-call | flops 2000000000 | bytes 2097152 | tf_op jit(solution)/shard_map/attend_here/pallas_call | solution.py:130
  136.1 91.3 %collective-permute-done.7.r2 = bf16[2,6,252,2,128]{4,3,2,1,0:T(2,128)(2,1)} collective-permute-done((bf16[2,6,252,2,128]{4,3,2,1,0:T(2,128)(2,1)}, bf16[2,6,252,2,128]{4,3,2,1,0:T(2,128)(2,1)}, u32[]{:S(2)}, u32[]{:S(2)}) %collective-permute-start.7) | collective-permute-done | bytes 1548320 | tf_op jit(solution)/shard_map/ppermute | solution.py:296
  228.3 32.8 %collective-permute-done.8.r3 = bf16[2,6,252,2,128]{4,3,2,1,0:T(2,128)(2,1)} collective-permute-done((bf16[2,6,252,2,128]{4,3,2,1,0:T(2,128)(2,1)}, bf16[2,6,252,2,128]{4,3,2,1,0:T(2,128)(2,1)}, u32[]{:S(2)}, u32[]{:S(2)}) %collective-permute-start.8) | collective-permute-done | bytes 1548320 | tf_op jit(solution)/shard_map/ppermute | solution.py:296
  261.3 7.6 %attend_here.6 = bf16[4,6,32,128]{3,2,1,0:T(8,128)(2,1)} custom-call(s32[1]{0:T(128)} %bitcast.me_ref, s32[32]{0:T(128)} %copy-done.19, bf16[4,32,48,128]{3,2,1,0:T(8,128)(2,1)} %copy-done, bf16[128,512,128]{2,1,0:T(8,128)(2,1)} %bitcast.135, bf16[128,512,128]{2,1,0:T(8,128)(2,1)} %bitcast.140, bf16[2,6,504,128]{3,2,1,0:T(8,128)(2,1)} %bitcast.23.rest_2_, ...), custom_call_target="tpu_custom_call" | custom-call | flops 6000000000 | bytes 6291456 | tf_op jit(solution)/shard_map/attend_here/pallas_call | solution.py:130
  271.1 9.1 %attend_here.5 = bf16[4,8,32,128]{3,2,1,0:T(8,128)(2,1)} custom-call(s32[1]{0:T(128)} %bitcast.me_ref, s32[32]{0:T(128)} %copy-done.19, bf16[4,32,48,128]{3,2,1,0:T(8,128)(2,1)} %copy-done, bf16[128,512,128]{2,1,0:T(8,128)(2,1)} %bitcast.136, bf16[128,512,128]{2,1,0:T(8,128)(2,1)} %bitcast.141, bf16[2,8,504,128]{3,2,1,0:T(8,128)(2,1)} %bitcast.153, ...), custom_call_target="tpu_custom_call" | custom-call | flops 8000000000 | bytes 8388608 | tf_op jit(solution)/shard_map/attend_here/pallas_call | solution.py:130
  288.5 13.3 %multiply_reduce_fusion = (f32[4,32]{1,0:T(4,128)S(1)}, f32[4,32,4096]{2,1,0:T(8,128)S(1)}) fusion(bf16[4,32,4096]{2,1,0:T(8,128)(2,1)} %reshape.186, bf16[4096,4096]{1,0:T(8,128)(2,1)} %param.25, bf16[4,32,4096]{2,1,0:T(8,128)(2,1)S(1)} %copy-done.1), kind=kOutput, calls=%fused_computation.37 | convolution fusion | flops 4298113024 | bytes 37749248 | tf_op jit(solution)/shard_map/sbe,ed->sbd/dot_general | solution.py:50
  301.8 36.5 %fusion.4 = f32[4,32,12288]{2,1,0:T(8,128)} fusion(bf16[4096,12288]{1,0:T(8,128)(2,1)} %param.27, f32[4,32,4096]{2,1,0:T(8,128)S(1)} %get-tuple-element.92, f32[4096]{0:T(1024)S(1)} %convert_element_type.64, f32[4,32]{1,0:T(4,128)S(1)} %add_rsqrt_fusion.2), kind=kOutput, calls=%fused_computation.4 | convolution fusion | flops 12886474752 | bytes 109068800 | tf_op jit(solution)/shard_map/sbd,df->sbf/dot_general | solution.py:53
  338.3 66.6 %fusion.41 = bf16[4,32,4096]{2,1,0:T(8,128)(2,1)} fusion(f32[4,32,4096]{2,1,0:T(8,128)S(1)} %get-tuple-element.92, bf16[12288,4096]{1,0:T(8,128)(2,1)} %param.29, bf16[4096,12288]{1,0:T(8,128)(2,1)} %param.28, f32[4,32,12288]{2,1,0:T(8,128)} %fusion.4, f32[4096]{0:T(1024)S(1)} %convert_element_type.64, f32[4,32]{1,0:T(4,128)S(1)} %add_rsqrt_fusion.2), kind=kOutput, calls=%fused_computation.25 | convolution fusion | flops 25781862400 | bytes 210780672 | tf_op jit(solution)/shard_map/sbf,fd->sbd/dot_general | solution.py:56
  406.1 7.7 %assemble.8 = (bf16[32,256,4,2,128]{4,3,2,1,0:T(2,128)(2,1)}, bf16[32,256,4,2,128]{4,3,2,1,0:T(2,128)(2,1)}) custom-call(s32[1]{0:T(128)} %bitcast.me_ref, s32[32]{0:T(128)} %copy-done.19, bf16[128,256,2,128]{3,2,1,0:T(2,128)(2,1)} %k_ref.27, bf16[128,256,2,128]{3,2,1,0:T(2,128)(2,1)} %v_ref.27, ...), custom_call_target="tpu_custom_call", output_to_operand_aliasing={{0}: (9, {}), {1}: (10, {})} | custom-call | flops 4800000000 | bytes 16777216 | tf_op jit(solution)/shard_map/assemble/pallas_call | solution.py:272
  413.8 6.6 %assemble.9 = (bf16[32,256,4,2,128]{4,3,2,1,0:T(2,128)(2,1)}, bf16[32,256,4,2,128]{4,3,2,1,0:T(2,128)(2,1)}) custom-call(s32[1]{0:T(128)} %bitcast.me_ref, s32[32]{0:T(128)} %copy-done.19, bf16[128,256,2,128]{3,2,1,0:T(2,128)(2,1)} %k_ref.27, bf16[128,256,2,128]{3,2,1,0:T(2,128)(2,1)} %v_ref.27, ...), custom_call_target="tpu_custom_call", output_to_operand_aliasing={{0}: (9, {}), {1}: (10, {})} | custom-call | flops 3600000000 | bytes 12582912 | tf_op jit(solution)/shard_map/assemble/pallas_call | solution.py:272
  420.5 3.4 assemble.10
  424.9 7.9 %assemble.11 = (bf16[32,256,4,2,128]{4,3,2,1,0:T(2,128)(2,1)}, bf16[32,256,4,2,128]{4,3,2,1,0:T(2,128)(2,1)}) custom-call(s32[1]{0:T(128)} %bitcast.me_ref, s32[32]{0:T(128)} %copy-done.19, bf16[128,256,2,128]{3,2,1,0:T(2,128)(2,1)} %k_ref.27, bf16[128,256,2,128]{3,2,1,0:T(2,128)(2,1)} %v_ref.27, ...), custom_call_target="tpu_custom_call", output_to_operand_aliasing={{0}: (9, {}), {1}: (10, {})} | custom-call | flops 4800000000 | bytes 16777216 | tf_op jit(solution)/shard_map/assemble/pallas_call | solution.py:272
  436.3 5.8 %assemble.12 = (bf16[32,256,4,2,128]{4,3,2,1,0:T(2,128)(2,1)}, bf16[32,256,4,2,128]{4,3,2,1,0:T(2,128)(2,1)}) custom-call(s32[1]{0:T(128)} %bitcast.me_ref, s32[32]{0:T(128)} %copy-done.19, bf16[128,256,2,128]{3,2,1,0:T(2,128)(2,1)} %k_ref.27, bf16[128,256,2,128]{3,2,1,0:T(2,128)(2,1)} %v_ref.27, ...), custom_call_target="tpu_custom_call", output_to_operand_aliasing={{0}: (9, {}), {1}: (10, {})} | custom-call | flops 3000000000 | bytes 10485760 | tf_op jit(solution)/shard_map/assemble/pallas_call | solution.py:272
  442.1 4.2 collective-permute-done.20.r3
  (166 shorter events, 72.5 us)
Async XLA Ops:
  3.8 68.3 %collective-permute-start = (bf16[2,2,252,2,128]{4,3,2,1,0:T(2,128)(2,1)}, bf16[2,2,252,2,128]{4,3,2,1,0:T(2,128)(2,1)}, u32[]{:S(2)}, u32[]{:S(2)}) collective-permute-start(bf16[2,2,252,2,128]{4,3,2,1,0:T(2,128)(2,1)} %get-tuple-element.38), channel_id=1, source_target_pairs={{0,1},{1,0},{2,3},{3,2},{4,5},{5,4},{6,7},{7,6},{8,9},{9,8},{10,11... | collective-permute-start | bytes 1548296 | tf_op jit(solution)/shard_map/ppermute | solution.py:296
  4.6 68.7 %collective-permute-start.1 = (bf16[2,2,252,2,128]{4,3,2,1,0:T(2,128)(2,1)}, bf16[2,2,252,2,128]{4,3,2,1,0:T(2,128)(2,1)}, u32[]{:S(2)}, u32[]{:S(2)}) collective-permute-start(bf16[2,2,252,2,128]{4,3,2,1,0:T(2,128)(2,1)} %get-tuple-element.39), channel_id=1, source_target_pairs={{0,2},{1,3},{2,0},{3,1},{4,6},{5,7},{6,4},{7,5},{8,10},{9,11},{10,... | collective-permute-start | bytes 1548296 | tf_op jit(solution)/shard_map/ppermute | solution.py:296
  38.8 7.5 %collective-permute-start.12 = (bf16[14,48,128]{2,1,0:T(8,128)(2,1)}, bf16[14,48,128]{2,1,0:T(8,128)(2,1)S(1)}, u32[]{:S(2)}, u32[]{:S(2)}) collective-permute-start(bf16[14,48,128]{2,1,0:T(8,128)(2,1)} %get-tuple-element.78), channel_id=1, source_target_pairs={{0,1},{1,0},{2,3},{3,2},{4,5},{5,4},{6,7},{7,6},{8,9},{9,8},{10,11... | collective-permute-start | bytes 516104 | tf_op jit(solution)/shard_map/ppermute | solution.py:296
  39.0 7.8 %collective-permute-start.13 = (bf16[14,48,128]{2,1,0:T(8,128)(2,1)}, bf16[14,48,128]{2,1,0:T(8,128)(2,1)S(1)}, u32[]{:S(2)}, u32[]{:S(2)}) collective-permute-start(bf16[14,48,128]{2,1,0:T(8,128)(2,1)} %get-tuple-element.77), channel_id=1, source_target_pairs={{0,2},{1,3},{2,0},{3,1},{4,6},{5,7},{6,4},{7,5},{8,10},{9,11},{10,... | collective-permute-start | bytes 516104 | tf_op jit(solution)/shard_map/ppermute | solution.py:296
  39.3 9.6 %collective-permute-start.14 = (bf16[14,48,128]{2,1,0:T(8,128)(2,1)}, bf16[14,48,128]{2,1,0:T(8,128)(2,1)S(1)}, u32[]{:S(2)}, u32[]{:S(2)}) collective-permute-start(bf16[14,48,128]{2,1,0:T(8,128)(2,1)} %get-tuple-element.76), channel_id=1, source_target_pairs={{0,3},{1,2},{2,1},{3,0},{4,7},{5,6},{6,5},{7,4},{8,11},{9,10},{10,... | collective-permute-start | bytes 516104 | tf_op jit(solution)/shard_map/ppermute | solution.py:296
  46.3 61.2 %collective-permute-start.6 = (bf16[2,6,252,2,128]{4,3,2,1,0:T(2,128)(2,1)}, bf16[2,6,252,2,128]{4,3,2,1,0:T(2,128)(2,1)}, u32[]{:S(2)}, u32[]{:S(2)}) collective-permute-start(bf16[2,6,252,2,128]{4,3,2,1,0:T(2,128)(2,1)} %get-tuple-element.44), channel_id=1, source_target_pairs={{0,1},{1,0},{2,3},{3,2},{4,5},{5,4},{6,7},{7,6},{8,9},{9,8},{10,11... | collective-permute-start | bytes 4644872 | tf_op jit(solution)/shard_map/ppermute | solution.py:296
  70.6 14.3 %collective-permute-start.2 = (bf16[2,2,252,2,128]{4,3,2,1,0:T(2,128)(2,1)S(1)}, bf16[2,2,252,2,128]{4,3,2,1,0:T(2,128)(2,1)S(1)}, u32[]{:S(2)}, u32[]{:S(2)}) collective-permute-start(bf16[2,2,252,2,128]{4,3,2,1,0:T(2,128)(2,1)S(1)} %copy-done.23), channel_id=1, source_target_pairs={{0,3},{1,2},{2,1},{3,0},{4,7},{5,6},{6,5},{7,4},{8,11},{9,10},{10,... | collective-permute-start | bytes 1548296 | tf_op jit(solution)/shard_map/ppermute | solution.py:296
  71.2 23.5 %collective-permute-start.10 = (bf16[2,2,252,2,128]{4,3,2,1,0:T(2,128)(2,1)}, bf16[2,2,252,2,128]{4,3,2,1,0:T(2,128)(2,1)}, u32[]{:S(2)}, u32[]{:S(2)}) collective-permute-start(bf16[2,2,252,2,128]{4,3,2,1,0:T(2,128)(2,1)} %get-tuple-element.48), channel_id=1, source_target_pairs={{0,2},{1,3},{2,0},{3,1},{4,6},{5,7},{6,4},{7,5},{8,10},{9,11},{10,... | collective-permute-start | bytes 1548296 | tf_op jit(solution)/shard_map/ppermute | solution.py:296
  72.1 34.7 %collective-permute-start.11 = (bf16[2,2,252,2,128]{4,3,2,1,0:T(2,128)(2,1)}, bf16[2,2,252,2,128]{4,3,2,1,0:T(2,128)(2,1)}, u32[]{:S(2)}, u32[]{:S(2)}) collective-permute-start(bf16[2,2,252,2,128]{4,3,2,1,0:T(2,128)(2,1)} %get-tuple-element.49), channel_id=1, source_target_pairs={{0,3},{1,2},{2,1},{3,0},{4,7},{5,6},{6,5},{7,4},{8,11},{9,10},{10,... | collective-permute-start | bytes 1548296 | tf_op jit(solution)/shard_map/ppermute | solution.py:296
  73.3 33.6 %collective-permute-start.9 = (bf16[2,2,252,2,128]{4,3,2,1,0:T(2,128)(2,1)}, bf16[2,2,252,2,128]{4,3,2,1,0:T(2,128)(2,1)}, u32[]{:S(2)}, u32[]{:S(2)}) collective-permute-start(bf16[2,2,252,2,128]{4,3,2,1,0:T(2,128)(2,1)} %get-tuple-element.47), channel_id=1, source_target_pairs={{0,1},{1,0},{2,3},{3,2},{4,5},{5,4},{6,7},{7,6},{8,9},{9,8},{10,11... | collective-permute-start | bytes 1548296 | tf_op jit(solution)/shard_map/ppermute | solution.py:296
  85.7 183.3 %collective-permute-start.3 = (bf16[2,8,252,2,128]{4,3,2,1,0:T(2,128)(2,1)}, bf16[2,8,252,2,128]{4,3,2,1,0:T(2,128)(2,1)S(1)}, u32[]{:S(2)}, u32[]{:S(2)}) collective-permute-start(bf16[2,8,252,2,128]{4,3,2,1,0:T(2,128)(2,1)} %get-tuple-element.41), channel_id=1, source_target_pairs={{0,1},{1,0},{2,3},{3,2},{4,5},{5,4},{6,7},{7,6},{8,9},{9,8},{10,11... | collective-permute-start | bytes 6193160 | tf_op jit(solution)/shard_map/ppermute | solution.py:296
  94.7 175.1 %collective-permute-start.4 = (bf16[2,8,252,2,128]{4,3,2,1,0:T(2,128)(2,1)}, bf16[2,8,252,2,128]{4,3,2,1,0:T(2,128)(2,1)}, u32[]{:S(2)}, u32[]{:S(2)}) collective-permute-start(bf16[2,8,252,2,128]{4,3,2,1,0:T(2,128)(2,1)} %get-tuple-element.42), channel_id=1, source_target_pairs={{0,2},{1,3},{2,0},{3,1},{4,6},{5,7},{6,4},{7,5},{8,10},{9,11},{10,... | collective-permute-start | bytes 6193160 | tf_op jit(solution)/shard_map/ppermute | solution.py:296
  106.8 164.2 %collective-permute-start.5 = (bf16[2,8,252,2,128]{4,3,2,1,0:T(2,128)(2,1)}, bf16[2,8,252,2,128]{4,3,2,1,0:T(2,128)(2,1)}, u32[]{:S(2)}, u32[]{:S(2)}) collective-permute-start(bf16[2,8,252,2,128]{4,3,2,1,0:T(2,128)(2,1)} %get-tuple-element.43), channel_id=1, source_target_pairs={{0,3},{1,2},{2,1},{3,0},{4,7},{5,6},{6,5},{7,4},{8,11},{9,10},{10,... | collective-permute-start | bytes 6193160 | tf_op jit(solution)/shard_map/ppermute | solution.py:296
  106.8 120.6 %collective-permute-start.7 = (bf16[2,6,252,2,128]{4,3,2,1,0:T(2,128)(2,1)}, bf16[2,6,252,2,128]{4,3,2,1,0:T(2,128)(2,1)}, u32[]{:S(2)}, u32[]{:S(2)}) collective-permute-start(bf16[2,6,252,2,128]{4,3,2,1,0:T(2,128)(2,1)} %get-tuple-element.45), channel_id=1, source_target_pairs={{0,2},{1,3},{2,0},{3,1},{4,6},{5,7},{6,4},{7,5},{8,10},{9,11},{10,... | collective-permute-start | bytes 4644872 | tf_op jit(solution)/shard_map/ppermute | solution.py:296
  107.5 153.6 %collective-permute-start.8 = (bf16[2,6,252,2,128]{4,3,2,1,0:T(2,128)(2,1)}, bf16[2,6,252,2,128]{4,3,2,1,0:T(2,128)(2,1)}, u32[]{:S(2)}, u32[]{:S(2)}) collective-permute-start(bf16[2,6,252,2,128]{4,3,2,1,0:T(2,128)(2,1)} %get-tuple-element.46), channel_id=1, source_target_pairs={{0,3},{1,2},{2,1},{3,0},{4,7},{5,6},{6,5},{7,4},{8,11},{9,10},{10,... | collective-permute-start | bytes 4644872 | tf_op jit(solution)/shard_map/ppermute | solution.py:296
  227.4 177.4 %collective-permute-start.24 = (bf16[2,8,252,2,128]{4,3,2,1,0:T(2,128)(2,1)}, bf16[2,8,252,2,128]{4,3,2,1,0:T(2,128)(2,1)}, u32[]{:S(2)}, u32[]{:S(2)}) collective-permute-start(bf16[2,8,252,2,128]{4,3,2,1,0:T(2,128)(2,1)} %get-tuple-element.56), channel_id=1, source_target_pairs={{0,1},{1,0},{2,3},{3,2},{4,5},{5,4},{6,7},{7,6},{8,9},{9,8},{10,11... | collective-permute-start | bytes 6193160 | tf_op jit(solution)/shard_map/ppermute | solution.py:296
  261.1 162.8 %collective-permute-start.25 = (bf16[2,8,252,2,128]{4,3,2,1,0:T(2,128)(2,1)}, bf16[2,8,252,2,128]{4,3,2,1,0:T(2,128)(2,1)}, u32[]{:S(2)}, u32[]{:S(2)}) collective-permute-start(bf16[2,8,252,2,128]{4,3,2,1,0:T(2,128)(2,1)} %get-tuple-element.57), channel_id=1, source_target_pairs={{0,2},{1,3},{2,0},{3,1},{4,6},{5,7},{6,4},{7,5},{8,10},{9,11},{10,... | collective-permute-start | bytes 6193160 | tf_op jit(solution)/shard_map/ppermute | solution.py:296
  269.0 155.8 %collective-permute-start.26 = (bf16[2,8,252,2,128]{4,3,2,1,0:T(2,128)(2,1)}, bf16[2,8,252,2,128]{4,3,2,1,0:T(2,128)(2,1)}, u32[]{:S(2)}, u32[]{:S(2)}) collective-permute-start(bf16[2,8,252,2,128]{4,3,2,1,0:T(2,128)(2,1)} %get-tuple-element.58), channel_id=1, source_target_pairs={{0,3},{1,2},{2,1},{3,0},{4,7},{5,6},{6,5},{7,4},{8,11},{9,10},{10,... | collective-permute-start | bytes 6193160 | tf_op jit(solution)/shard_map/ppermute | solution.py:296
  269.8 162.9 %collective-permute-start.21 = (bf16[2,5,252,2,128]{4,3,2,1,0:T(2,128)(2,1)}, bf16[2,5,252,2,128]{4,3,2,1,0:T(2,128)(2,1)}, u32[]{:S(2)}, u32[]{:S(2)}) collective-permute-start(bf16[2,5,252,2,128]{4,3,2,1,0:T(2,128)(2,1)} %get-tuple-element.53), channel_id=1, source_target_pairs={{0,1},{1,0},{2,3},{3,2},{4,5},{5,4},{6,7},{7,6},{8,9},{9,8},{10,11... | collective-permute-start | bytes 3870728 | tf_op jit(solution)/shard_map/ppermute | solution.py:296
  271.0 163.1 %collective-permute-start.22 = (bf16[2,5,252,2,128]{4,3,2,1,0:T(2,128)(2,1)}, bf16[2,5,252,2,128]{4,3,2,1,0:T(2,128)(2,1)}, u32[]{:S(2)}, u32[]{:S(2)}) collective-permute-start(bf16[2,5,252,2,128]{4,3,2,1,0:T(2,128)(2,1)} %get-tuple-element.54), channel_id=1, source_target_pairs={{0,2},{1,3},{2,0},{3,1},{4,6},{5,7},{6,4},{7,5},{8,10},{9,11},{10,... | collective-permute-start | bytes 3870728 | tf_op jit(solution)/shard_map/ppermute | solution.py:296
  404.8 30.4 %collective-permute-start.23 = (bf16[2,5,252,2,128]{4,3,2,1,0:T(2,128)(2,1)}, bf16[2,5,252,2,128]{4,3,2,1,0:T(2,128)(2,1)S(1)}, u32[]{:S(2)}, u32[]{:S(2)}) collective-permute-start(bf16[2,5,252,2,128]{4,3,2,1,0:T(2,128)(2,1)} %get-tuple-element.55), channel_id=1, source_target_pairs={{0,3},{1,2},{2,1},{3,0},{4,7},{5,6},{6,5},{7,4},{8,11},{9,10},{10,... | collective-permute-start | bytes 3870728 | tf_op jit(solution)/shard_map/ppermute | solution.py:296
  423.9 18.1 %collective-permute-start.18 = (bf16[2,1,252,2,128]{4,3,2,1,0:T(2,128)(2,1)S(1)}, bf16[2,1,252,2,128]{4,3,2,1,0:T(2,128)(2,1)S(1)}, u32[]{:S(2)}, u32[]{:S(2)}) collective-permute-start(bf16[2,1,252,2,128]{4,3,2,1,0:T(2,128)(2,1)S(1)} %copy-done.26), channel_id=1, source_target_pairs={{0,1},{1,0},{2,3},{3,2},{4,5},{5,4},{6,7},{7,6},{8,9},{9,8},{10,11... | collective-permute-start | bytes 774152 | tf_op jit(solution)/shard_map/ppermute | solution.py:296
  424.7 17.4 %collective-permute-start.19 = (bf16[2,1,252,2,128]{4,3,2,1,0:T(2,128)(2,1)S(1)}, bf16[2,1,252,2,128]{4,3,2,1,0:T(2,128)(2,1)S(1)}, u32[]{:S(2)}, u32[]{:S(2)}) collective-permute-start(bf16[2,1,252,2,128]{4,3,2,1,0:T(2,128)(2,1)S(1)} %copy-done.25), channel_id=1, source_target_pairs={{0,2},{1,3},{2,0},{3,1},{4,6},{5,7},{6,4},{7,5},{8,10},{9,11},{10,... | collective-permute-start | bytes 774152 | tf_op jit(solution)/shard_map/ppermute | solution.py:296
  432.8 13.5 %collective-permute-start.20 = (bf16[2,1,252,2,128]{4,3,2,1,0:T(2,128)(2,1)S(1)}, bf16[2,1,252,2,128]{4,3,2,1,0:T(2,128)(2,1)S(1)}, u32[]{:S(2)}, u32[]{:S(2)}) collective-permute-start(bf16[2,1,252,2,128]{4,3,2,1,0:T(2,128)(2,1)S(1)} %copy-done.24), channel_id=1, source_target_pairs={{0,3},{1,2},{2,1},{3,0},{4,7},{5,6},{6,5},{7,4},{8,11},{9,10},{10,... | collective-permute-start | bytes 774152 | tf_op jit(solution)/shard_map/ppermute | solution.py:296
  (34 other events, 193.6 us)

commit v3 on v2

--- a/solution.py
+++ b/solution.py
@@ -10,10 +10,11 @@
 THETA = 1000000.0
 GROUP = 4
 STEPS = 4
-GROUPS = ((0, 2), (2, 8), (10, 6), (16, 2))
-EARLY = 18
-LATE = ((18, 8), (26, 5), (31, 1))
+GROUPS = ((0, 2), (2, 4), (6, 4), (10, 6), (16, 3))
+EARLY = 19
+LATE = ((19, 8), (27, 4), (31, 1))
 UNITS = GROUPS + LATE
+ASSEMBLIES = ((0, 1), (2,), (3,), (4, 5), (6,), (7,))
 
 
 def rms_norm(values, gain_vec):
@@ -78,7 +79,7 @@
     seqs = k_rows.shape[0] // GROUP
     rows = k_rows.shape[1]
     here = recvs is not None
-    live = rows - 2 * STEPS
+    live = recvs[0].shape[2] if here else rows - 2 * STEPS
     n_in = 5 if here else 2
 
     def body(me_ref, pos_ref, packed_ref, *rest):
@@ -96,7 +97,8 @@
         @pl.loop(0, count)
         def _(b):
             for off in range(GROUP):
-                v_buf[off, b, live:rows] = jnp.zeros((rows - live, 128), jnp.bfloat16)
+                if live < rows:
+                    v_buf[off, b, live:rows] = jnp.zeros((rows - live, 128), jnp.bfloat16)
                 load(0, off, b).start()
                 load(1, off, b).start()
 
@@ -206,65 +208,81 @@
     return dict(zip(offs, out))
 
 
-def assemble(k_heads, v_heads, recvs, fresh, pos, me, first, count, prev):
+def assemble(k_heads, v_heads, units, fresh, pos, me, prev):
     seqs = k_heads.shape[0] // GROUP
     slots = k_heads.shape[1]
-    live = slots - STEPS
-
-    def body(me_ref, pos_ref, k_ref, v_ref, r1, r2, r3, k_fresh, v_fresh, *rest):
+    total = sum(count for _, count, _ in units)
+    starts = [sum(count for _, count, _ in units[:u]) for u in range(len(units))]
+
+    def body(me_ref, pos_ref, k_ref, v_ref, k_fresh, v_fresh, *rest):
         k_out, v_out, buf, fresh_buf, in_sems, fresh_sems, out_sems = rest[-7:]
         mine = me_ref[0]
 
-        def load(c, b, off):
+        def load(u, c, b, off):
+            at = starts[u] + b
+            live = units[u][2][0].shape[2]
             if off == 0:
-                return pltpu.make_async_copy((k_ref, v_ref)[c].at[mine * seqs + first + b], buf.at[c, b, :, mine], in_sems.at[c, b, 0])
-            return pltpu.make_async_copy((r1, r2, r3)[off - 1].at[c, b], buf.at[c, b, pl.ds(0, live), mine ^ off], in_sems.at[c, b, off])
-
-        def load_fresh(c):
-            return pltpu.make_async_copy((k_fresh, v_fresh)[c].at[pl.ds(first, count)], fresh_buf.at[c], fresh_sems.at[c])
-
-        def store(c, b):
-            return pltpu.make_async_copy(buf.at[c, b], (k_out, v_out)[c].at[first + b], out_sems.at[c, b])
+                src = (k_ref, v_ref)[c].at[mine * seqs + units[u][0] + b]
+                return pltpu.make_async_copy(src, buf.at[c, at, :, mine], in_sems.at[c, at, 0])
+            return pltpu.make_async_copy(rest[3 * u + off - 1].at[c, b], buf.at[c, at, pl.ds(0, live), mine ^ off], in_sems.at[c, at, off])
+
+        def load_fresh(u, c):
+            first, count, _ = units[u]
+            return pltpu.make_async_copy((k_fresh, v_fresh)[c].at[pl.ds(first, count)], fresh_buf.at[c, pl.ds(starts[u], count)], fresh_sems.at[u, c])
+
+        def store(u, c, b):
+            at = starts[u] + b
+            return pltpu.make_async_copy(buf.at[c, at], (k_out, v_out)[c].at[units[u][0] + b], out_sems.at[c, at])
 
         own = lax.broadcasted_iota(jnp.int32, (GROUP, 2, 128), 0) == mine
-        for c in range(2):
-            load_fresh(c).start()
-
-        @pl.loop(0, count)
-        def _(b):
+        for u in range(len(units)):
             for c in range(2):
-                for off in range(GROUP):
-                    load(c, b, off).start()
-
-        for c in range(2):
-            load_fresh(c).wait()
-
-        @pl.loop(0, count)
-        def _(b):
-            where = pos_ref[first + b]
+                load_fresh(u, c).start()
+
+        for u, (_, count, _) in enumerate(units):
+
+            @pl.loop(0, count)
+            def _(b):
+                for c in range(2):
+                    for off in range(GROUP):
+                        load(u, c, b, off).start()
+
+        for u, (first, count, recvs) in enumerate(units):
+            live = recvs[0].shape[2]
             for c in range(2):
-                for off in range(GROUP):
-                    load(c, b, off).wait()
-                for i in range(STEPS):
-                    spare = spare_slot(where, i, live)
-                    moved = jnp.where(own, buf[c, b, spare], buf[c, b, where + i])
-
-                    @pl.when(where + i < live)
-                    def _():
-                        buf[c, b, spare] = moved
-
-                for s in range(STEPS):
-                    buf[c, b, where + s] = fresh_buf[c, b, s]
-                store(c, b).start()
-
-        @pl.loop(0, count)
-        def _(b):
-            for c in range(2):
-                store(c, b).wait()
+                load_fresh(u, c).wait()
+
+            @pl.loop(0, count)
+            def _(b):
+                at = starts[u] + b
+                where = pos_ref[first + b]
+                for c in range(2):
+                    for off in range(GROUP):
+                        load(u, c, b, off).wait()
+                    for i in range(STEPS if live < slots else 0):
+                        spare = spare_slot(where, i, live)
+                        moved = jnp.where(own, buf[c, at, spare], buf[c, at, where + i])
+
+                        @pl.when(where + i < live)
+                        def _():
+                            buf[c, at, spare] = moved
+
+                    for s in range(STEPS):
+                        buf[c, at, where + s] = fresh_buf[c, at, s]
+                    store(u, c, b).start()
+
+        for u, (_, count, _) in enumerate(units):
+
+            @pl.loop(0, count)
+            def _(b):
+                for c in range(2):
+                    store(u, c, b).wait()
 
     any_spec = pl.BlockSpec(memory_space=pl.ANY)
     smem = pl.BlockSpec(memory_space=pltpu.SMEM)
-    args = [me, pos, k_heads, v_heads, *recvs, *fresh]
+    args = [me, pos, k_heads, v_heads, *fresh]
+    for _, _, recvs in units:
+        args += recvs
     aliases = {}
     if prev is not None:
         aliases = {len(args): 0, len(args) + 1: 1}
@@ -275,14 +293,14 @@
         out_specs=[any_spec] * 2,
         out_shape=[jax.ShapeDtypeStruct((seqs, slots, GROUP, 2, 128), jnp.bfloat16)] * 2,
         scratch_shapes=[
-            pltpu.VMEM((2, count, slots, GROUP, 2, 128), jnp.bfloat16),
-            pltpu.VMEM((2, count, STEPS, GROUP, 2, 128), jnp.bfloat16),
-            pltpu.SemaphoreType.DMA((2, count, GROUP)),
-            pltpu.SemaphoreType.DMA((2,)),
-            pltpu.SemaphoreType.DMA((2, count)),
+            pltpu.VMEM((2, total, slots, GROUP, 2, 128), jnp.bfloat16),
+            pltpu.VMEM((2, total, STEPS, GROUP, 2, 128), jnp.bfloat16),
+            pltpu.SemaphoreType.DMA((2, total, GROUP)),
+            pltpu.SemaphoreType.DMA((len(units), 2)),
+            pltpu.SemaphoreType.DMA((2, total)),
         ],
         input_output_aliases=aliases,
-        cost_estimate=pl.CostEstimate(flops=count * 600_000_000, bytes_accessed=2 * count * slots * 8 * 128 * 4, transcendentals=0),
+        cost_estimate=pl.CostEstimate(flops=total * 600_000_000, bytes_accessed=2 * total * slots * 8 * 128 * 4, transcendentals=0),
         name="assemble",
     )(*args)
 
@@ -308,8 +326,17 @@
 
         def send_unit(u):
             first, count = UNITS[u]
-            parts = cut(k_heads, v_heads, start_pos, me_arr, first, count)
-            out = {off: swap(parts[off], off) for off in (2, 3, 1)}
+            if u == 0:
+                out = {}
+                for off in (2, 3, 1):
+                    at = ((me ^ off) * num_rows + first, 0, 0)
+                    both = [swap(lax.dynamic_slice(rows, at, (count,) + rows.shape[1:]), off) for rows in (k_rows, v_rows)]
+                    out[off] = both
+            else:
+                parts = cut(k_heads, v_heads, start_pos, me_arr, first, count)
+                out = {off: swap(parts[off], off) for off in (2, 3, 1)}
+            if u == 0:
+                out = {off: jnp.stack(both).reshape(2, count, slots, 2, head_dim) for off, both in out.items()}
             return [out[off] for off in (1, 2, 3)]
 
         recvs = [send_unit(u) for u in range(len(UNITS))]
@@ -341,8 +368,8 @@
         k_fresh = keys_new.reshape(kv_shape).transpose(1, 0, 2, 3, 4)
         v_fresh = values_new.reshape(kv_shape).transpose(1, 0, 2, 3, 4)
         outs = None
-        for u, (first, count) in enumerate(UNITS):
-            outs = assemble(k_heads, v_heads, recvs[u], (k_fresh, v_fresh), my_pos, me_arr, first, count, outs)
+        for some in ASSEMBLIES:
+            outs = assemble(k_heads, v_heads, [(*UNITS[u], recvs[u]) for u in some], (k_fresh, v_fresh), my_pos, me_arr, outs)
         k_out, v_out = outs
         full = (num_rows, slots, 2 * GROUP, head_dim)
         return out_hidden, k_out.reshape(full), v_out.reshape(full)

time: 451 us -> 447 us (level)
  waiting for transfers between devices: 153 us -> 119 us
  other arithmetic: 11.5 us -> 24 us
  starting transfers between devices: 19.6 us -> 27.7 us
  local copies, waits for them, and re-layouts: 18.9 us -> 25.9 us
    ppermute x27 -> x33, waiting for transfers between devices: 153 us -> 119 us  [swap(): return lax.ppermute(arr, 'x', [(i, i ^ off) for i in range(GROUP)])]
    another operation x2 -> x8, other arithmetic: 1.04 us -> 14 us  [the longest x6 13 us: send_unit(): jnp.stack(both).reshape(2, count, slots, 2, head_dim)]
    ppermute x27 -> x33, starting transfers between devices: 19.6 us -> 27.7 us  [swap(): return lax.ppermute(arr, 'x', [(i, i ^ off) for i in range(GROUP)])]
    unnamed x68 -> x67, local copies, waits for them, and re-layouts: 8.25 us -> 12.7 us
    pallas_call x5 -> x6, Pallas kernels: 39.4 us -> 42.9 us  [attend(): pl.pallas_call(body, in_specs=[smem, smem, vmem] + [any_spec] * n_in, out...]
    pallas_call x7 -> x6, Pallas kernels: 37.6 us -> 35.4 us  [assemble(): pl.pallas_call(body, in_specs=[smem, smem] + [any_spec] * (len(args) - 2)...]
  transfers between devices with their start and end apart: 27 -> 33, of which waited for: 10 -> 8; matrix products, arithmetic and copies ran while one was open for 36% -> 41% of each run, Pallas kernels for 23% -> 24%
where the time goes in v3:
time: 447 us; the launch traced here: 446 us
  matrix products  139 us (31%)
  waiting for transfers between devices  119 us (27%)
  Pallas kernels  109 us (24%)
  starting transfers between devices  27.7 us (6%)
  local copies, waits for them, and re-layouts  25.9 us (6%)
  other arithmetic  24 us (5%)
    ppermute x33, waiting for transfers between devices, swap(): return lax.ppermute(arr, 'x', [(i, i ^ off) for i in range(GROUP)])  119 us
    dot_general x1, matrix products, finish(): jnp.einsum('sbf,fd->sbd', activated, w_down, preferred_element_type=jnp.f...  66.6 us
    pallas_call x6, Pallas kernels, attend(): pl.pallas_call(body, in_specs=[smem, smem, vmem] + [any_spec] * n_in, out...  42.9 us
    dot_general x1, matrix products, finish(): jnp.einsum('sbd,df->sbf', normed, w_gate, preferred_element_type=jnp.floa...  36.5 us
    pallas_call x6, Pallas kernels, assemble(): pl.pallas_call(body, in_specs=[smem, smem] + [any_spec] * (len(args) - 2)...  35.4 us
    pallas_call x7, Pallas kernels, cut(): pl.pallas_call(body, in_specs=[smem, smem, any_spec, any_spec], out_specs...  30.2 us
    ppermute x33, starting transfers between devices, swap(): return lax.ppermute(arr, 'x', [(i, i ^ off) for i in range(GROUP)])  27.7 us
    dot_general x1, matrix products, finish(): jnp.einsum('sbe,ed->sbd', flat_attn, w_o, preferred_element_type=jnp.floa...  13.3 us
  transfers between devices with their start and end apart: 33, of which 8 were waited for; matrix products, arithmetic and copies ran while one was open for 41% of the time, Pallas kernels for 24%

profile of v3, /device:TPU:0, one launch (start us, length us, event | category | flops | bytes accessed | tf_op | source)
XLA Modules:
  0.0 445.6 jit_solution(2595286974410321741)
XLA Ops:
  8.9 4.7 %fusion.52 = bf16[4,32,1024]{2,1,0:T(8,128)(2,1)S(1)} fusion(bf16[4096,1024]{1,0:T(8,128)(2,1)} %param.22, bf16[4,32,4096]{2,1,0:T(8,128)(2,1)S(1)} %copy-done.1, f32[4096]{0:T(1024)S(1)} %convert_element_type.55, f32[4,32]{1,0:T(4,128)S(1)} %add_rsqrt_fusion.3), kind=kOutput, calls=%fused_computation.41 | convolution fusion | flops 1075970048 | bytes 9716224 | tf_op jit(solution)/shard_map/sbd,de->sbe/dot_general | solution.py:44
  14.6 4.7 %fusion.20 = f32[4,32,1024]{2,1,0:T(8,128)S(1)} fusion(bf16[4096,1024]{1,0:T(8,128)(2,1)} %param.21, bf16[4,32,4096]{2,1,0:T(8,128)(2,1)S(1)} %copy-done.1, f32[4096]{0:T(1024)S(1)} %convert_element_type.55, f32[4,32]{1,0:T(4,128)S(1)} %add_rsqrt_fusion.3), kind=kOutput, calls=%fused_computation.14 | convolution fusion | flops 1075838976 | bytes 9978368 | tf_op jit(solution)/shard_map/sbd,de->sbe/dot_general | solution.py:43
  22.2 12.9 %fusion.8 = f32[4,32,4096]{2,1,0:T(8,128)S(1)} fusion(bf16[4096,4096]{1,0:T(8,128)(2,1)} %param.20, bf16[4,32,4096]{2,1,0:T(8,128)(2,1)S(1)} %copy-done.1, f32[4096]{0:T(1024)S(1)} %convert_element_type.55, f32[4,32]{1,0:T(4,128)S(1)} %copy-done.19), kind=kOutput, calls=%fused_computation.8 | convolution fusion | flops 4297064448 | bytes 36717056 | tf_op jit(solution)/shard_map/sbd,de->sbe/dot_general | solution.py:42
  55.8 5.6 %cut.9 = (bf16[2,6,252,2,128]{4,3,2,1,0:T(2,128)(2,1)}, bf16[2,6,252,2,128]{4,3,2,1,0:T(2,128)(2,1)}, bf16[2,6,252,2,128]{4,3,2,1,0:T(2,128)(2,1)}) custom-call(s32[1]{0:T(128)} %bitcast.me_ref, s32[128]{0:T(128)} %pos_ref.15, bf16[128,256,2,128]{3,2,1,0:T(2,128)(2,1)} %k_ref.25, bf16[128,256,2,128]{3,2,1,0:T(2,128)(2,1)} %v_ref.25), custom_call_target="tpu_custom_call" | custom-call | flops 3600000000 | bytes 9437184 | tf_op jit(solution)/shard_map/cut/pallas_call | solution.py:195
  61.5 6.6 %cut.13 = (bf16[2,8,252,2,128]{4,3,2,1,0:T(2,128)(2,1)}, bf16[2,8,252,2,128]{4,3,2,1,0:T(2,128)(2,1)}, bf16[2,8,252,2,128]{4,3,2,1,0:T(2,128)(2,1)}) custom-call(s32[1]{0:T(128)} %bitcast.me_ref, s32[128]{0:T(128)} %pos_ref.15, bf16[128,256,2,128]{3,2,1,0:T(2,128)(2,1)} %k_ref.25, bf16[128,256,2,128]{3,2,1,0:T(2,128)(2,1)} %v_ref.25), custom_call_target="tpu_custom_call" | custom-call | flops 4800000000 | bytes 12582912 | tf_op jit(solution)/shard_map/cut/pallas_call | solution.py:195
  81.3 12.6 %attend_source.1 = bf16[4,13,32,128]{3,2,1,0:T(8,128)(2,1)} custom-call(s32[1]{0:T(128)} %bitcast.me_ref, s32[128]{0:T(128)} %pos_ref.15, bf16[4,13,48,128]{3,2,1,0:T(8,128)(2,1)} %pad_maximum_fusion.1.packed_ref, bf16[128,512,128]{2,1,0:T(8,128)(2,1)} %bitcast.145, bf16[128,512,128]{2,1,0:T(8,128)(2,1)} %bitcast.152), custom_call_target="tpu_custom_call" | custom-call | flops 12999999488 | bytes 13631488 | tf_op jit(solution)/shard_map/attend_source/pallas_call | solution.py:132
  99.0 10.0 %collective-permute-done.23 = bf16[13,32,128]{2,1,0:T(8,128)(2,1)S(1)} collective-permute-done((bf16[13,32,128]{2,1,0:T(8,128)(2,1)S(1)}, bf16[13,32,128]{2,1,0:T(8,128)(2,1)S(1)}, u32[]{:S(2)}, u32[]{:S(2)}) %collective-permute-start.23) | collective-permute-done | bytes 106528 | tf_op jit(solution)/shard_map/ppermute | solution.py:314
  126.4 4.7 %attend_here.5 = bf16[4,2,32,128]{3,2,1,0:T(8,128)(2,1)} custom-call(s32[1]{0:T(128)} %bitcast.me_ref, s32[32]{0:T(128)} %copy-done.22, bf16[4,32,48,128]{3,2,1,0:T(8,128)(2,1)} %copy-done, bf16[128,512,128]{2,1,0:T(8,128)(2,1)} %bitcast.146, bf16[128,512,128]{2,1,0:T(8,128)(2,1)} %bitcast.153, bf16[2,2,512,128]{3,2,1,0:T(8,128)(2,1)} %pad_maximum_fusion.2.rest_2_, ...), custom_call_target="tpu_custom_call" | custom-call | flops 2000000000 | bytes 2097152 | tf_op jit(solution)/shard_map/attend_here/pallas_call | solution.py:132
  136.6 15.4 %collective-permute-done.7.rest_4_ = bf16[2,4,252,2,128]{4,3,2,1,0:T(2,128)(2,1)S(1)} collective-permute-done((bf16[2,4,252,2,128]{4,3,2,1,0:T(2,128)(2,1)}, bf16[2,4,252,2,128]{4,3,2,1,0:T(2,128)(2,1)S(1)}, u32[]{:S(2)}, u32[]{:S(2)}) %collective-permute-start.7) | collective-permute-done | bytes 1032224 | tf_op jit(solution)/shard_map/ppermute | solution.py:314
  154.4 18.7 %collective-permute-done.8.rest_5_ = bf16[2,4,252,2,128]{4,3,2,1,0:T(2,128)(2,1)} collective-permute-done((bf16[2,4,252,2,128]{4,3,2,1,0:T(2,128)(2,1)}, bf16[2,4,252,2,128]{4,3,2,1,0:T(2,128)(2,1)}, u32[]{:S(2)}, u32[]{:S(2)}) %collective-permute-start.8) | collective-permute-done | bytes 1032224 | tf_op jit(solution)/shard_map/ppermute | solution.py:314
  175.1 5.5 %attend_here.9 = bf16[4,3,32,128]{3,2,1,0:T(8,128)(2,1)} custom-call(s32[1]{0:T(128)} %bitcast.me_ref, s32[32]{0:T(128)} %copy-done.22, bf16[4,32,48,128]{3,2,1,0:T(8,128)(2,1)} %copy-done, bf16[128,512,128]{2,1,0:T(8,128)(2,1)} %bitcast.147, bf16[128,512,128]{2,1,0:T(8,128)(2,1)} %bitcast.154, bf16[2,3,504,128]{3,2,1,0:T(8,128)(2,1)} %bitcast.177, ...), custom_call_target="tpu_custom_call" | custom-call | flops 3000000000 | bytes 3145728 | tf_op jit(solution)/shard_map/attend_here/pallas_call | solution.py:132
  180.5 6.2 %attend_here.6 = bf16[4,4,32,128]{3,2,1,0:T(8,128)(2,1)} custom-call(s32[1]{0:T(128)} %bitcast.me_ref, s32[32]{0:T(128)} %copy-done.22, bf16[4,32,48,128]{3,2,1,0:T(8,128)(2,1)} %copy-done, bf16[128,512,128]{2,1,0:T(8,128)(2,1)} %bitcast.148, bf16[128,512,128]{2,1,0:T(8,128)(2,1)} %bitcast.155, bf16[2,4,504,128]{3,2,1,0:T(8,128)(2,1)} %bitcast.175, ...), custom_call_target="tpu_custom_call" | custom-call | flops 4000000000 | bytes 4194304 | tf_op jit(solution)/shard_map/attend_here/pallas_call | solution.py:132
  188.4 8.0 %collective-permute-done.10.rest_1_ = bf16[2,4,252,2,128]{4,3,2,1,0:T(2,128)(2,1)} collective-permute-done((bf16[2,4,252,2,128]{4,3,2,1,0:T(2,128)(2,1)}, bf16[2,4,252,2,128]{4,3,2,1,0:T(2,128)(2,1)}, u32[]{:S(2)}, u32[]{:S(2)}) %collective-permute-start.10) | collective-permute-done | bytes 1032224 | tf_op jit(solution)/shard_map/ppermute | solution.py:314
  196.3 21.1 %collective-permute-done.11.rest_2_ = bf16[2,4,252,2,128]{4,3,2,1,0:T(2,128)(2,1)} collective-permute-done((bf16[2,4,252,2,128]{4,3,2,1,0:T(2,128)(2,1)}, bf16[2,4,252,2,128]{4,3,2,1,0:T(2,128)(2,1)}, u32[]{:S(2)}, u32[]{:S(2)}) %collective-permute-start.11) | collective-permute-done | bytes 1032224 | tf_op jit(solution)/shard_map/ppermute | solution.py:314
  218.0 6.2 %attend_here.7 = bf16[4,4,32,128]{3,2,1,0:T(8,128)(2,1)} custom-call(s32[1]{0:T(128)} %bitcast.me_ref, s32[32]{0:T(128)} %copy-done.22, bf16[4,32,48,128]{3,2,1,0:T(8,128)(2,1)} %copy-done, bf16[128,512,128]{2,1,0:T(8,128)(2,1)} %bitcast.149, bf16[128,512,128]{2,1,0:T(8,128)(2,1)} %bitcast.156, bf16[2,4,504,128]{3,2,1,0:T(8,128)(2,1)} %bitcast.26.rest_2_, ...), custom_call_target="tpu_custom_call" | custom-call | flops 4000000000 | bytes 4194304 | tf_op jit(solution)/shard_map/attend_here/pallas_call | solution.py:132
  225.8 6.6 %assemble.6 = (bf16[32,256,4,2,128]{4,3,2,1,0:T(2,128)(2,1)}, bf16[32,256,4,2,128]{4,3,2,1,0:T(2,128)(2,1)}) custom-call(s32[1]{0:T(128)} %bitcast.me_ref, s32[32]{0:T(128)} %copy-done.22, bf16[128,256,2,128]{3,2,1,0:T(2,128)(2,1)} %k_ref.25, bf16[128,256,2,128]{3,2,1,0:T(2,128)(2,1)} %v_ref.25, bf16[32,4,4,2,128]{4,3,2,1,0:T(2,128)(2,1)} %fusion.69.k_fresh, ...), custom_call_target="tpu_custom_call" | custom-call | flops 3600000000 | bytes 12582912 | tf_op jit(solution)/shard_map/assemble/pallas_call | solution.py:290
  238.7 12.8 %collective-permute-done.13.rest_1_ = bf16[2,6,252,2,128]{4,3,2,1,0:T(2,128)(2,1)S(1)} collective-permute-done((bf16[2,6,252,2,128]{4,3,2,1,0:T(2,128)(2,1)}, bf16[2,6,252,2,128]{4,3,2,1,0:T(2,128)(2,1)S(1)}, u32[]{:S(2)}, u32[]{:S(2)}) %collective-permute-start.13) | collective-permute-done | bytes 1548320 | tf_op jit(solution)/shard_map/ppermute | solution.py:314
  251.5 32.2 %collective-permute-done.14.rest_2_ = bf16[2,6,252,2,128]{4,3,2,1,0:T(2,128)(2,1)} collective-permute-done((bf16[2,6,252,2,128]{4,3,2,1,0:T(2,128)(2,1)}, bf16[2,6,252,2,128]{4,3,2,1,0:T(2,128)(2,1)}, u32[]{:S(2)}, u32[]{:S(2)}) %collective-permute-start.14) | collective-permute-done | bytes 1548320 | tf_op jit(solution)/shard_map/ppermute | solution.py:314
  284.4 7.7 %attend_here.8 = bf16[4,6,32,128]{3,2,1,0:T(8,128)(2,1)} custom-call(s32[1]{0:T(128)} %bitcast.me_ref, s32[32]{0:T(128)} %copy-done.22, bf16[4,32,48,128]{3,2,1,0:T(8,128)(2,1)} %copy-done, bf16[128,512,128]{2,1,0:T(8,128)(2,1)} %bitcast.150, bf16[128,512,128]{2,1,0:T(8,128)(2,1)} %bitcast.157, bf16[2,6,504,128]{3,2,1,0:T(8,128)(2,1)} %bitcast.168, ...), custom_call_target="tpu_custom_call" | custom-call | flops 6000000000 | bytes 6291456 | tf_op jit(solution)/shard_map/attend_here/pallas_call | solution.py:132
  300.3 13.3 %multiply_reduce_fusion = (f32[4,32]{1,0:T(4,128)S(1)}, f32[4,32,4096]{2,1,0:T(8,128)S(1)}) fusion(bf16[4,32,4096]{2,1,0:T(8,128)(2,1)} %reshape.201, bf16[4096,4096]{1,0:T(8,128)(2,1)} %param.25, bf16[4,32,4096]{2,1,0:T(8,128)(2,1)S(1)} %copy-done.2), kind=kOutput, calls=%fused_computation.37 | convolution fusion | flops 4298113024 | bytes 37749248 | tf_op jit(solution)/shard_map/sbe,ed->sbd/dot_general | solution.py:51
  313.6 36.5 %fusion.4 = f32[4,32,12288]{2,1,0:T(8,128)} fusion(bf16[4096,12288]{1,0:T(8,128)(2,1)} %param.27, f32[4,32,4096]{2,1,0:T(8,128)S(1)} %get-tuple-element.94, f32[4096]{0:T(1024)S(1)} %convert_element_type.64, f32[4,32]{1,0:T(4,128)S(1)} %add_rsqrt_fusion.2), kind=kOutput, calls=%fused_computation.4 | convolution fusion | flops 12886474752 | bytes 109068800 | tf_op jit(solution)/shard_map/sbd,df->sbf/dot_general | solution.py:54
  351.7 66.6 %fusion.41 = bf16[4,32,4096]{2,1,0:T(8,128)(2,1)} fusion(f32[4,32,4096]{2,1,0:T(8,128)S(1)} %get-tuple-element.94, bf16[12288,4096]{1,0:T(8,128)(2,1)} %param.29, bf16[4096,12288]{1,0:T(8,128)(2,1)} %param.28, f32[4,32,12288]{2,1,0:T(8,128)} %fusion.4, f32[4096]{0:T(1024)S(1)} %convert_element_type.64, f32[4,32]{1,0:T(4,128)S(1)} %add_rsqrt_fusion.2), kind=kOutput, calls=%fused_computation.25 | convolution fusion | flops 25781862400 | bytes 210780672 | tf_op jit(solution)/shard_map/sbf,fd->sbd/dot_general | solution.py:57
  418.3 6.7 %assemble.8 = (bf16[32,256,4,2,128]{4,3,2,1,0:T(2,128)(2,1)}, bf16[32,256,4,2,128]{4,3,2,1,0:T(2,128)(2,1)}) custom-call(s32[1]{0:T(128)} %bitcast.me_ref, s32[32]{0:T(128)} %copy-done.22, bf16[128,256,2,128]{3,2,1,0:T(2,128)(2,1)} %k_ref.25, bf16[128,256,2,128]{3,2,1,0:T(2,128)(2,1)} %v_ref.25, ...), custom_call_target="tpu_custom_call", output_to_operand_aliasing={{0}: (9, {}), {1}: (10, {})} | custom-call | flops 3600000000 | bytes 12582912 | tf_op jit(solution)/shard_map/assemble/pallas_call | solution.py:290
  427.0 10.0 %assemble.9 = (bf16[32,256,4,2,128]{4,3,2,1,0:T(2,128)(2,1)}, bf16[32,256,4,2,128]{4,3,2,1,0:T(2,128)(2,1)}) custom-call(s32[1]{0:T(128)} %bitcast.me_ref, s32[32]{0:T(128)} %copy-done.22, bf16[128,256,2,128]{3,2,1,0:T(2,128)(2,1)} %k_ref.25, bf16[128,256,2,128]{3,2,1,0:T(2,128)(2,1)} %v_ref.25, ...), custom_call_target="tpu_custom_call", output_to_operand_aliasing={{0}: (12, {}), {1}: (13, {})} | custom-call | flops 6600000000 | bytes 23068672 | tf_op jit(solution)/shard_map/assemble/pallas_call | solution.py:290
  (184 shorter events, 108.6 us)
Async XLA Ops:
  2.8 76.6 %collective-permute-start.5 = (bf16[2,512,128]{2,1,0:T(8,128)(2,1)}, bf16[2,512,128]{2,1,0:T(8,128)(2,1)}, u32[]{:S(2)}, u32[]{:S(2)}) collective-permute-start(bf16[2,512,128]{2,1,0:T(8,128)(2,1)} %get-tuple-element.72), channel_id=1, source_target_pairs={{0,3},{1,2},{2,1},{3,0},{4,7},{5,6},{6,5},{7,4},{8,11},{9,10},{10,... | collective-permute-start | bytes 786440 | tf_op jit(solution)/shard_map/ppermute | solution.py:314
  5.4 73.9 %collective-permute-start.3 = (bf16[2,512,128]{2,1,0:T(8,128)(2,1)}, bf16[2,512,128]{2,1,0:T(8,128)(2,1)}, u32[]{:S(2)}, u32[]{:S(2)}) collective-permute-start(bf16[2,512,128]{2,1,0:T(8,128)(2,1)} %get-tuple-element.73), channel_id=1, source_target_pairs={{0,2},{1,3},{2,0},{3,1},{4,6},{5,7},{6,4},{7,5},{8,10},{9,11},{10,... | collective-permute-start | bytes 786440 | tf_op jit(solution)/shard_map/ppermute | solution.py:314
  6.0 73.9 %collective-permute-start.1 = (bf16[2,512,128]{2,1,0:T(8,128)(2,1)}, bf16[2,512,128]{2,1,0:T(8,128)(2,1)}, u32[]{:S(2)}, u32[]{:S(2)}) collective-permute-start(bf16[2,512,128]{2,1,0:T(8,128)(2,1)} %get-tuple-element.74), channel_id=1, source_target_pairs={{0,1},{1,0},{2,3},{3,2},{4,5},{5,4},{6,7},{7,6},{8,9},{9,8},{10,11... | collective-permute-start | bytes 786440 | tf_op jit(solution)/shard_map/ppermute | solution.py:314
  40.5 31.0 %collective-permute-start.20 = (bf16[13,48,128]{2,1,0:T(8,128)(2,1)S(1)}, bf16[13,48,128]{2,1,0:T(8,128)(2,1)S(1)}, u32[]{:S(2)}, u32[]{:S(2)}) collective-permute-start(bf16[13,48,128]{2,1,0:T(8,128)(2,1)S(1)} %get-tuple-element.80), channel_id=1, source_target_pairs={{0,3},{1,2},{2,1},{3,0},{4,7},{5,6},{6,5},{7,4},{8,11},{9,10},{10,... | collective-permute-start | bytes 479240 | tf_op jit(solution)/shard_map/ppermute | solution.py:314
  42.0 34.4 %collective-permute-start.19 = (bf16[13,48,128]{2,1,0:T(8,128)(2,1)S(1)}, bf16[13,48,128]{2,1,0:T(8,128)(2,1)S(1)}, u32[]{:S(2)}, u32[]{:S(2)}) collective-permute-start(bf16[13,48,128]{2,1,0:T(8,128)(2,1)S(1)} %get-tuple-element.81), channel_id=1, source_target_pairs={{0,2},{1,3},{2,0},{3,1},{4,6},{5,7},{6,4},{7,5},{8,10},{9,11},{10,... | collective-permute-start | bytes 479240 | tf_op jit(solution)/shard_map/ppermute | solution.py:314
  76.4 17.6 %collective-permute-start.4 = (bf16[2,512,128]{2,1,0:T(8,128)(2,1)S(1)}, bf16[2,512,128]{2,1,0:T(8,128)(2,1)S(1)}, u32[]{:S(2)}, u32[]{:S(2)}) collective-permute-start(bf16[2,512,128]{2,1,0:T(8,128)(2,1)S(1)} %get-tuple-element.69), channel_id=1, source_target_pairs={{0,3},{1,2},{2,1},{3,0},{4,7},{5,6},{6,5},{7,4},{8,11},{9,10},{10,... | collective-permute-start | bytes 786440 | tf_op jit(solution)/shard_map/ppermute | solution.py:314
  79.4 35.5 %collective-permute-start.15 = (bf16[2,3,252,2,128]{4,3,2,1,0:T(2,128)(2,1)}, bf16[2,3,252,2,128]{4,3,2,1,0:T(2,128)(2,1)S(1)}, u32[]{:S(2)}, u32[]{:S(2)}) collective-permute-start(bf16[2,3,252,2,128]{4,3,2,1,0:T(2,128)(2,1)} %get-tuple-element.45), channel_id=1, source_target_pairs={{0,1},{1,0},{2,3},{3,2},{4,5},{5,4},{6,7},{7,6},{8,9},{9,8},{10,11... | collective-permute-start | bytes 2322440 | tf_op jit(solution)/shard_map/ppermute | solution.py:314
  79.9 37.4 %collective-permute-start.16 = (bf16[2,3,252,2,128]{4,3,2,1,0:T(2,128)(2,1)}, bf16[2,3,252,2,128]{4,3,2,1,0:T(2,128)(2,1)}, u32[]{:S(2)}, u32[]{:S(2)}) collective-permute-start(bf16[2,3,252,2,128]{4,3,2,1,0:T(2,128)(2,1)} %get-tuple-element.46), channel_id=1, source_target_pairs={{0,2},{1,3},{2,0},{3,1},{4,6},{5,7},{6,4},{7,5},{8,10},{9,11},{10,... | collective-permute-start | bytes 2322440 | tf_op jit(solution)/shard_map/ppermute | solution.py:314
  94.0 38.7 %collective-permute-start.9 = (bf16[2,4,252,2,128]{4,3,2,1,0:T(2,128)(2,1)}, bf16[2,4,252,2,128]{4,3,2,1,0:T(2,128)(2,1)}, u32[]{:S(2)}, u32[]{:S(2)}) collective-permute-start(bf16[2,4,252,2,128]{4,3,2,1,0:T(2,128)(2,1)} %get-tuple-element.39), channel_id=1, source_target_pairs={{0,1},{1,0},{2,3},{3,2},{4,5},{5,4},{6,7},{7,6},{8,9},{9,8},{10,11... | collective-permute-start | bytes 3096584 | tf_op jit(solution)/shard_map/ppermute | solution.py:314
  109.0 22.1 %collective-permute-start.17 = (bf16[2,3,252,2,128]{4,3,2,1,0:T(2,128)(2,1)}, bf16[2,3,252,2,128]{4,3,2,1,0:T(2,128)(2,1)}, u32[]{:S(2)}, u32[]{:S(2)}) collective-permute-start(bf16[2,3,252,2,128]{4,3,2,1,0:T(2,128)(2,1)} %get-tuple-element.47), channel_id=1, source_target_pairs={{0,3},{1,2},{2,1},{3,0},{4,7},{5,6},{6,5},{7,4},{8,11},{9,10},{10,... | collective-permute-start | bytes 2322440 | tf_op jit(solution)/shard_map/ppermute | solution.py:314
  114.3 20.8 %collective-permute-start.6 = (bf16[2,4,252,2,128]{4,3,2,1,0:T(2,128)(2,1)}, bf16[2,4,252,2,128]{4,3,2,1,0:T(2,128)(2,1)S(1)}, u32[]{:S(2)}, u32[]{:S(2)}) collective-permute-start(bf16[2,4,252,2,128]{4,3,2,1,0:T(2,128)(2,1)} %get-tuple-element.36), channel_id=1, source_target_pairs={{0,1},{1,0},{2,3},{3,2},{4,5},{5,4},{6,7},{7,6},{8,9},{9,8},{10,11... | collective-permute-start | bytes 3096584 | tf_op jit(solution)/shard_map/ppermute | solution.py:314
  115.9 36.1 %collective-permute-start.7 = (bf16[2,4,252,2,128]{4,3,2,1,0:T(2,128)(2,1)}, bf16[2,4,252,2,128]{4,3,2,1,0:T(2,128)(2,1)S(1)}, u32[]{:S(2)}, u32[]{:S(2)}) collective-permute-start(bf16[2,4,252,2,128]{4,3,2,1,0:T(2,128)(2,1)} %get-tuple-element.37), channel_id=1, source_target_pairs={{0,2},{1,3},{2,0},{3,1},{4,6},{5,7},{6,4},{7,5},{8,10},{9,11},{10,... | collective-permute-start | bytes 3096584 | tf_op jit(solution)/shard_map/ppermute | solution.py:314
  117.3 55.9 %collective-permute-start.8 = (bf16[2,4,252,2,128]{4,3,2,1,0:T(2,128)(2,1)}, bf16[2,4,252,2,128]{4,3,2,1,0:T(2,128)(2,1)}, u32[]{:S(2)}, u32[]{:S(2)}) collective-permute-start(bf16[2,4,252,2,128]{4,3,2,1,0:T(2,128)(2,1)} %get-tuple-element.38), channel_id=1, source_target_pairs={{0,3},{1,2},{2,1},{3,0},{4,7},{5,6},{6,5},{7,4},{8,11},{9,10},{10,... | collective-permute-start | bytes 3096584 | tf_op jit(solution)/shard_map/ppermute | solution.py:314
  131.2 65.1 %collective-permute-start.10 = (bf16[2,4,252,2,128]{4,3,2,1,0:T(2,128)(2,1)}, bf16[2,4,252,2,128]{4,3,2,1,0:T(2,128)(2,1)}, u32[]{:S(2)}, u32[]{:S(2)}) collective-permute-start(bf16[2,4,252,2,128]{4,3,2,1,0:T(2,128)(2,1)} %get-tuple-element.40), channel_id=1, source_target_pairs={{0,2},{1,3},{2,0},{3,1},{4,6},{5,7},{6,4},{7,5},{8,10},{9,11},{10,... | collective-permute-start | bytes 3096584 | tf_op jit(solution)/shard_map/ppermute | solution.py:314
  132.6 84.8 %collective-permute-start.11 = (bf16[2,4,252,2,128]{4,3,2,1,0:T(2,128)(2,1)}, bf16[2,4,252,2,128]{4,3,2,1,0:T(2,128)(2,1)}, u32[]{:S(2)}, u32[]{:S(2)}) collective-permute-start(bf16[2,4,252,2,128]{4,3,2,1,0:T(2,128)(2,1)} %get-tuple-element.41), channel_id=1, source_target_pairs={{0,3},{1,2},{2,1},{3,0},{4,7},{5,6},{6,5},{7,4},{8,11},{9,10},{10,... | collective-permute-start | bytes 3096584 | tf_op jit(solution)/shard_map/ppermute | solution.py:314
  136.1 100.9 %collective-permute-start.12 = (bf16[2,6,252,2,128]{4,3,2,1,0:T(2,128)(2,1)}, bf16[2,6,252,2,128]{4,3,2,1,0:T(2,128)(2,1)S(1)}, u32[]{:S(2)}, u32[]{:S(2)}) collective-permute-start(bf16[2,6,252,2,128]{4,3,2,1,0:T(2,128)(2,1)} %get-tuple-element.42), channel_id=1, source_target_pairs={{0,1},{1,0},{2,3},{3,2},{4,5},{5,4},{6,7},{7,6},{8,9},{9,8},{10,11... | collective-permute-start | bytes 4644872 | tf_op jit(solution)/shard_map/ppermute | solution.py:314
  153.0 98.5 %collective-permute-start.13 = (bf16[2,6,252,2,128]{4,3,2,1,0:T(2,128)(2,1)}, bf16[2,6,252,2,128]{4,3,2,1,0:T(2,128)(2,1)S(1)}, u32[]{:S(2)}, u32[]{:S(2)}) collective-permute-start(bf16[2,6,252,2,128]{4,3,2,1,0:T(2,128)(2,1)} %get-tuple-element.43), channel_id=1, source_target_pairs={{0,2},{1,3},{2,0},{3,1},{4,6},{5,7},{6,4},{7,5},{8,10},{9,11},{10,... | collective-permute-start | bytes 4644872 | tf_op jit(solution)/shard_map/ppermute | solution.py:314
  173.2 110.6 %collective-permute-start.14 = (bf16[2,6,252,2,128]{4,3,2,1,0:T(2,128)(2,1)}, bf16[2,6,252,2,128]{4,3,2,1,0:T(2,128)(2,1)}, u32[]{:S(2)}, u32[]{:S(2)}) collective-permute-start(bf16[2,6,252,2,128]{4,3,2,1,0:T(2,128)(2,1)} %get-tuple-element.44), channel_id=1, source_target_pairs={{0,3},{1,2},{2,1},{3,0},{4,7},{5,6},{6,5},{7,4},{8,11},{9,10},{10,... | collective-permute-start | bytes 4644872 | tf_op jit(solution)/shard_map/ppermute | solution.py:314
  196.3 153.8 %collective-permute-start.27 = (bf16[2,4,252,2,128]{4,3,2,1,0:T(2,128)(2,1)}, bf16[2,4,252,2,128]{4,3,2,1,0:T(2,128)(2,1)}, u32[]{:S(2)}, u32[]{:S(2)}) collective-permute-start(bf16[2,4,252,2,128]{4,3,2,1,0:T(2,128)(2,1)} %get-tuple-element.51), channel_id=1, source_target_pairs={{0,1},{1,0},{2,3},{3,2},{4,5},{5,4},{6,7},{7,6},{8,9},{9,8},{10,11... | collective-permute-start | bytes 3096584 | tf_op jit(solution)/shard_map/ppermute | solution.py:314
  217.4 219.5 %collective-permute-start.28 = (bf16[2,4,252,2,128]{4,3,2,1,0:T(2,128)(2,1)}, bf16[2,4,252,2,128]{4,3,2,1,0:T(2,128)(2,1)}, u32[]{:S(2)}, u32[]{:S(2)}) collective-permute-start(bf16[2,4,252,2,128]{4,3,2,1,0:T(2,128)(2,1)} %get-tuple-element.52), channel_id=1, source_target_pairs={{0,2},{1,3},{2,0},{3,1},{4,6},{5,7},{6,4},{7,5},{8,10},{9,11},{10,... | collective-permute-start | bytes 3096584 | tf_op jit(solution)/shard_map/ppermute | solution.py:314
  237.0 199.9 %collective-permute-start.29 = (bf16[2,4,252,2,128]{4,3,2,1,0:T(2,128)(2,1)}, bf16[2,4,252,2,128]{4,3,2,1,0:T(2,128)(2,1)}, u32[]{:S(2)}, u32[]{:S(2)}) collective-permute-start(bf16[2,4,252,2,128]{4,3,2,1,0:T(2,128)(2,1)} %get-tuple-element.53), channel_id=1, source_target_pairs={{0,3},{1,2},{2,1},{3,0},{4,7},{5,6},{6,5},{7,4},{8,11},{9,10},{10,... | collective-permute-start | bytes 3096584 | tf_op jit(solution)/shard_map/ppermute | solution.py:314
  251.5 173.5 %collective-permute-start.30 = (bf16[2,8,252,2,128]{4,3,2,1,0:T(2,128)(2,1)}, bf16[2,8,252,2,128]{4,3,2,1,0:T(2,128)(2,1)}, u32[]{:S(2)}, u32[]{:S(2)}) collective-permute-start(bf16[2,8,252,2,128]{4,3,2,1,0:T(2,128)(2,1)} %get-tuple-element.54), channel_id=1, source_target_pairs={{0,1},{1,0},{2,3},{3,2},{4,5},{5,4},{6,7},{7,6},{8,9},{9,8},{10,11... | collective-permute-start | bytes 6193160 | tf_op jit(solution)/shard_map/ppermute | solution.py:314
  283.8 141.3 %collective-permute-start.31 = (bf16[2,8,252,2,128]{4,3,2,1,0:T(2,128)(2,1)}, bf16[2,8,252,2,128]{4,3,2,1,0:T(2,128)(2,1)}, u32[]{:S(2)}, u32[]{:S(2)}) collective-permute-start(bf16[2,8,252,2,128]{4,3,2,1,0:T(2,128)(2,1)} %get-tuple-element.55), channel_id=1, source_target_pairs={{0,2},{1,3},{2,0},{3,1},{4,6},{5,7},{6,4},{7,5},{8,10},{9,11},{10,... | collective-permute-start | bytes 6193160 | tf_op jit(solution)/shard_map/ppermute | solution.py:314
  350.1 76.5 %collective-permute-start.32 = (bf16[2,8,252,2,128]{4,3,2,1,0:T(2,128)(2,1)}, bf16[2,8,252,2,128]{4,3,2,1,0:T(2,128)(2,1)}, u32[]{:S(2)}, u32[]{:S(2)}) collective-permute-start(bf16[2,8,252,2,128]{4,3,2,1,0:T(2,128)(2,1)} %get-tuple-element.56), channel_id=1, source_target_pairs={{0,3},{1,2},{2,1},{3,0},{4,7},{5,6},{6,5},{7,4},{8,11},{9,10},{10,... | collective-permute-start | bytes 6193160 | tf_op jit(solution)/shard_map/ppermute | solution.py:314
  (39 other events, 303.7 us)

commit v4 on v3

--- a/solution.py
+++ b/solution.py
@@ -10,11 +10,11 @@
 THETA = 1000000.0
 GROUP = 4
 STEPS = 4
-GROUPS = ((0, 2), (2, 4), (6, 4), (10, 6), (16, 3))
-EARLY = 19
-LATE = ((19, 8), (27, 4), (31, 1))
+GROUPS = ((0, 2), (2, 8), (10, 9), (19, 3))
+EARLY = 22
+LATE = ((22, 6), (28, 3), (31, 1))
 UNITS = GROUPS + LATE
-ASSEMBLIES = ((0, 1), (2,), (3,), (4, 5), (6,), (7,))
+ASSEMBLIES = ((0, 1), (2,), (3, 4), (5,), (6,))
 
 
 def rms_norm(values, gain_vec):
@@ -47,15 +47,63 @@
     return queries, keys_new, values_new.astype(jnp.bfloat16)
 
 
-def finish(hidden, flat_attn, w_o, mlp_norm, w_gate, w_up, w_down):
+def gated_mlp(rows, w_gate, w_up, w_down, core):
+    n, d = rows.shape[1:]
+    ff = w_gate.shape[1]
+    blk = 512
+    steps = ff // 2 // blk
+
+    def body(core_ref, rows_ref, gate_ref, up_ref, down_ref, mine_ref, other_ref, acc_ref):
+        x = rows_ref[...].reshape(2 * n, d)
+        gate_val = jnp.dot(x, gate_ref[...], preferred_element_type=jnp.float32)
+        up_val = jnp.dot(x, up_ref[...], preferred_element_type=jnp.float32)
+        activated = (gate_val * jax.nn.sigmoid(gate_val) * up_val).astype(jnp.bfloat16)
+        part = jnp.dot(activated, down_ref[...], preferred_element_type=jnp.float32)
+
+        @pl.when(pl.program_id(0) == 0)
+        def _():
+            acc_ref[...] = part
+
+        @pl.when(pl.program_id(0) > 0)
+        def _():
+            acc_ref[...] += part
+
+        @pl.when(pl.program_id(0) == steps - 1)
+        def _():
+            mine_ref[...] = acc_ref[0:n]
+            other_ref[...] = acc_ref[n:2 * n]
+
+    column = pl.BlockSpec((d, blk), lambda j, core_ref: (0, core_ref[0] * steps + j))
+    whole = pl.BlockSpec((n, d), lambda j, core_ref: (0, 0))
+    return pl.pallas_call(
+        body,
+        grid_spec=pltpu.PrefetchScalarGridSpec(
+            num_scalar_prefetch=1,
+            grid=(steps,),
+            in_specs=[
+                pl.BlockSpec((2, n, d), lambda j, core_ref: (0, 0, 0)),
+                column,
+                column,
+                pl.BlockSpec((blk, d), lambda j, core_ref: (core_ref[0] * steps + j, 0)),
+            ],
+            out_specs=[whole, whole],
+            scratch_shapes=[pltpu.VMEM((2 * n, d), jnp.float32)],
+        ),
+        out_shape=[jax.ShapeDtypeStruct((n, d), jnp.float32)] * 2,
+        compiler_params=pltpu.CompilerParams(vmem_limit_bytes=62 * 1024 * 1024),
+        cost_estimate=pl.CostEstimate(flops=6 * n * d * ff, bytes_accessed=3 * d * ff, transcendentals=n * ff),
+        name="gated_mlp",
+    )(core, rows, w_gate, w_up, w_down)
+
+
+def finish(hidden, flat_attn, w_o, mlp_norm, w_gate, w_up, w_down, core, swap_core):
     attn_out = jnp.einsum('sbe,ed->sbd', flat_attn, w_o, preferred_element_type=jnp.float32)
     residual = (hidden.astype(jnp.float32) + attn_out).astype(jnp.bfloat16)
     normed = rms_norm(residual, mlp_norm).astype(jnp.bfloat16)
-    gate_val = jnp.einsum('sbd,df->sbf', normed, w_gate, preferred_element_type=jnp.float32)
-    up_val = jnp.einsum('sbd,df->sbf', normed, w_up, preferred_element_type=jnp.float32)
-    activated = (jax.nn.silu(gate_val) * up_val).astype(jnp.bfloat16)
-    down_val = jnp.einsum('sbf,fd->sbd', activated, w_down, preferred_element_type=jnp.float32)
-    return (residual.astype(jnp.float32) + down_val).astype(jnp.bfloat16)
+    flat = normed.reshape(-1, normed.shape[-1])
+    mine, other = gated_mlp(jnp.stack([flat, swap_core(flat)]), w_gate, w_up, w_down, core)
+    down_val = mine + swap_core(other)
+    return (residual.astype(jnp.float32) + down_val.reshape(residual.shape)).astype(jnp.bfloat16)
 
 
 def attend_four(packed, keys, values, bounds, own_cols, new_ok):
@@ -334,9 +382,11 @@
                     out[off] = both
             else:
                 parts = cut(k_heads, v_heads, start_pos, me_arr, first, count)
-                out = {off: swap(parts[off], off) for off in (2, 3, 1)}
+                out = {}
+                for off in (3, 2, 1):
+                    out[off] = swap(parts[off], off)
             if u == 0:
-                out = {off: jnp.stack(both).reshape(2, count, slots, 2, head_dim) for off, both in out.items()}
+                out = {off: lax.optimization_barrier(jnp.stack(both)).reshape(2, count, slots, 2, head_dim) for off, both in out.items()}
             return [out[off] for off in (1, 2, 3)]
 
         recvs = [send_unit(u) for u in range(len(UNITS))]
@@ -363,7 +413,7 @@
         there = jnp.stack([owner_part(back, j) for j in range(GROUP)])
         owners = jnp.concatenate(here + [there], axis=1)
         attended = owners.reshape(GROUP, num_rows, 2, 4, n_steps, head_dim).transpose(4, 1, 0, 2, 3, 5).reshape(n_steps, num_rows, -1)
-        out_hidden = finish(hidden_in, attended, w_o, mlp_norm, w_gate, w_up, w_down)
+        out_hidden = finish(hidden_in, attended, w_o, mlp_norm, w_gate, w_up, w_down, me_arr & 1, lambda arr: swap(arr, 1))
 
         k_fresh = keys_new.reshape(kv_shape).transpose(1, 0, 2, 3, 4)
         v_fresh = values_new.reshape(kv_shape).transpose(1, 0, 2, 3, 4)

time: 447 us -> 478 us (1.069)
  matrix products: 139 us -> 35.9 us
  waiting for transfers between devices: 119 us -> 207 us
  Pallas kernels: 109 us -> 163 us
  local copies, waits for them, and re-layouts: 25.9 us -> 19.4 us
    dot_general x2 -> x0, matrix products: 103 us -> none  [the longest x1 66.6 us: finish(): jnp.einsum('sbf,fd->sbd', activated, w_down, preferred_element_type=jnp.f...]
    ppermute x33 -> x32, waiting for transfers between devices: 119 us -> 207 us  [swap(): return lax.ppermute(arr, 'x', [(i, i ^ off) for i in range(GROUP)])]
    pallas_call x0 -> x1, Pallas kernels: none -> 60 us  [gated_mlp(): pl.pallas_call(body, grid_spec=pltpu.PrefetchScalarGridSpec(num_scalar_pr...]
    another operation x8 -> x6, other arithmetic: 14 us -> 7.38 us  [the longest x3 3.6 us: send_unit(): jnp.stack(both)]
    unnamed x67 -> x86, local copies, waits for them, and re-layouts: 12.7 us -> 8.11 us
    pallas_call x6 -> x5, Pallas kernels: 42.9 us -> 39.6 us  [attend(): pl.pallas_call(body, in_specs=[smem, smem, vmem] + [any_spec] * n_in, out...]
    pallas_call x6 -> x5, Pallas kernels: 35.4 us -> 34.1 us  [assemble(): pl.pallas_call(body, in_specs=[smem, smem] + [any_spec] * (len(args) - 2)...]
    pallas_call x7 -> x6, Pallas kernels: 30.2 us -> 28.9 us  [cut(): pl.pallas_call(body, in_specs=[smem, smem, any_spec, any_spec], out_specs...]
  transfers between devices with their start and end apart: 33 -> 32, of which waited for: 8 -> 15; matrix products, arithmetic and copies ran while one was open for 41% -> 3% of each run, Pallas kernels for 24% -> 32%
where the time goes in v4:
time: 478 us; the launch traced here: 477 us
  waiting for transfers between devices  207 us (43%)
  Pallas kernels  163 us (34%)
  matrix products  35.9 us (8%)
  starting transfers between devices  27.5 us (6%)
  other arithmetic  22.5 us (5%)
  local copies, waits for them, and re-layouts  19.4 us (4%)
    ppermute x32, waiting for transfers between devices, swap(): return lax.ppermute(arr, 'x', [(i, i ^ off) for i in range(GROUP)])  207 us
    pallas_call x1, Pallas kernels, gated_mlp(): pl.pallas_call(body, grid_spec=pltpu.PrefetchScalarGridSpec(num_scalar_pr...  60 us
    pallas_call x5, Pallas kernels, attend(): pl.pallas_call(body, in_specs=[smem, smem, vmem] + [any_spec] * n_in, out...  39.6 us
    pallas_call x5, Pallas kernels, assemble(): pl.pallas_call(body, in_specs=[smem, smem] + [any_spec] * (len(args) - 2)...  34.1 us
    pallas_call x6, Pallas kernels, cut(): pl.pallas_call(body, in_specs=[smem, smem, any_spec, any_spec], out_specs...  28.9 us
    ppermute x32, starting transfers between devices, swap(): return lax.ppermute(arr, 'x', [(i, i ^ off) for i in range(GROUP)])  27.5 us
    dot_general x1, matrix products, project(): jnp.einsum('sbd,de->sbe', normed, w_q, preferred_element_type=jnp.float32)  13.1 us
    dot_general x1, matrix products, finish(): jnp.einsum('sbe,ed->sbd', flat_attn, w_o, preferred_element_type=jnp.floa...  13 us
  transfers between devices with their start and end apart: 32, of which 15 were waited for; matrix products, arithmetic and copies ran while one was open for 3% of the time, Pallas kernels for 32%

profile of v4, /device:TPU:0, one launch (start us, length us, event | category | flops | bytes accessed | tf_op | source)
XLA Modules:
  0.0 476.5 jit_solution(15668498517564247212)
XLA Ops:
  5.0 5.1 %fusion.22 = bf16[4,32,1024]{2,1,0:T(8,128)(2,1)S(1)} fusion(bf16[4096,1024]{1,0:T(8,128)(2,1)} %param.22, bf16[4,32,4096]{2,1,0:T(8,128)(2,1)} %param.16, f32[4096]{0:T(1024)S(1)} %convert_element_type.52, f32[4,32]{1,0:T(4,128)S(1)} %add_rsqrt_fusion.3), kind=kOutput, calls=%fused_computation.27 | convolution fusion | flops 1075970048 | bytes 9716224 | tf_op jit(solution)/shard_map/sbd,de->sbe/dot_general | solution.py:44
  10.4 4.7 fusion.6
  17.3 13.1 %fusion.2 = f32[4,32,4096]{2,1,0:T(8,128)S(1)} fusion(bf16[4096,4096]{1,0:T(8,128)(2,1)} %param.20, bf16[4,32,4096]{2,1,0:T(8,128)(2,1)S(1)} %copy-done.1, f32[4096]{0:T(1024)S(1)} %convert_element_type.52, f32[4,32]{1,0:T(4,128)S(1)} %add_rsqrt_fusion.3), kind=kOutput, calls=%fused_computation.2 | convolution fusion | flops 4297064448 | bytes 36717056 | tf_op jit(solution)/shard_map/sbd,de->sbe/dot_general | solution.py:42
  44.9 6.6 %cut.6 = (bf16[2,8,252,2,128]{4,3,2,1,0:T(2,128)(2,1)}, bf16[2,8,252,2,128]{4,3,2,1,0:T(2,128)(2,1)}, bf16[2,8,252,2,128]{4,3,2,1,0:T(2,128)(2,1)}) custom-call(s32[1]{0:T(128)} %bitcast.me_ref, s32[128]{0:T(128)} %pos_ref.13, bf16[128,256,2,128]{3,2,1,0:T(2,128)(2,1)} %k_ref.21, bf16[128,256,2,128]{3,2,1,0:T(2,128)(2,1)} %v_ref.21), custom_call_target="tpu_custom_call" | custom-call | flops 4800000000 | bytes 12582912 | tf_op jit(solution)/shard_map/cut/pallas_call | solution.py:243
  52.5 10.2 %attend_source.1 = bf16[4,10,32,128]{3,2,1,0:T(8,128)(2,1)} custom-call(s32[1]{0:T(128)} %bitcast.me_ref, s32[128]{0:T(128)} %pos_ref.13, bf16[4,10,48,128]{3,2,1,0:T(8,128)(2,1)} %pad_maximum_fusion.5.packed_ref, bf16[128,512,128]{2,1,0:T(8,128)(2,1)} %bitcast.116, bf16[128,512,128]{2,1,0:T(8,128)(2,1)} %bitcast.122), custom_call_target="tpu_custom_call" | custom-call | flops 10000000000 | bytes 10485760 | tf_op jit(solution)/shard_map/attend_source/pallas_call | solution.py:180
  97.0 7.2 %cut.7 = (bf16[2,9,252,2,128]{4,3,2,1,0:T(2,128)(2,1)}, bf16[2,9,252,2,128]{4,3,2,1,0:T(2,128)(2,1)}, bf16[2,9,252,2,128]{4,3,2,1,0:T(2,128)(2,1)}) custom-call(s32[1]{0:T(128)} %bitcast.me_ref, s32[128]{0:T(128)} %pos_ref.13, bf16[128,256,2,128]{3,2,1,0:T(2,128)(2,1)} %k_ref.21, bf16[128,256,2,128]{3,2,1,0:T(2,128)(2,1)} %v_ref.21), custom_call_target="tpu_custom_call" | custom-call | flops 5400000000 | bytes 14155776 | tf_op jit(solution)/shard_map/cut/pallas_call | solution.py:243
  104.3 5.3 %collective-permute-done.13.rest_1_ = bf16[2,3,252,2,128]{4,3,2,1,0:T(2,128)(2,1)S(1)} collective-permute-done((bf16[2,3,252,2,128]{4,3,2,1,0:T(2,128)(2,1)}, bf16[2,3,252,2,128]{4,3,2,1,0:T(2,128)(2,1)S(1)}, u32[]{:S(2)}, u32[]{:S(2)}) %collective-permute-start.13) | collective-permute-done | bytes 774176 | tf_op jit(solution)/shard_map/ppermute | solution.py:362
  109.6 16.0 %collective-permute-done.14.rest_2_ = bf16[2,3,252,2,128]{4,3,2,1,0:T(2,128)(2,1)S(1)} collective-permute-done((bf16[2,3,252,2,128]{4,3,2,1,0:T(2,128)(2,1)}, bf16[2,3,252,2,128]{4,3,2,1,0:T(2,128)(2,1)S(1)}, u32[]{:S(2)}, u32[]{:S(2)}) %collective-permute-start.14) | collective-permute-done | bytes 774176 | tf_op jit(solution)/shard_map/ppermute | solution.py:362
  132.8 4.7 attend_here.4
  138.4 5.5 %attend_here.7 = bf16[4,3,32,128]{3,2,1,0:T(8,128)(2,1)} custom-call(s32[1]{0:T(128)} %bitcast.me_ref, s32[32]{0:T(128)} %copy-done.37, bf16[4,32,48,128]{3,2,1,0:T(8,128)(2,1)} %copy-done, bf16[128,512,128]{2,1,0:T(8,128)(2,1)} %bitcast.119, bf16[128,512,128]{2,1,0:T(8,128)(2,1)} %bitcast.125, bf16[2,3,504,128]{3,2,1,0:T(8,128)(2,1)} %bitcast.148, ...), custom_call_target="tpu_custom_call" | custom-call | flops 3000000000 | bytes 3145728 | tf_op jit(solution)/shard_map/attend_here/pallas_call | solution.py:180
  143.9 26.7 %collective-permute-done.7.rest_4_ = bf16[2,8,252,2,128]{4,3,2,1,0:T(2,128)(2,1)} collective-permute-done((bf16[2,8,252,2,128]{4,3,2,1,0:T(2,128)(2,1)}, bf16[2,8,252,2,128]{4,3,2,1,0:T(2,128)(2,1)}, u32[]{:S(2)}, u32[]{:S(2)}) %collective-permute-start.7) | collective-permute-done | bytes 2064416 | tf_op jit(solution)/shard_map/ppermute | solution.py:362
  170.5 43.7 %collective-permute-done.8.rest_5_ = bf16[2,8,252,2,128]{4,3,2,1,0:T(2,128)(2,1)} collective-permute-done((bf16[2,8,252,2,128]{4,3,2,1,0:T(2,128)(2,1)}, bf16[2,8,252,2,128]{4,3,2,1,0:T(2,128)(2,1)}, u32[]{:S(2)}, u32[]{:S(2)}) %collective-permute-start.8) | collective-permute-done | bytes 2064416 | tf_op jit(solution)/shard_map/ppermute | solution.py:362
  214.2 9.1 %attend_here.5 = bf16[4,8,32,128]{3,2,1,0:T(8,128)(2,1)} custom-call(s32[1]{0:T(128)} %bitcast.me_ref, s32[32]{0:T(128)} %copy-done.37, bf16[4,32,48,128]{3,2,1,0:T(8,128)(2,1)} %copy-done, bf16[128,512,128]{2,1,0:T(8,128)(2,1)} %bitcast.120, bf16[128,512,128]{2,1,0:T(8,128)(2,1)} %bitcast.126, bf16[2,8,504,128]{3,2,1,0:T(8,128)(2,1)} %bitcast.23.rest_2_, ...), custom_call_target="tpu_custom_call" | custom-call | flops 8000000000 | bytes 8388608 | tf_op jit(solution)/shard_map/attend_here/pallas_call | solution.py:180
  224.3 40.2 %collective-permute-done.10.rest_1_ = bf16[2,9,252,2,128]{4,3,2,1,0:T(2,128)(2,1)} collective-permute-done((bf16[2,9,252,2,128]{4,3,2,1,0:T(2,128)(2,1)}, bf16[2,9,252,2,128]{4,3,2,1,0:T(2,128)(2,1)}, u32[]{:S(2)}, u32[]{:S(2)}) %collective-permute-start.10) | collective-permute-done | bytes 2322464 | tf_op jit(solution)/shard_map/ppermute | solution.py:362
  264.5 49.2 %collective-permute-done.11.rest_2_ = bf16[2,9,252,2,128]{4,3,2,1,0:T(2,128)(2,1)} collective-permute-done((bf16[2,9,252,2,128]{4,3,2,1,0:T(2,128)(2,1)}, bf16[2,9,252,2,128]{4,3,2,1,0:T(2,128)(2,1)}, u32[]{:S(2)}, u32[]{:S(2)}) %collective-permute-start.11) | collective-permute-done | bytes 2322464 | tf_op jit(solution)/shard_map/ppermute | solution.py:362
  313.7 10.1 %attend_here.6 = bf16[4,9,32,128]{3,2,1,0:T(8,128)(2,1)} custom-call(s32[1]{0:T(128)} %bitcast.me_ref, s32[32]{0:T(128)} %copy-done.37, bf16[4,32,48,128]{3,2,1,0:T(8,128)(2,1)} %copy-done, bf16[128,512,128]{2,1,0:T(8,128)(2,1)} %bitcast.121, bf16[128,512,128]{2,1,0:T(8,128)(2,1)} %bitcast.127, bf16[2,9,504,128]{3,2,1,0:T(8,128)(2,1)} %bitcast.26.rest_2_, ...), custom_call_target="tpu_custom_call" | custom-call | flops 8999999488 | bytes 9437184 | tf_op jit(solution)/shard_map/attend_here/pallas_call | solution.py:180
  328.2 13.0 %multiply_reduce_fusion = (f32[4,32]{1,0:T(4,128)S(1)}, f32[4,32,4096]{2,1,0:T(8,128)S(1)}) fusion(bf16[4,32,4096]{2,1,0:T(8,128)(2,1)S(1)} %reshape.189, bf16[4096,4096]{1,0:T(8,128)(2,1)} %param.25, bf16[4,32,4096]{2,1,0:T(8,128)(2,1)S(1)} %copy-done.1), kind=kOutput, calls=%fused_computation.23 | convolution fusion | flops 4298113024 | bytes 37749248 | tf_op jit(solution)/shard_map/sbe,ed->sbd/dot_general | solution.py:100
  346.9 5.6 %cut.11 = (bf16[2,6,252,2,128]{4,3,2,1,0:T(2,128)(2,1)}, bf16[2,6,252,2,128]{4,3,2,1,0:T(2,128)(2,1)}, bf16[2,6,252,2,128]{4,3,2,1,0:T(2,128)(2,1)}) custom-call(s32[1]{0:T(128)} %bitcast.me_ref, s32[128]{0:T(128)} %pos_ref.13, bf16[128,256,2,128]{3,2,1,0:T(2,128)(2,1)} %k_ref.21, bf16[128,256,2,128]{3,2,1,0:T(2,128)(2,1)} %v_ref.21), custom_call_target="tpu_custom_call" | custom-call | flops 3600000000 | bytes 9437184 | tf_op jit(solution)/shard_map/cut/pallas_call | solution.py:243
  357.1 60.0 %gated_mlp.1 = (f32[128,4096]{1,0:T(8,128)}, f32[128,4096]{1,0:T(8,128)}) custom-call(s32[1]{0:T(128)S(6)} %and.4.core_ref, bf16[2,128,4096]{2,1,0:T(8,128)(2,1)} %pad_maximum_fusion.rows_ref, bf16[4096,12288]{1,0:T(8,128)(2,1)} %gate_ref.1, bf16[4096,12288]{1,0:T(8,128)(2,1)} %up_ref.1, bf16[12288,4096]{1,0:T(8,128)(2,1)} %down_ref.1), custom_call_target="tpu_custom_call" | custom-call | flops 38654705664 | bytes 150994944 | tf_op jit(solution)/shard_map/gated_mlp/pallas_call | solution.py:78
  424.5 9.6 %assemble.5 = (bf16[32,256,4,2,128]{4,3,2,1,0:T(2,128)(2,1)}, bf16[32,256,4,2,128]{4,3,2,1,0:T(2,128)(2,1)}) custom-call(s32[1]{0:T(128)} %bitcast.me_ref, s32[32]{0:T(128)} %copy-done.37, bf16[128,256,2,128]{3,2,1,0:T(2,128)(2,1)} %k_ref.21, bf16[128,256,2,128]{3,2,1,0:T(2,128)(2,1)} %v_ref.21, bf16[32,4,4,2,128]{4,3,2,1,0:T(2,128)(2,1)} %fusion.32.k_fresh, ...), custom_call_target="tpu_custom_call" | custom-call | flops 6000000000 | bytes 20971520 | tf_op jit(solution)/shard_map/assemble/pallas_call | solution.py:338
  434.1 4.7 collective-permute-done.27.rest_1_
  439.7 8.9 %assemble.6 = (bf16[32,256,4,2,128]{4,3,2,1,0:T(2,128)(2,1)}, bf16[32,256,4,2,128]{4,3,2,1,0:T(2,128)(2,1)}) custom-call(s32[1]{0:T(128)} %bitcast.me_ref, s32[32]{0:T(128)} %copy-done.37, bf16[128,256,2,128]{3,2,1,0:T(2,128)(2,1)} %k_ref.21, bf16[128,256,2,128]{3,2,1,0:T(2,128)(2,1)} %v_ref.21, ...), custom_call_target="tpu_custom_call", output_to_operand_aliasing={{0}: (9, {}), {1}: (10, {})} | custom-call | flops 5400000000 | bytes 18874368 | tf_op jit(solution)/shard_map/assemble/pallas_call | solution.py:338
  451.1 8.8 %assemble.7 = (bf16[32,256,4,2,128]{4,3,2,1,0:T(2,128)(2,1)}, bf16[32,256,4,2,128]{4,3,2,1,0:T(2,128)(2,1)}) custom-call(s32[1]{0:T(128)} %bitcast.me_ref, s32[32]{0:T(128)} %copy-done.37, bf16[128,256,2,128]{3,2,1,0:T(2,128)(2,1)} %k_ref.21, bf16[128,256,2,128]{3,2,1,0:T(2,128)(2,1)} %v_ref.21, ...), custom_call_target="tpu_custom_call", output_to_operand_aliasing={{0}: (12, {}), {1}: (13, {})} | custom-call | flops 5400000000 | bytes 18874368 | tf_op jit(solution)/shard_map/assemble/pallas_call | solution.py:338
  464.4 4.9 %collective-permute-done.25.rest_2_ = bf16[2,1,252,2,128]{4,3,2,1,0:T(2,128)(2,1)S(1)} collective-permute-done((bf16[2,1,252,2,128]{4,3,2,1,0:T(2,128)(2,1)S(1)}, bf16[2,1,252,2,128]{4,3,2,1,0:T(2,128)(2,1)S(1)}, u32[]{:S(2)}, u32[]{:S(2)}) %collective-permute-start.25) | collective-permute-done | bytes 258080 | tf_op jit(solution)/shard_map/ppermute | solution.py:362
  (198 shorter events, 102.2 us)
Async XLA Ops:
  37.8 13.8 %collective-permute-start.17 = (bf16[10,48,128]{2,1,0:T(8,128)(2,1)}, bf16[10,48,128]{2,1,0:T(8,128)(2,1)S(1)}, u32[]{:S(2)}, u32[]{:S(2)}) collective-permute-start(bf16[10,48,128]{2,1,0:T(8,128)(2,1)} %get-tuple-element.74), channel_id=1, source_target_pairs={{0,3},{1,2},{2,1},{3,0},{4,7},{5,6},{6,5},{7,4},{8,11},{9,10},{10,... | collective-permute-start | bytes 368648 | tf_op jit(solution)/shard_map/ppermute | solution.py:362
  44.5 51.0 %collective-permute-start.12 = (bf16[2,3,252,2,128]{4,3,2,1,0:T(2,128)(2,1)}, bf16[2,3,252,2,128]{4,3,2,1,0:T(2,128)(2,1)S(1)}, u32[]{:S(2)}, u32[]{:S(2)}) collective-permute-start(bf16[2,3,252,2,128]{4,3,2,1,0:T(2,128)(2,1)} %get-tuple-element.39), channel_id=1, source_target_pairs={{0,1},{1,0},{2,3},{3,2},{4,5},{5,4},{6,7},{7,6},{8,9},{9,8},{10,11... | collective-permute-start | bytes 2322440 | tf_op jit(solution)/shard_map/ppermute | solution.py:362
  51.5 75.9 %collective-permute-start.6 = (bf16[2,8,252,2,128]{4,3,2,1,0:T(2,128)(2,1)}, bf16[2,8,252,2,128]{4,3,2,1,0:T(2,128)(2,1)}, u32[]{:S(2)}, u32[]{:S(2)}) collective-permute-start(bf16[2,8,252,2,128]{4,3,2,1,0:T(2,128)(2,1)} %get-tuple-element.33), channel_id=1, source_target_pairs={{0,1},{1,0},{2,3},{3,2},{4,5},{5,4},{6,7},{7,6},{8,9},{9,8},{10,11... | collective-permute-start | bytes 6193160 | tf_op jit(solution)/shard_map/ppermute | solution.py:362
  68.2 13.6 %collective-permute-start.3 = (bf16[2,512,128]{2,1,0:T(8,128)(2,1)S(1)}, bf16[2,512,128]{2,1,0:T(8,128)(2,1)S(1)}, u32[]{:S(2)}, u32[]{:S(2)}) collective-permute-start(bf16[2,512,128]{2,1,0:T(8,128)(2,1)S(1)} %get-tuple-element.67), channel_id=1, source_target_pairs={{0,2},{1,3},{2,0},{3,1},{4,6},{5,7},{6,4},{7,5},{8,10},{9,11},{10,... | collective-permute-start | bytes 786440 | tf_op jit(solution)/shard_map/ppermute | solution.py:362
  71.8 11.7 %collective-permute-start.1 = (bf16[2,512,128]{2,1,0:T(8,128)(2,1)S(1)}, bf16[2,512,128]{2,1,0:T(8,128)(2,1)S(1)}, u32[]{:S(2)}, u32[]{:S(2)}) collective-permute-start(bf16[2,512,128]{2,1,0:T(8,128)(2,1)S(1)} %get-tuple-element.68), channel_id=1, source_target_pairs={{0,1},{1,0},{2,3},{3,2},{4,5},{5,4},{6,7},{7,6},{8,9},{9,8},{10,11... | collective-permute-start | bytes 786440 | tf_op jit(solution)/shard_map/ppermute | solution.py:362
  75.6 11.2 %collective-permute-start.4 = (bf16[2,512,128]{2,1,0:T(8,128)(2,1)S(1)}, bf16[2,512,128]{2,1,0:T(8,128)(2,1)S(1)}, u32[]{:S(2)}, u32[]{:S(2)}) collective-permute-start(bf16[2,512,128]{2,1,0:T(8,128)(2,1)S(1)} %get-tuple-element.63), channel_id=1, source_target_pairs={{0,3},{1,2},{2,1},{3,0},{4,7},{5,6},{6,5},{7,4},{8,11},{9,10},{10,... | collective-permute-start | bytes 786440 | tf_op jit(solution)/shard_map/ppermute | solution.py:362
  87.5 22.1 %collective-permute-start.13 = (bf16[2,3,252,2,128]{4,3,2,1,0:T(2,128)(2,1)}, bf16[2,3,252,2,128]{4,3,2,1,0:T(2,128)(2,1)S(1)}, u32[]{:S(2)}, u32[]{:S(2)}) collective-permute-start(bf16[2,3,252,2,128]{4,3,2,1,0:T(2,128)(2,1)} %get-tuple-element.40), channel_id=1, source_target_pairs={{0,2},{1,3},{2,0},{3,1},{4,6},{5,7},{6,4},{7,5},{8,10},{9,11},{10,... | collective-permute-start | bytes 2322440 | tf_op jit(solution)/shard_map/ppermute | solution.py:362
  93.7 31.9 %collective-permute-start.14 = (bf16[2,3,252,2,128]{4,3,2,1,0:T(2,128)(2,1)}, bf16[2,3,252,2,128]{4,3,2,1,0:T(2,128)(2,1)S(1)}, u32[]{:S(2)}, u32[]{:S(2)}) collective-permute-start(bf16[2,3,252,2,128]{4,3,2,1,0:T(2,128)(2,1)} %get-tuple-element.41), channel_id=1, source_target_pairs={{0,3},{1,2},{2,1},{3,0},{4,7},{5,6},{6,5},{7,4},{8,11},{9,10},{10,... | collective-permute-start | bytes 2322440 | tf_op jit(solution)/shard_map/ppermute | solution.py:362
  94.6 75.9 %collective-permute-start.7 = (bf16[2,8,252,2,128]{4,3,2,1,0:T(2,128)(2,1)}, bf16[2,8,252,2,128]{4,3,2,1,0:T(2,128)(2,1)}, u32[]{:S(2)}, u32[]{:S(2)}) collective-permute-start(bf16[2,8,252,2,128]{4,3,2,1,0:T(2,128)(2,1)} %get-tuple-element.34), channel_id=1, source_target_pairs={{0,2},{1,3},{2,0},{3,1},{4,6},{5,7},{6,4},{7,5},{8,10},{9,11},{10,... | collective-permute-start | bytes 6193160 | tf_op jit(solution)/shard_map/ppermute | solution.py:362
  95.5 118.6 %collective-permute-start.8 = (bf16[2,8,252,2,128]{4,3,2,1,0:T(2,128)(2,1)}, bf16[2,8,252,2,128]{4,3,2,1,0:T(2,128)(2,1)}, u32[]{:S(2)}, u32[]{:S(2)}) collective-permute-start(bf16[2,8,252,2,128]{4,3,2,1,0:T(2,128)(2,1)} %get-tuple-element.35), channel_id=1, source_target_pairs={{0,3},{1,2},{2,1},{3,0},{4,7},{5,6},{6,5},{7,4},{8,11},{9,10},{10,... | collective-permute-start | bytes 6193160 | tf_op jit(solution)/shard_map/ppermute | solution.py:362
  109.6 114.7 %collective-permute-start.9 = (bf16[2,9,252,2,128]{4,3,2,1,0:T(2,128)(2,1)}, bf16[2,9,252,2,128]{4,3,2,1,0:T(2,128)(2,1)}, u32[]{:S(2)}, u32[]{:S(2)}) collective-permute-start(bf16[2,9,252,2,128]{4,3,2,1,0:T(2,128)(2,1)} %get-tuple-element.36), channel_id=1, source_target_pairs={{0,1},{1,0},{2,3},{3,2},{4,5},{5,4},{6,7},{7,6},{8,9},{9,8},{10,11... | collective-permute-start | bytes 6967304 | tf_op jit(solution)/shard_map/ppermute | solution.py:362
  125.6 138.9 %collective-permute-start.10 = (bf16[2,9,252,2,128]{4,3,2,1,0:T(2,128)(2,1)}, bf16[2,9,252,2,128]{4,3,2,1,0:T(2,128)(2,1)}, u32[]{:S(2)}, u32[]{:S(2)}) collective-permute-start(bf16[2,9,252,2,128]{4,3,2,1,0:T(2,128)(2,1)} %get-tuple-element.37), channel_id=1, source_target_pairs={{0,2},{1,3},{2,0},{3,1},{4,6},{5,7},{6,4},{7,5},{8,10},{9,11},{10,... | collective-permute-start | bytes 6967304 | tf_op jit(solution)/shard_map/ppermute | solution.py:362
  127.3 186.4 %collective-permute-start.11 = (bf16[2,9,252,2,128]{4,3,2,1,0:T(2,128)(2,1)}, bf16[2,9,252,2,128]{4,3,2,1,0:T(2,128)(2,1)}, u32[]{:S(2)}, u32[]{:S(2)}) collective-permute-start(bf16[2,9,252,2,128]{4,3,2,1,0:T(2,128)(2,1)} %get-tuple-element.38), channel_id=1, source_target_pairs={{0,3},{1,2},{2,1},{3,0},{4,7},{5,6},{6,5},{7,4},{8,11},{9,10},{10,... | collective-permute-start | bytes 6967304 | tf_op jit(solution)/shard_map/ppermute | solution.py:362
  342.9 11.5 %collective-permute-start.21 = (bf16[128,4096]{1,0:T(8,128)(2,1)S(1)}, bf16[128,4096]{1,0:T(8,128)(2,1)}, u32[]{:S(2)}, u32[]{:S(2)}) collective-permute-start(bf16[128,4096]{1,0:T(8,128)(2,1)S(1)} %bitcast.146), channel_id=1, source_target_pairs={{0,1},{1,0},{2,3},{3,2},{4,5},{5,4},{6,7},{7,6},{8,9},{9,8},{10,11... | collective-permute-start | bytes 3145736 | tf_op jit(solution)/shard_map/ppermute | solution.py:362
  346.4 71.2 %collective-permute-start.26 = (bf16[2,3,252,2,128]{4,3,2,1,0:T(2,128)(2,1)}, bf16[2,3,252,2,128]{4,3,2,1,0:T(2,128)(2,1)}, u32[]{:S(2)}, u32[]{:S(2)}) collective-permute-start(bf16[2,3,252,2,128]{4,3,2,1,0:T(2,128)(2,1)} %get-tuple-element.47), channel_id=1, source_target_pairs={{0,1},{1,0},{2,3},{3,2},{4,5},{5,4},{6,7},{7,6},{8,9},{9,8},{10,11... | collective-permute-start | bytes 2322440 | tf_op jit(solution)/shard_map/ppermute | solution.py:362
  352.5 96.1 %collective-permute-start.29 = (bf16[2,6,252,2,128]{4,3,2,1,0:T(2,128)(2,1)}, bf16[2,6,252,2,128]{4,3,2,1,0:T(2,128)(2,1)S(1)}, u32[]{:S(2)}, u32[]{:S(2)}) collective-permute-start(bf16[2,6,252,2,128]{4,3,2,1,0:T(2,128)(2,1)} %get-tuple-element.50), channel_id=1, source_target_pairs={{0,1},{1,0},{2,3},{3,2},{4,5},{5,4},{6,7},{7,6},{8,9},{9,8},{10,11... | collective-permute-start | bytes 4644872 | tf_op jit(solution)/shard_map/ppermute | solution.py:362
  352.7 97.0 %collective-permute-start.30 = (bf16[2,6,252,2,128]{4,3,2,1,0:T(2,128)(2,1)}, bf16[2,6,252,2,128]{4,3,2,1,0:T(2,128)(2,1)}, u32[]{:S(2)}, u32[]{:S(2)}) collective-permute-start(bf16[2,6,252,2,128]{4,3,2,1,0:T(2,128)(2,1)} %get-tuple-element.51), channel_id=1, source_target_pairs={{0,2},{1,3},{2,0},{3,1},{4,6},{5,7},{6,4},{7,5},{8,10},{9,11},{10,... | collective-permute-start | bytes 4644872 | tf_op jit(solution)/shard_map/ppermute | solution.py:362
  354.4 95.6 %collective-permute-start.31 = (bf16[2,6,252,2,128]{4,3,2,1,0:T(2,128)(2,1)}, bf16[2,6,252,2,128]{4,3,2,1,0:T(2,128)(2,1)}, u32[]{:S(2)}, u32[]{:S(2)}) collective-permute-start(bf16[2,6,252,2,128]{4,3,2,1,0:T(2,128)(2,1)} %get-tuple-element.52), channel_id=1, source_target_pairs={{0,3},{1,2},{2,1},{3,0},{4,7},{5,6},{6,5},{7,4},{8,11},{9,10},{10,... | collective-permute-start | bytes 4644872 | tf_op jit(solution)/shard_map/ppermute | solution.py:362
  417.1 56.0 %collective-permute-start.22 = (f32[128,4096]{1,0:T(8,128)}, f32[128,4096]{1,0:T(8,128)}, u32[]{:S(2)}, u32[]{:S(2)}) collective-permute-start(f32[128,4096]{1,0:T(8,128)} %get-tuple-element.43), channel_id=1, source_target_pairs={{0,1},{1,0},{2,3},{3,2},{4,5},{5,4},{6,7},{7,6},{8,9},{9,8},{10,11... | collective-permute-start | bytes 6291464 | tf_op jit(solution)/shard_map/ppermute | solution.py:362
  417.7 21.1 %collective-permute-start.27 = (bf16[2,3,252,2,128]{4,3,2,1,0:T(2,128)(2,1)}, bf16[2,3,252,2,128]{4,3,2,1,0:T(2,128)(2,1)S(1)}, u32[]{:S(2)}, u32[]{:S(2)}) collective-permute-start(bf16[2,3,252,2,128]{4,3,2,1,0:T(2,128)(2,1)} %get-tuple-element.48), channel_id=1, source_target_pairs={{0,2},{1,3},{2,0},{3,1},{4,6},{5,7},{6,4},{7,5},{8,10},{9,11},{10,... | collective-permute-start | bytes 2322440 | tf_op jit(solution)/shard_map/ppermute | solution.py:362
  438.8 21.1 %collective-permute-start.28 = (bf16[2,3,252,2,128]{4,3,2,1,0:T(2,128)(2,1)}, bf16[2,3,252,2,128]{4,3,2,1,0:T(2,128)(2,1)}, u32[]{:S(2)}, u32[]{:S(2)}) collective-permute-start(bf16[2,3,252,2,128]{4,3,2,1,0:T(2,128)(2,1)} %get-tuple-element.49), channel_id=1, source_target_pairs={{0,3},{1,2},{2,1},{3,0},{4,7},{5,6},{6,5},{7,4},{8,11},{9,10},{10,... | collective-permute-start | bytes 2322440 | tf_op jit(solution)/shard_map/ppermute | solution.py:362
  448.6 15.0 %collective-permute-start.23 = (bf16[2,1,252,2,128]{4,3,2,1,0:T(2,128)(2,1)}, bf16[2,1,252,2,128]{4,3,2,1,0:T(2,128)(2,1)S(1)}, u32[]{:S(2)}, u32[]{:S(2)}) collective-permute-start(bf16[2,1,252,2,128]{4,3,2,1,0:T(2,128)(2,1)} %get-tuple-element.44), channel_id=1, source_target_pairs={{0,1},{1,0},{2,3},{3,2},{4,5},{5,4},{6,7},{7,6},{8,9},{9,8},{10,11... | collective-permute-start | bytes 774152 | tf_op jit(solution)/shard_map/ppermute | solution.py:362
  449.7 14.8 %collective-permute-start.24 = (bf16[2,1,252,2,128]{4,3,2,1,0:T(2,128)(2,1)}, bf16[2,1,252,2,128]{4,3,2,1,0:T(2,128)(2,1)S(1)}, u32[]{:S(2)}, u32[]{:S(2)}) collective-permute-start(bf16[2,1,252,2,128]{4,3,2,1,0:T(2,128)(2,1)} %get-tuple-element.45), channel_id=1, source_target_pairs={{0,2},{1,3},{2,0},{3,1},{4,6},{5,7},{6,4},{7,5},{8,10},{9,11},{10,... | collective-permute-start | bytes 774152 | tf_op jit(solution)/shard_map/ppermute | solution.py:362
  450.0 19.4 %collective-permute-start.25 = (bf16[2,1,252,2,128]{4,3,2,1,0:T(2,128)(2,1)S(1)}, bf16[2,1,252,2,128]{4,3,2,1,0:T(2,128)(2,1)S(1)}, u32[]{:S(2)}, u32[]{:S(2)}) collective-permute-start(bf16[2,1,252,2,128]{4,3,2,1,0:T(2,128)(2,1)S(1)} %copy-done.39), channel_id=1, source_target_pairs={{0,3},{1,2},{2,1},{3,0},{4,7},{5,6},{6,5},{7,4},{8,11},{9,10},{10,... | collective-permute-start | bytes 774152 | tf_op jit(solution)/shard_map/ppermute | solution.py:362
  (48 other events, 531.2 us)
